TPU v7x, 32 devices: a whole 2x2x4 slice. The times are simulated.
32 devices in a mesh: dp: 4 (over z), exp: 8 (over y, x, core).
Axes of the slice: x: 2, y: 2, z: 4, core: 2. Of those that a mesh axis runs over, the one named last changes fastest.
Arguments:
- tokens: bfloat16 [16384, 1536], P(('dp', 'exp')), may hold values from -6 to 6
- targets: bfloat16 [16384, 1536], P(('dp', 'exp')), may hold values from -6 to 6
- valid_count: int32 [1], replicated, may hold values from 8192 to 16384
- segments: int32 [16384], P(('dp', 'exp')), may hold values from 0 to 2, as said below
- routes: int32 [16384, 4], P(('dp', 'exp')), may hold values from 0 to 7, all different within a row; in each aligned block of 512 rows (0 to 511, 512 to 1023, ...) at most 320 rows name the same one
- gain_attn: bfloat16 [1536], P(('dp', 'exp')), may hold values from 0.5 to 1.5
- w_query: bfloat16 [1536, 1536], P(('dp', 'exp')), may hold values from -0.15625 to 0.15625
- w_key: bfloat16 [1536, 256], P(('dp', 'exp')), may hold values from -0.15625 to 0.15625
- w_value: bfloat16 [1536, 256], P(('dp', 'exp')), may hold values from -0.15625 to 0.15625
- w_out: bfloat16 [1536, 1536], P(('dp', 'exp')), may hold values from -1.5 to 1.5
- gain_moe: bfloat16 [1536], P(('dp', 'exp')), may hold values from 0.5 to 1.5
- w_router: bfloat16 [1536, 8], P(('dp', 'exp')), may hold values from -0.15625 to 0.15625
- w_gate: bfloat16 [8, 1536, 768], P('exp', 'dp'), may hold values from -0.15625 to 0.15625
- w_up: bfloat16 [8, 1536, 768], P('exp', 'dp'), may hold values from -0.15625 to 0.15625
- w_down: bfloat16 [8, 768, 1536], P('exp', 'dp'), may hold values from -0.4375 to 0.4375
Outputs:
- layer_out: bfloat16 [16384, 1536], P(('dp', 'exp'))
- grad_tokens: float32 [16384, 1536], P(('dp', 'exp'))
- grad_gain_attn: float32 [1536], P(('dp', 'exp'))
- grad_w_query: float32 [1536, 1536], P(('dp', 'exp'))
- grad_w_key: float32 [1536, 256], P(('dp', 'exp'))
- grad_w_value: float32 [1536, 256], P(('dp', 'exp'))
- grad_w_out: float32 [1536, 1536], P(('dp', 'exp'))
- grad_gain_moe: float32 [1536], P(('dp', 'exp'))
- grad_w_router: float32 [1536, 8], P(('dp', 'exp'))
- grad_w_gate: float32 [8, 1536, 768], P('exp', 'dp')
- grad_w_up: float32 [8, 1536, 768], P('exp', 'dp')
- grad_w_down: float32 [8, 768, 1536], P('exp', 'dp')
Inputs may be any that keep to these rules, and one draw needn't show every extreme that they name: `segments`: in each group of 512 rows the first 256 are 0 and the rest rise from 1 to 2 without falling, each continuation nonempty. `routes`: the 4 experts of a token differ; in the rows of one device no expert is named more than 320 times.
All inputs are finite; a program needn't handle non-finite values.
Results may differ from a plain program's by a relative error of at most 0.04.
Values may be sent and summed in bfloat16 or wider, within the bound.
A program may use at most 256 MiB of HBM per device.

v0:
```python
import jax
import jax.numpy as jnp
from jax import lax
from jax.sharding import PartitionSpec as P

HD = 128
PROMPT = 256
NCONT = 2


EPS = 1e-06
THETA = 10000.0
HIGH = lax.Precision.HIGHEST
NEG_BIG = -1e30


def positions(segments):
    count_rows = segments.shape[0]
    row_ids = jnp.arange(count_rows, dtype=jnp.int32)
    labels = jnp.arange(NCONT + 1, dtype=jnp.int32)
    member = segments[:, None] == labels[None, :]
    first_row = jnp.min(jnp.where(member, row_ids[:, None], count_rows), axis=0)
    start_row = jnp.sum(jnp.where(member, first_row[None, :], 0), axis=1)
    return jnp.where(segments == 0, row_ids, PROMPT + row_ids - start_row)


def key_mask(segments):
    row_ids = jnp.arange(segments.shape[0], dtype=jnp.int32)
    causal = row_ids[None, :] <= row_ids[:, None]
    visible = (segments[None, :] == 0) | (segments[None, :] == segments[:, None])
    return causal & visible


def rotate(values, pos_rows, sign_value):
    half_size = HD // 2
    freq = THETA ** (-2.0 * jnp.arange(half_size, dtype=jnp.float32) / HD)
    angle = pos_rows.astype(jnp.float32)[:, None] * freq[None, :]
    cosine = jnp.cos(angle)[:, None, :]
    sine_part = sign_value * jnp.sin(angle)[:, None, :]
    first_half = values[..., :half_size]
    second = values[..., half_size:]
    return jnp.concatenate(
        [first_half * cosine - second * sine_part, second * cosine + first_half * sine_part],
        axis=-1,
    )


def attention_scores(query_b, key_b, allowed):
    logits = jnp.einsum(
        "qkgd,pkd->kgqp", query_b, key_b, preferred_element_type=jnp.float32
    ) * HD ** (-0.5)
    return jnp.where(allowed[None, None], logits, NEG_BIG)


def expert_gates(rows_in, gate_w, up_w):
    gate_val = jnp.einsum("sacd,adf->sacf", rows_in, gate_w, preferred_element_type=jnp.float32)
    up_val = jnp.einsum("sacd,adf->sacf", rows_in, up_w, preferred_element_type=jnp.float32)
    return (gate_val, up_val)


def body(
    tokens,
    targets,
    valid_count,
    segments,
    routes,
    gain_attn,
    w_query,
    w_key,
    w_value,
    w_out,
    gain_moe,
    w_router,
    w_gate,
    w_up,
    w_down,
):
    gain_one, query_w, key_w, value_w, out_w, gain_two, router_w = (
        lax.all_gather(gain_attn, ("dp", "exp"), axis=0, tiled=True),
        lax.all_gather(w_query, ("dp", "exp"), axis=0, tiled=True),
        lax.all_gather(w_key, ("dp", "exp"), axis=0, tiled=True),
        lax.all_gather(w_value, ("dp", "exp"), axis=0, tiled=True),
        lax.all_gather(w_out, ("dp", "exp"), axis=0, tiled=True),
        lax.all_gather(gain_moe, ("dp", "exp"), axis=0, tiled=True),
        lax.all_gather(w_router, ("dp", "exp"), axis=0, tiled=True),
    )
    gate_w, up_w, down_w = (
        lax.all_gather(w_gate, "dp", axis=1, tiled=True),
        lax.all_gather(w_up, "dp", axis=1, tiled=True),
        lax.all_gather(w_down, "dp", axis=1, tiled=True),
    )
    num_rows = tokens.shape[0]
    width = tokens.shape[1]
    num_heads = query_w.shape[1] // HD
    kv_heads = key_w.shape[1] // HD
    group_size = num_heads // kv_heads
    num_experts = router_w.shape[1]
    top_count = routes.shape[1]
    exp_local = gate_w.shape[0]
    exp_ranks = lax.axis_size("exp")
    capacity = 5 * num_rows * top_count // (4 * num_experts)
    tok_pos = positions(segments)
    allowed = key_mask(segments)
    resid_in = tokens.astype(jnp.float32)
    inv_one = lax.rsqrt(jnp.mean(resid_in * resid_in, axis=-1, keepdims=True) + EPS)
    normed_one = resid_in * inv_one
    hidden_one = (normed_one * gain_one.astype(jnp.float32)).astype(jnp.bfloat16)
    query_raw = jnp.dot(hidden_one, query_w, preferred_element_type=jnp.float32)
    key_raw = jnp.dot(hidden_one, key_w, preferred_element_type=jnp.float32)
    value_b = jnp.dot(hidden_one, value_w, preferred_element_type=jnp.float32).astype(jnp.bfloat16)
    query_b = rotate(query_raw.reshape(num_rows, num_heads, HD), tok_pos, 1.0).astype(jnp.bfloat16)
    query_b = query_b.reshape(num_rows, kv_heads, group_size, HD)
    key_b = rotate(key_raw.reshape(num_rows, kv_heads, HD), tok_pos, 1.0).astype(jnp.bfloat16)
    value_h = value_b.reshape(num_rows, kv_heads, HD)
    logit_att = attention_scores(query_b, key_b, allowed)
    row_max = jnp.max(logit_att, axis=-1, keepdims=True)
    log_total = row_max + jnp.log(jnp.sum(jnp.exp(logit_att - row_max), axis=-1, keepdims=True))
    probs_b = jnp.exp(logit_att - log_total).astype(jnp.bfloat16)
    attn_vals = jnp.einsum("kgqp,pkd->qkgd", probs_b, value_h, preferred_element_type=jnp.float32)
    attn_vals = attn_vals.reshape(num_rows, num_heads * HD).astype(jnp.bfloat16)
    resid_mid = resid_in + jnp.dot(attn_vals, out_w, preferred_element_type=jnp.float32)
    inv_two = lax.rsqrt(jnp.mean(resid_mid * resid_mid, axis=-1, keepdims=True) + EPS)
    normed_two = resid_mid * inv_two
    gain_two_f = gain_two.astype(jnp.float32)
    hidden_two = (normed_two * gain_two_f).astype(jnp.bfloat16)
    router_prob = jax.nn.softmax(
        jnp.dot(hidden_two, router_w, preferred_element_type=jnp.float32), axis=-1
    )
    expert_ids = jnp.arange(num_experts, dtype=jnp.int32)
    route_hot = routes[:, :, None] == expert_ids[None, None, :]
    chosen = jnp.sum(jnp.where(route_hot, router_prob[:, None, :], 0.0), axis=-1)
    weight_sum = jnp.sum(chosen, axis=1, keepdims=True)
    combine = chosen / weight_sum
    flat_hot = route_hot.reshape(num_rows * top_count, num_experts).astype(jnp.int32)
    slot_index = jnp.sum((jnp.cumsum(flat_hot, axis=0) - flat_hot) * flat_hot, axis=1)
    dest_index = routes.reshape(-1) * capacity + slot_index
    send_shape = (exp_ranks, exp_local, capacity, width)
    send_rows = jnp.zeros((num_experts * capacity, width), jnp.bfloat16)
    send_rows = (
        send_rows.at[dest_index].set(jnp.repeat(hidden_two, top_count, axis=0)).reshape(send_shape)
    )
    gate_val, up_val = expert_gates(
        lax.all_to_all(send_rows, "exp", split_axis=0, concat_axis=0, tiled=True), gate_w, up_w
    )
    act_b = (jax.nn.relu(gate_val) * up_val).astype(jnp.bfloat16)
    out_b = jnp.einsum("sacf,afd->sacd", act_b, down_w, preferred_element_type=jnp.float32).astype(
        jnp.bfloat16
    )
    returned = lax.all_to_all(out_b, "exp", split_axis=0, concat_axis=0, tiled=True)
    route_out = returned.reshape(num_experts * capacity, width)[dest_index].reshape(
        num_rows, top_count, width
    )
    route_out_f = route_out.astype(jnp.float32)
    resid_out = resid_mid + jnp.sum(combine[:, :, None] * route_out_f, axis=1)
    layer_out = resid_out.astype(jnp.bfloat16)
    total_rows = num_rows * lax.axis_size(("dp", "exp"))
    global_row = lax.axis_index(("dp", "exp")) * num_rows + jnp.arange(num_rows, dtype=jnp.int32)
    loss_scale = total_rows / valid_count[0].astype(jnp.float32)
    grad_out = jnp.where(
        (global_row < valid_count[0])[:, None],
        (resid_out - targets.astype(jnp.float32)) * loss_scale,
        0.0,
    )
    gain_one, query_w, key_w, value_w, out_w, gain_two, router_w = (
        lax.all_gather(gain_attn, ("dp", "exp"), axis=0, tiled=True),
        lax.all_gather(w_query, ("dp", "exp"), axis=0, tiled=True),
        lax.all_gather(w_key, ("dp", "exp"), axis=0, tiled=True),
        lax.all_gather(w_value, ("dp", "exp"), axis=0, tiled=True),
        lax.all_gather(w_out, ("dp", "exp"), axis=0, tiled=True),
        lax.all_gather(gain_moe, ("dp", "exp"), axis=0, tiled=True),
        lax.all_gather(w_router, ("dp", "exp"), axis=0, tiled=True),
    )
    gain_two_f = gain_two.astype(jnp.float32)
    grad_route = (combine[:, :, None] * grad_out[:, None, :]).astype(jnp.bfloat16)
    grad_comb = jnp.sum(grad_out[:, None, :] * route_out_f, axis=-1)
    grad_send = jnp.zeros((num_experts * capacity, width), jnp.bfloat16)
    grad_send = (
        grad_send.at[dest_index]
        .set(grad_route.reshape(num_rows * top_count, width))
        .reshape(send_shape)
    )
    expert_rows, grad_recv = (
        lax.all_to_all(send_rows, "exp", split_axis=0, concat_axis=0, tiled=True),
        lax.all_to_all(grad_send, "exp", split_axis=0, concat_axis=0, tiled=True),
    )
    gate_val, up_val = expert_gates(expert_rows, gate_w, up_w)
    gate_relu = jax.nn.relu(gate_val)
    act_b = (gate_relu * up_val).astype(jnp.bfloat16)
    grad_act = jnp.einsum("sacd,afd->sacf", grad_recv, down_w, preferred_element_type=jnp.float32)
    grad_down_w = jnp.einsum("sacf,sacd->afd", act_b, grad_recv, preferred_element_type=jnp.float32)
    grad_gate_b = jnp.where(gate_val > 0, grad_act * up_val, 0.0).astype(jnp.bfloat16)
    grad_up_b = (grad_act * gate_relu).astype(jnp.bfloat16)
    grad_gate_w = jnp.einsum(
        "sacd,sacf->adf", expert_rows, grad_gate_b, preferred_element_type=jnp.float32
    )
    grad_up_w = jnp.einsum(
        "sacd,sacf->adf", expert_rows, grad_up_b, preferred_element_type=jnp.float32
    )
    grad_rows = (
        jnp.einsum("sacf,adf->sacd", grad_gate_b, gate_w, preferred_element_type=jnp.float32)
        + jnp.einsum("sacf,adf->sacd", grad_up_b, up_w, preferred_element_type=jnp.float32)
    ).astype(jnp.bfloat16)
    grad_back = lax.all_to_all(grad_rows, "exp", split_axis=0, concat_axis=0, tiled=True)
    grad_copies = grad_back.reshape(num_experts * capacity, width)[dest_index].reshape(
        num_rows, top_count, width
    )
    grad_hidden_two = jnp.sum(grad_copies.astype(jnp.float32), axis=1)
    grad_chosen = (grad_comb - jnp.sum(grad_comb * combine, axis=1, keepdims=True)) / weight_sum
    grad_prob = jnp.sum(jnp.where(route_hot, grad_chosen[:, :, None], 0.0), axis=1)
    grad_logit = router_prob * (
        grad_prob - jnp.sum(router_prob * grad_prob, axis=-1, keepdims=True)
    )
    router_f = router_w.astype(jnp.float32)
    grad_hidden_two = grad_hidden_two + jnp.einsum(
        "re,de->rd", grad_logit, router_f, precision=HIGH
    )
    grad_router = jnp.einsum(
        "rd,re->de", hidden_two.astype(jnp.float32), grad_logit, precision=HIGH
    )
    grad_gain_two = jnp.sum(grad_hidden_two * normed_two, axis=0)
    grad_norm_two = grad_hidden_two * gain_two_f
    grad_mid = grad_out + inv_two * (
        grad_norm_two - normed_two * jnp.mean(grad_norm_two * normed_two, axis=-1, keepdims=True)
    )
    grad_proj_b = grad_mid.astype(jnp.bfloat16)
    grad_out_w = jnp.einsum("rh,rd->hd", attn_vals, grad_proj_b, preferred_element_type=jnp.float32)
    grad_vals_b = jnp.einsum(
        "rd,hd->rh", grad_proj_b, out_w, preferred_element_type=jnp.float32
    ).astype(jnp.bfloat16)
    grad_vals_b = grad_vals_b.reshape(num_rows, kv_heads, group_size, HD)
    logit_att = attention_scores(query_b, key_b, allowed)
    probs = jnp.exp(logit_att - log_total)
    probs_b = probs.astype(jnp.bfloat16)
    grad_value = jnp.einsum(
        "kgqp,qkgd->pkd", probs_b, grad_vals_b, preferred_element_type=jnp.float32
    )
    grad_prob_att = jnp.einsum(
        "qkgd,pkd->kgqp", grad_vals_b, value_h, preferred_element_type=jnp.float32
    )
    delta_row = jnp.sum(probs * grad_prob_att, axis=-1, keepdims=True)
    grad_score_b = (probs * (grad_prob_att - delta_row)).astype(jnp.bfloat16)
    grad_query = jnp.einsum(
        "kgqp,pkd->qkgd", grad_score_b, key_b, preferred_element_type=jnp.float32
    ) * HD ** (-0.5)
    grad_key = jnp.einsum(
        "kgqp,qkgd->pkd", grad_score_b, query_b, preferred_element_type=jnp.float32
    ) * HD ** (-0.5)
    grad_query_b = rotate(grad_query.reshape(num_rows, num_heads, HD), tok_pos, -1.0).astype(
        jnp.bfloat16
    )
    grad_query_b = grad_query_b.reshape(num_rows, num_heads * HD)
    grad_key_b = (
        rotate(grad_key, tok_pos, -1.0).astype(jnp.bfloat16).reshape(num_rows, kv_heads * HD)
    )
    grad_value_b = grad_value.astype(jnp.bfloat16).reshape(num_rows, kv_heads * HD)
    grad_query_w = jnp.einsum(
        "rd,rh->dh", hidden_one, grad_query_b, preferred_element_type=jnp.float32
    )
    grad_key_w = jnp.einsum("rd,rh->dh", hidden_one, grad_key_b, preferred_element_type=jnp.float32)
    grad_value_w = jnp.einsum(
        "rd,rh->dh", hidden_one, grad_value_b, preferred_element_type=jnp.float32
    )
    grad_hidden_one = (
        jnp.einsum("rh,dh->rd", grad_query_b, query_w, preferred_element_type=jnp.float32)
        + jnp.einsum("rh,dh->rd", grad_key_b, key_w, preferred_element_type=jnp.float32)
        + jnp.einsum("rh,dh->rd", grad_value_b, value_w, preferred_element_type=jnp.float32)
    )
    grad_gain_one = jnp.sum(grad_hidden_one * normed_one, axis=0)
    grad_norm_one = grad_hidden_one * gain_one.astype(jnp.float32)
    grad_in = grad_mid + inv_one * (
        grad_norm_one - normed_one * jnp.mean(grad_norm_one * normed_one, axis=-1, keepdims=True)
    )
    dense_sums = (
        lax.psum_scatter(grad_gain_one, ("dp", "exp"), scatter_dimension=0, tiled=True),
        lax.psum_scatter(grad_query_w, ("dp", "exp"), scatter_dimension=0, tiled=True),
        lax.psum_scatter(grad_key_w, ("dp", "exp"), scatter_dimension=0, tiled=True),
        lax.psum_scatter(grad_value_w, ("dp", "exp"), scatter_dimension=0, tiled=True),
        lax.psum_scatter(grad_out_w, ("dp", "exp"), scatter_dimension=0, tiled=True),
        lax.psum_scatter(grad_gain_two, ("dp", "exp"), scatter_dimension=0, tiled=True),
        lax.psum_scatter(grad_router, ("dp", "exp"), scatter_dimension=0, tiled=True),
    )
    expert_sums = (
        lax.psum_scatter(
            grad_gate_w.astype(jnp.bfloat16), "dp", scatter_dimension=1, tiled=True
        ).astype(jnp.float32),
        lax.psum_scatter(
            grad_up_w.astype(jnp.bfloat16), "dp", scatter_dimension=1, tiled=True
        ).astype(jnp.float32),
        lax.psum_scatter(
            grad_down_w.astype(jnp.bfloat16), "dp", scatter_dimension=1, tiled=True
        ).astype(jnp.float32),
    )
    return (
        layer_out,
        grad_in,
        dense_sums[0],
        dense_sums[1],
        dense_sums[2],
        dense_sums[3],
        dense_sums[4],
        dense_sums[5],
        dense_sums[6],
        expert_sums[0],
        expert_sums[1],
        expert_sums[2],
    )


def solution(mesh):
    in_specs = (
        P(("dp", "exp"), None),
        P(("dp", "exp"), None),
        P(),
        P(("dp", "exp")),
        P(("dp", "exp"), None),
        P(("dp", "exp")),
        P(("dp", "exp"), None),
        P(("dp", "exp"), None),
        P(("dp", "exp"), None),
        P(("dp", "exp"), None),
        P(("dp", "exp")),
        P(("dp", "exp"), None),
        P("exp", "dp", None),
        P("exp", "dp", None),
        P("exp", "dp", None),
    )
    out_specs = (
        P(("dp", "exp"), None),
        P(("dp", "exp"), None),
        P(("dp", "exp")),
        P(("dp", "exp"), None),
        P(("dp", "exp"), None),
        P(("dp", "exp"), None),
        P(("dp", "exp"), None),
        P(("dp", "exp")),
        P(("dp", "exp"), None),
        P("exp", "dp", None),
        P("exp", "dp", None),
        P("exp", "dp", None),
    )
    return jax.shard_map(body, mesh=mesh, in_specs=in_specs, out_specs=out_specs, check_vma=False)
```

profile of v0, /device:TPU:0, one launch (start us, length us, event | category | flops | bytes accessed | tf_op | source)
XLA Modules:
  0.0 1377.4 jit_solution(7133461163245013822)
XLA Ops:
  13.0 42.3 %all-reduce.5 = (bf16[1536]{0:T(1024)(128)(2,1)S(1)}, bf16[1536]{0:T(1024)(128)(2,1)S(1)}) all-reduce(bf16[1536]{0:T(1024)(128)(2,1)S(1)} %dynamic-update-slice, bf16[1536]{0:T(1024)(128)(2,1)S(1)} %dynamic-update-slice.1), channel_id=1, replica_groups=mesh['dp'=4,'exp'=8] {'dp','exp'}, use_global_device_ids=true, to_apply=%add | all-reduce | flops 3072 | bytes 12288
  57.2 43.9 %all_gather.39 = bf16[1536,256]{1,0:T(8,128)(2,1)S(1)} all-gather(bf16[48,256]{1,0:T(8,128)(2,1)S(1)} %copy-done.47), channel_id=1, replica_groups=mesh['dp'=4,'exp'=8] {'dp','exp'}, dimensions={0}, use_global_device_ids=true | all-gather | bytes 811008 | tf_op jit(solution)/shard_map/all_gather | solution.py:81
  107.5 41.6 %all_gather.38 = bf16[1536,256]{1,0:T(8,128)(2,1)S(1)} all-gather(bf16[48,256]{1,0:T(8,128)(2,1)S(1)} %copy-done.48), channel_id=1, replica_groups=mesh['dp'=4,'exp'=8] {'dp','exp'}, dimensions={0}, use_global_device_ids=true | all-gather | bytes 811008 | tf_op jit(solution)/shard_map/all_gather | solution.py:82
  192.0 10.7 reshape.466
  202.7 15.4 %scatter_custom_fusion = bf16[2560,1536]{1,0:T(8,128)(2,1)} fusion(s32[2048]{0:T(1024)S(1)} %bitcast.247, bf16[2048,1536]{1,0:T(8,128)(2,1)} %reshape.466, bf16[]{:T(256)} %constant.15.clone.1), kind=kCustom, calls=%fused_computation.50 | custom fusion | bytes 7864832 | tf_op jit(solution)/shard_map/scatter | solution.py:140
  224.3 87.2 %all-to-all-done = bf16[8,1,320,1536]{3,2,1,0:T(8,128)(2,1)} async-done(((bf16[8,1,320,1536]{3,2,1,0:T(8,128)(2,1)}), bf16[8,1,320,1536]{3,2,1,0:T(8,128)(2,1)}, u32[]{:S(2)}, u32[]{:S(2)}) %all-to-all-start) | async-done | bytes 7864352 | tf_op jit(solution)/shard_map/all_to_all | solution.py:143
  311.5 12.6 fusion.56
  324.1 13.1 multiply_convert_fusion.2
  337.2 10.6 convert_bitcast_fusion
  352.9 117.6 %all-gather = bf16[32,48,8]{1,2,0:T(8,128)(2,1)S(1)} all-gather(bf16[1,48,8]{1,2,0:T(8,128)(2,1)S(1)} %bitcast.251), channel_id=1, replica_groups=mesh['dp'=4,'exp'=8] {'dp','exp'}, dimensions={0}, use_global_device_ids=true | all-gather | bytes 25344 | tf_op jit(solution)/shard_map/all_gather | solution.py:85
  473.8 17.9 %gather_fusion = bf16[2048,1536]{1,0:T(8,128)(2,1)} fusion(bf16[2560,1536]{1,0:T(8,128)(2,1)} %bitcast.28, s32[2048]{0:T(1024)S(1)} %broadcast_clamp_fusion), kind=kCustom, calls=%fused_computation | custom fusion | bytes 12591104 | tf_op jit(solution)/shard_map/gather | solution.py:150
  491.7 12.2 reshape.444
  504.0 32.4 %multiply_reduce_fusion.1 = f32[512,1536]{1,0:T(8,128)S(1)} fusion(f32[512,4,1536]{2,1,0:T(4,128)} %reshape.444, f32[512,4]{1,0:T(8,128)S(1)} %copy.162), kind=kLoop, calls=%fused_computation.13 | loop fusion | flops 5505024 | bytes 15736832 | tf_op jit(solution)/shard_map/reduce_sum | solution.py:154
  545.8 14.9 %mul.422 = f32[2048,1536]{1,0:T(8,128)} reshape(f32[512,4,1536]{2,1,0:T(4,128)} %mul.421) | data formatting | bytes 25165824 | tf_op jit(solution)/shard_map/mul | solution.py:174
  560.6 16.3 %scatter_custom_fusion.1 = bf16[2560,1536]{1,0:T(8,128)(2,1)} fusion(s32[2048]{0:T(1024)S(1)} %bitcast.249, f32[2048,1536]{1,0:T(8,128)} %mul.422, f32[2048]{0:T(1024)S(1)} %div.66, bf16[]{:T(256)} %constant.15.clone.1), kind=kCustom, calls=%fused_computation.37 | custom fusion | flops 6291456 | bytes 20455426 | tf_op jit(solution)/shard_map/scatter | solution.py:179
  581.9 10.8 multiply_reduce_fusion
  597.3 74.8 %all-to-all-done.2 = bf16[8,1,320,1536]{3,2,1,0:T(8,128)(2,1)} async-done(((bf16[8,1,320,1536]{3,2,1,0:T(8,128)(2,1)}), bf16[8,1,320,1536]{3,2,1,0:T(8,128)(2,1)}, u32[]{:S(2)}, u32[]{:S(2)}) %all-to-all-start.2) | async-done | bytes 7864352 | tf_op jit(solution)/shard_map/all_to_all | solution.py:184
  672.1 11.0 fusion.40
  683.1 13.8 %multiply_convert_fusion.1 = (bf16[8,320,768]{2,1,0:T(8,128)(2,1)S(1)}, bf16[8,320,768]{2,1,0:T(8,128)(2,1)}) fusion(f32[8,320,768]{2,1,0:T(8,128)} %get-tuple-element.50, f32[8,320,768]{2,1,0:T(8,128)} %get-tuple-element.46, u8[320,768]{1,0:T(8,128)(4,1)S(1)} %copy-done.55, bf16[1,768,1536]{2,1,0:T(8,128)(2,1)} %all-gather.15.cloned.1.call-done, ...), kind=kOutput, calls=%fused_computation.33 | convolution fusion | flops 6059458560 | bytes 34062336 | tf_op jit(solution)/shard_map/sacd,afd->sacf/dot_general | solution.py:189
  697.0 13.0 fusion.53
  710.0 11.8 fusion.4
  726.9 10.9 fusion.43
  738.8 10.9 fusion.46
  749.8 65.3 %all-to-all-done.3 = bf16[8,1,320,1536]{3,2,1,0:T(8,128)(2,1)} async-done(((bf16[8,1,320,1536]{3,2,1,0:T(8,128)(2,1)}), bf16[8,1,320,1536]{3,2,1,0:T(8,128)(2,1)}, u32[]{:S(2)}, u32[]{:S(2)}) %all-to-all-start.3) | async-done | bytes 7864352 | tf_op jit(solution)/shard_map/all_to_all | solution.py:203
  815.1 18.0 %gather_fusion.1 = bf16[2048,1536]{1,0:T(8,128)(2,1)} fusion(bf16[2560,1536]{1,0:T(8,128)(2,1)} %bitcast.36, s32[2048]{0:T(1024)S(1)} %copy-done.42), kind=kCustom, calls=%fused_computation.1 | custom fusion | bytes 12591104 | tf_op jit(solution)/shard_map/gather | solution.py:204
  833.0 12.2 reshape.445
  845.3 12.6 reduce_sum.183
  889.9 10.9 fusion.2
  944.3 37.1 %all-reduce.4 = (f32[1536]{0:T(1024)S(1)}, f32[1536]{0:T(1024)S(1)}) all-reduce(f32[1536]{0:T(1024)S(1)} %get-tuple-element.14, f32[1536]{0:T(1024)S(1)} %copy-done.44), channel_id=2, replica_groups=mesh['dp'=4,'exp'=8] {'dp','exp'}, use_global_device_ids=true, to_apply=%region_25.26.clone | all-reduce | flops 3072 | bytes 24576
  987.4 99.8 %reduce-scatter.13.cloned.1.call-done = f32[48,256]{1,0:T(8,128)} async-done(((f32[1536,256]{1,0:T(8,128)}), f32[48,256]{1,0:T(8,128)}) %reduce-scatter.13.cloned.1.call-update) | async-done | bytes 49168 | tf_op jit(solution)/shard_map/reduce_scatter | solution.py:276
  1087.2 141.6 %reduce-scatter.11.cloned.1.call-done = f32[48,1536]{1,0:T(8,128)} async-done(((f32[1536,1536]{1,0:T(8,128)}), f32[48,1536]{1,0:T(8,128)}) %reduce-scatter.11.cloned.1.call-update) | async-done | bytes 294928 | tf_op jit(solution)/shard_map/reduce_scatter | solution.py:275
  1228.8 141.9 %reduce-scatter.17.cloned.1.call-done = f32[48,1536]{1,0:T(8,128)} async-done(((f32[1536,1536]{1,0:T(8,128)}), f32[48,1536]{1,0:T(8,128)}) %reduce-scatter.17.cloned.1.call-update) | async-done | bytes 294928 | tf_op jit(solution)/shard_map/reduce_scatter | solution.py:278
  (254 shorter events, 176.3 us)
Async XLA Ops:
  7.2 94.8 %copy-start.11 = (bf16[512,1536]{1,0:T(8,128)(2,1)S(1)}, bf16[512,1536]{1,0:T(8,128)(2,1)}, u32[]{:S(2)}) copy-start(bf16[512,1536]{1,0:T(8,128)(2,1)} %param.15) | copy-start | bytes 4718596
  7.2 50.0 %copy-start.47 = (bf16[48,256]{1,0:T(8,128)(2,1)S(1)}, bf16[48,256]{1,0:T(8,128)(2,1)}, u32[]{:S(2)}) copy-start(bf16[48,256]{1,0:T(8,128)(2,1)} %param.22) | copy-start | bytes 73732
  7.2 148.8 %all-gather.7.cloned.1.call-start = ((), (), s32[]{:S(2)}) async-start(), calls=%async_computation.12 | async-start | bytes 4866048 | tf_op jit(solution)/shard_map/all_gather | solution.py:80
  7.9 172.0 %all-gather.9.cloned.1.call-start = ((), (), s32[]{:S(2)}) async-start(), calls=%async_computation.13 | async-start | bytes 4866048 | tf_op jit(solution)/shard_map/all_gather | solution.py:83
  8.7 215.6 %all-gather.11.cloned.1.call-start = ((), (), s32[]{:S(2)}) async-start(), calls=%async_computation.14 | async-start | bytes 2949120 | tf_op jit(solution)/shard_map/all_gather | solution.py:88
  55.4 100.6 %copy-start.39 = (f32[1536]{0:T(1024)}, f32[1536]{0:T(1024)S(1)}, u32[]{:S(2)}) copy-start(f32[1536]{0:T(1024)S(1)} %convert_element_type.168) | copy-start | bytes 18436
  57.2 98.8 %copy-start.49 = (f32[512]{0:T(512)}, f32[512]{0:T(512)S(1)}, u32[]{:S(2)}) copy-start(f32[512]{0:T(512)S(1)} %add_rsqrt_fusion.1) | copy-start | bytes 6148
  106.2 54.7 %copy-start.24 = (f32[512,64]{0,1:T(8,128)}, f32[512,64]{0,1:T(8,128)S(1)}, u32[]{:S(2)}) copy-start(f32[512,64]{0,1:T(8,128)S(1)} %get-tuple-element.40) | copy-start | bytes 393220
  106.4 47.4 %copy-start.22 = (f32[512,64]{1,0:T(8,128)}, f32[512,64]{1,0:T(8,128)S(1)}, u32[]{:S(2)}) copy-start(f32[512,64]{1,0:T(8,128)S(1)} %copy.154) | copy-start | bytes 393220
  107.4 65.5 %copy-start.14 = (pred[512,512]{0,1:T(8,128)(4,1)}, pred[512,512]{0,1:T(8,128)(4,1)S(1)}, u32[]{:S(2)}) copy-start(pred[512,512]{0,1:T(8,128)(4,1)S(1)} %fusion.60) | copy-start | bytes 786436
  150.5 35.6 %copy-start.37 = (f32[1536]{0:T(1024)}, f32[1536]{0:T(1024)S(1)}, u32[]{:S(2)}) copy-start(f32[1536]{0:T(1024)S(1)} %convert_element_type.176) | copy-start | bytes 18436
  218.1 93.4 %all-to-all-start = ((bf16[8,1,320,1536]{3,2,1,0:T(8,128)(2,1)}), bf16[8,1,320,1536]{3,2,1,0:T(8,128)(2,1)}, u32[]{:S(2)}, u32[]{:S(2)}) async-start(bf16[8,1,320,1536]{3,2,1,0:T(8,128)(2,1)} %bitcast.226), calls=%async_computation | async-start | bytes 15728640 | tf_op jit(solution)/shard_map/all_to_all | solution.py:143
  223.1 101.0 %all-gather.13.cloned.1.call-start = ((), (), s32[]{:S(2)}) async-start(), calls=%async_computation.15 | async-start | bytes 2949120 | tf_op jit(solution)/shard_map/all_gather | solution.py:89
  223.6 113.6 %all-gather.15.cloned.1.call-start = ((), (), s32[]{:S(2)}) async-start(), calls=%async_computation.16 | async-start | bytes 2949120 | tf_op jit(solution)/shard_map/all_gather | solution.py:90
  347.8 125.6 %copy-start.36 = (s32[512,4]{0,1:T(4,128)S(1)}, s32[512,4]{0,1:T(4,128)}, u32[]{:S(2)}) copy-start(s32[512,4]{0,1:T(4,128)} %param.19) | copy-start | bytes 24580
  347.8 126.0 %all-to-all-start.1 = ((bf16[8,1,320,1536]{3,2,1,0:T(8,128)(2,1)}), bf16[8,1,320,1536]{3,2,1,0:T(8,128)(2,1)}, u32[]{:S(2)}, u32[]{:S(2)}) async-start(bf16[8,1,320,1536]{3,2,1,0:T(8,128)(2,1)} %convert_bitcast_fusion), calls=%async_computation.1 | async-start | bytes 15728640 | tf_op jit(solution)/shard_map/all_to_all | solution.py:149
  471.4 20.3 %copy-start.41 = (s32[2048]{0:T(1024)}, s32[2048]{0:T(1024)S(1)}, u32[]{:S(2)}) copy-start(s32[2048]{0:T(1024)S(1)} %broadcast_clamp_fusion) | copy-start | bytes 24580
  504.0 32.4 %copy-start.26 = (bf16[512,1536]{1,0:T(8,128)(2,1)S(1)}, bf16[512,1536]{1,0:T(8,128)(2,1)}, u32[]{:S(2)}) copy-start(bf16[512,1536]{1,0:T(8,128)(2,1)} %param.16) | copy-start | bytes 4718596
  577.0 95.1 %all-to-all-start.2 = ((bf16[8,1,320,1536]{3,2,1,0:T(8,128)(2,1)}), bf16[8,1,320,1536]{3,2,1,0:T(8,128)(2,1)}, u32[]{:S(2)}, u32[]{:S(2)}) async-start(bf16[8,1,320,1536]{3,2,1,0:T(8,128)(2,1)} %bitcast.225), calls=%async_computation.2 | async-start | bytes 15728640 | tf_op jit(solution)/shard_map/all_to_all | solution.py:184
  581.9 344.5 %reduce-scatter.25.cloned.1.call-start = ((), (), s32[]{:S(2)}) async-start(), calls=%async_computation.24 | async-start | bytes 811008
  597.1 86.1 %copy-start.55 = (u8[320,768]{1,0:T(8,128)(4,1)S(1)}, u8[320,768]{1,0:T(8,128)(4,1)}, u32[]{:S(2)}) copy-start(u8[320,768]{1,0:T(8,128)(4,1)} %get-tuple-element.49) | copy-start | bytes 737284
  597.1 330.8 %reduce-scatter.23.cloned.1.call-start = ((), (), s32[]{:S(2)}) async-start(), calls=%async_computation.23 | async-start | bytes 2949120 | tf_op jit(solution)/shard_map/reduce_scatter | solution.py:289
  683.1 13.9 %copy-start.52 = (bf16[1,1536,768]{2,1,0:T(8,128)(2,1)S(1)}, bf16[1,1536,768]{2,1,0:T(8,128)(2,1)}, u32[]{:S(2)}) copy-start(bf16[1,1536,768]{2,1,0:T(8,128)(2,1)} %all-gather.11.cloned.1.call-done) | copy-start | bytes 7077892
  697.0 13.0 copy-start.54
  721.8 93.3 %all-to-all-start.3 = ((bf16[8,1,320,1536]{3,2,1,0:T(8,128)(2,1)}), bf16[8,1,320,1536]{3,2,1,0:T(8,128)(2,1)}, u32[]{:S(2)}, u32[]{:S(2)}) async-start(bf16[8,1,320,1536]{3,2,1,0:T(8,128)(2,1)} %fusion.4), calls=%async_computation.3 | async-start | bytes 15728640 | tf_op jit(solution)/shard_map/all_to_all | solution.py:203
  726.7 203.4 %reduce-scatter.19.cloned.1.call-start = ((), (), s32[]{:S(2)}) async-start(), calls=%async_computation.21 | async-start | bytes 2949120 | tf_op jit(solution)/shard_map/reduce_scatter | solution.py:283
  737.9 194.3 %reduce-scatter.21.cloned.1.call-start = ((), (), s32[]{:S(2)}) async-start(), calls=%async_computation.22 | async-start | bytes 2949120 | tf_op jit(solution)/shard_map/reduce_scatter | solution.py:286
  738.8 76.3 %copy-start.42 = (s32[2048]{0:T(1024)S(1)}, s32[2048]{0:T(1024)}, u32[]{:S(2)}) copy-start(s32[2048]{0:T(1024)} %copy-done.41) | copy-start | bytes 24580
  749.7 237.7 %reduce-scatter.15.cloned.1.call-start = ((), (), s32[]{:S(2)}) async-start(), calls=%async_computation.19 | async-start | bytes 1622016 | tf_op jit(solution)/shard_map/reduce_scatter | solution.py:277
  889.9 197.3 %reduce-scatter.13.cloned.1.call-start = ((), (), s32[]{:S(2)}) async-start(), calls=%async_computation.18 | async-start | bytes 1622016 | tf_op jit(solution)/shard_map/reduce_scatter | solution.py:276
  906.0 322.7 %reduce-scatter.11.cloned.1.call-start = ((), (), s32[]{:S(2)}) async-start(), calls=%async_computation.17 | async-start | bytes 9732096 | tf_op jit(solution)/shard_map/reduce_scatter | solution.py:275
  917.5 453.1 %reduce-scatter.17.cloned.1.call-start = ((), (), s32[]{:S(2)}) async-start(), calls=%async_computation.20 | async-start | bytes 9732096 | tf_op jit(solution)/shard_map/reduce_scatter | solution.py:278
  (43 other events, 216.6 us)
Sparse Core Ops, SparseCore 0:
  10.9 69.4 all-gather.6
  83.3 64.5 all-gather.8
  149.4 49.6 all-gather.10
  225.1 48.5 all-gather.12
  275.1 48.7 all-gather.14
  597.2 99.0 reduce-scatter.24
  698.5 46.7 reduce-scatter.22
  747.6 47.0 reduce-scatter.18
  797.0 47.0 reduce-scatter.20
  890.0 94.2 reduce-scatter.14
  990.2 96.9 reduce-scatter.12
  1093.5 135.2 reduce-scatter.10
  1235.2 135.3 reduce-scatter.16
where the time goes:
time: 1380 us
  waiting for transfers between devices  614 us (44%)
  blocking collectives  283 us (21%)
  matrix products  194 us (14%)
  local copies, waits for them, and re-layouts  139 us (10%)
  other arithmetic  112 us (8%)
  starting transfers between devices  20.7 us (2%)
  between operations  15.8 us (1%)
    reduce_scatter x1, waiting for transfers between devices, body(): lax.psum_scatter(grad_out_w, ('dp', 'exp'), scatter_dimension=0, tiled=True)  142 us
    reduce_scatter x1, waiting for transfers between devices, body(): lax.psum_scatter(grad_query_w, ('dp', 'exp'), scatter_dimension=0, tiled=...  142 us
    all_gather x1, blocking collectives, body(): lax.all_gather(w_router, ('dp', 'exp'), axis=0, tiled=True)  118 us
    reduce_scatter x1, waiting for transfers between devices, body(): lax.psum_scatter(grad_key_w, ('dp', 'exp'), scatter_dimension=0, tiled=True)  99.8 us
    all_to_all x1, waiting for transfers between devices, body(): lax.all_to_all(send_rows, 'exp', split_axis=0, concat_axis=0, tiled=True)  87.2 us
    unnamed x2, blocking collectives  79.5 us
    all_to_all x1, waiting for transfers between devices, body(): lax.all_to_all(grad_send, 'exp', split_axis=0, concat_axis=0, tiled=True)  74.8 us
    all_to_all x1, waiting for transfers between devices, body(): lax.all_to_all(grad_rows, 'exp', split_axis=0, concat_axis=0, tiled=True)  65.3 us
  transfers between devices with their start and end apart: 17, of which 6 were waited for; matrix products, arithmetic and copies ran while one was open for 23% of the time, Pallas kernels for 0%

commit v1 on v0

--- a/solution.py
+++ b/solution.py
@@ -1,6 +1,10 @@
+import functools
+
 import jax
 import jax.numpy as jnp
 from jax import lax
+from jax.experimental import pallas as pl
+from jax.experimental.pallas import tpu as pltpu
 from jax.sharding import PartitionSpec as P
 
 HD = 128
@@ -58,7 +62,7 @@
     return (gate_val, up_val)
 
 
-def body(
+def body_general(
     tokens,
     targets,
     valid_count,
@@ -306,6 +310,809 @@
     )
 
 
+MESH = pl.DeviceIdType.MESH
+ANY = pl.BlockSpec(memory_space=pl.ANY)
+VMEM_BYTES = 62 * 2**20
+
+
+def nn_dot(left, right):
+    return jnp.dot(left, right, preferred_element_type=jnp.float32)
+
+
+def nt_dot(left, right):
+    return lax.dot_general(
+        left, right, (((1,), (1,)), ((), ())), preferred_element_type=jnp.float32
+    )
+
+
+def plane_peers():
+    me = lax.axis_index("exp")
+    core = lax.rem(me, 2)
+    x_pos = lax.rem(lax.div(me, 2), 2)
+    y_pos = lax.div(me, 4)
+    return me, me + 1 - 2 * core, me + 2 - 4 * x_pos, me + 4 - 8 * y_pos
+
+
+def remote(src, dst, send_sem, recv_sem, peer):
+    return pltpu.make_async_remote_copy(
+        src_ref=src,
+        dst_ref=dst,
+        send_sem=send_sem,
+        recv_sem=recv_sem,
+        device_id={"exp": peer},
+        device_id_type=MESH,
+    )
+
+
+def plane_barrier(peers):
+    barrier = pltpu.get_barrier_semaphore()
+    for peer in peers:
+        pl.semaphore_signal(barrier, inc=1, device_id={"exp": peer}, device_id_type=MESH)
+    pl.semaphore_wait(barrier, len(peers))
+
+
+def step_place(step, quad):
+    odd = lax.rem(step, 2)
+    last = lax.div(quad, 3)
+    mid = lax.rem(lax.div(quad + 1, 2), 2)
+    return mid * (1 - odd) + last, mid * odd + last
+
+
+class Gather:
+    def __init__(self, own, buf, send, recv):
+        self.own, self.buf, self.send, self.recv = own, buf, send, recv
+        self.me, self.sib, self.xn, self.yn = plane_peers()
+        self.diag = self.xn + self.yn - self.me
+
+    def own_copy(self, half, peer, sem):
+        return remote(
+            self.own.at[half],
+            self.buf.at[self.me, half],
+            self.send.at[sem],
+            self.recv.at[self.me, half],
+            peer,
+        )
+
+    def pass_copy(self, slot, half, peer, sem):
+        return remote(
+            self.buf.at[slot, half],
+            self.buf.at[slot, half],
+            self.send.at[sem],
+            self.recv.at[slot, half],
+            peer,
+        )
+
+    def own_copies(self):
+        return (
+            self.own_copy(0, self.xn, 0),
+            self.own_copy(1, self.yn, 1),
+            self.own_copy(0, self.sib, 2),
+            self.own_copy(1, self.sib, 3),
+            self.own_copy(1, self.xn, 4),
+            self.own_copy(0, self.yn, 5),
+        )
+
+    def near_copies(self):
+        return (
+            self.pass_copy(self.xn, 0, self.yn, 6),
+            self.pass_copy(self.yn, 1, self.xn, 7),
+            self.pass_copy(self.xn, 0, self.sib, 8),
+            self.pass_copy(self.yn, 1, self.sib, 9),
+        )
+
+    def late_copies(self):
+        return (
+            self.pass_copy(self.xn, 1, self.sib, 10),
+            self.pass_copy(self.yn, 0, self.sib, 11),
+        )
+
+    def far_copies(self):
+        return (
+            self.pass_copy(self.diag, 0, self.sib, 12),
+            self.pass_copy(self.diag, 1, self.sib, 13),
+        )
+
+    def wait_block(self, slot, half):
+        self.pass_copy(slot, half, self.sib, 0).wait_recv()
+
+    def begin(self):
+        plane_barrier((self.sib, self.xn, self.yn))
+        for copy in self.own_copies():
+            copy.start()
+
+    def place(self, step):
+        quad = lax.div(step, 4)
+        far_x, far_y = step_place(step, quad)
+        odd = lax.rem(step, 2)
+        third = lax.div(quad, 2) * (1 - lax.div(quad, 3))
+        other = lax.div(lax.rem(step, 4), 2)
+        slot = (
+            self.me
+            + far_x * (self.xn - self.me)
+            + far_y * (self.yn - self.me)
+            + other * (self.sib - self.me)
+        )
+        return slot, odd + third * (1 - 2 * odd), other
+
+    def arrive(self, step):
+        @pl.when(step == 4)
+        def _():
+            self.wait_block(self.xn, 0)
+            self.wait_block(self.yn, 1)
+            for copy in self.near_copies():
+                copy.start()
+
+        @pl.when(step == 8)
+        def _():
+            self.wait_block(self.xn, 1)
+            self.wait_block(self.yn, 0)
+            for copy in self.late_copies():
+                copy.start()
+
+        @pl.when(step == 12)
+        def _():
+            self.wait_block(self.diag, 0)
+            self.wait_block(self.diag, 1)
+            for copy in self.far_copies():
+                copy.start()
+
+        slot, half, other = self.place(step)
+
+        @pl.when(other == 1)
+        def _():
+            self.wait_block(slot, half)
+
+        return slot, half
+
+    def finish(self):
+        for copies in (self.own_copies(), self.near_copies(), self.late_copies(), self.far_copies()):
+            for copy in copies:
+                copy.wait_send()
+
+
+def expert_in_kernel(own, gate_hbm, up_hbm, rows_out, gua_out, buf, gua, gate_w, up_w, send, recv, load, store_a, store_b):
+    width, hidden = gate_w.shape
+    gather = Gather(own, buf, send, recv)
+    loads = (
+        pltpu.make_async_copy(gate_hbm, gate_w, load.at[0]),
+        pltpu.make_async_copy(up_hbm, up_w, load.at[1]),
+        pltpu.make_async_copy(own.at[0], buf.at[gather.me, 0], load.at[2]),
+        pltpu.make_async_copy(own.at[1], buf.at[gather.me, 1], load.at[3]),
+    )
+    for copy in loads:
+        copy.start()
+    gather.begin()
+    for copy in loads:
+        copy.wait()
+
+    def row_store(slot, half, step):
+        return pltpu.make_async_copy(buf.at[slot, half], rows_out.at[slot, half], store_a.at[step])
+
+    def gua_store(slot, half, step):
+        return pltpu.make_async_copy(gua.at[slot, half], gua_out.at[slot, half], store_b.at[step])
+
+    def one(step, carry):
+        slot, half = gather.arrive(step)
+        row_store(slot, half, step).start()
+        rows = buf[slot, half, :, :width]
+        lanes = lax.broadcasted_iota(jnp.int32, (buf.shape[2], 128), 1)
+        tail = buf[slot, half, :, width:].astype(jnp.float32)
+        weight = jnp.sum(jnp.where(lanes == gather.me, tail, 0.0), axis=1, keepdims=True)
+        gate_val = nn_dot(rows, gate_w[...])
+        up_val = nn_dot(rows, up_w[...])
+        gua[slot, half, :, :hidden] = gate_val.astype(jnp.bfloat16)
+        gua[slot, half, :, hidden : 2 * hidden] = up_val.astype(jnp.bfloat16)
+        act_val = jnp.maximum(gate_val, 0.0) * up_val * weight
+        gua[slot, half, :, 2 * hidden :] = act_val.astype(jnp.bfloat16)
+        gua_store(slot, half, step).start()
+        return carry
+
+    lax.fori_loop(0, 16, one, 0)
+    gather.finish()
+
+    def drain(step, carry):
+        slot, half, _ = gather.place(step)
+        row_store(slot, half, step).wait()
+        gua_store(slot, half, step).wait()
+        return carry
+
+    lax.fori_loop(0, 16, drain, 0)
+
+
+def expert_in(own, gate_w, up_w):
+    _, half, columns = own.shape
+    width, hidden = gate_w.shape
+    bf = jnp.bfloat16
+    return pl.pallas_call(
+        expert_in_kernel,
+        out_shape=(
+            jax.ShapeDtypeStruct((8, 2, half, columns), bf),
+            jax.ShapeDtypeStruct((8, 2, half, 3 * hidden), bf),
+        ),
+        in_specs=[ANY] * 3,
+        out_specs=(ANY, ANY),
+        scratch_shapes=[
+            pltpu.VMEM((8, 2, half, columns), bf),
+            pltpu.VMEM((8, 2, half, 3 * hidden), bf),
+            pltpu.VMEM((width, hidden), bf),
+            pltpu.VMEM((width, hidden), bf),
+            pltpu.SemaphoreType.DMA((14,)),
+            pltpu.SemaphoreType.DMA((8, 2)),
+            pltpu.SemaphoreType.DMA((4,)),
+            pltpu.SemaphoreType.DMA((16,)),
+            pltpu.SemaphoreType.DMA((16,)),
+        ],
+        compiler_params=pltpu.CompilerParams(
+            collective_id=1, has_side_effects=True, vmem_limit_bytes=VMEM_BYTES
+        ),
+        name="expert_in",
+    )(own, gate_w, up_w)
+
+
+def add_rows(target, others, chunk=64):
+    def one(index, carry):
+        rows = pl.ds(pl.multiple_of(index * chunk, chunk), chunk)
+        total = target[rows, :].astype(jnp.float32)
+        for other in others:
+            total = total + other[rows, :].astype(jnp.float32)
+        target[rows, :] = total.astype(target.dtype)
+        return carry
+
+    lax.fori_loop(0, target.shape[0] // chunk, one, 0)
+
+
+class Scatter:
+    def __init__(self, part, side, relay, final, send, side_sem, relay_sem, final_sem):
+        self.part, self.side, self.relay, self.final = part, side, relay, final
+        self.send, self.side_sem = send, side_sem
+        self.relay_sem, self.final_sem = relay_sem, final_sem
+        self.me, self.sib, self.xn, self.yn = plane_peers()
+        self.diag = self.xn + self.yn - self.me
+
+    def begin(self):
+        plane_barrier((self.sib, self.xn, self.yn))
+
+    def place(self, step):
+        quad = lax.div(step, 4)
+        far_x, far_y = step_place(step, 3 - quad)
+        odd = lax.rem(step, 2)
+        third = lax.div(quad, 2) * (1 - lax.div(quad, 3))
+        other = 1 - lax.div(lax.rem(step, 4), 2)
+        slot = (
+            self.me
+            + far_x * (self.xn - self.me)
+            + far_y * (self.yn - self.me)
+            + other * (self.sib - self.me)
+        )
+        return slot, odd + third * (1 - 2 * odd), other, far_x + 2 * far_y
+
+    def side_copy(self, step):
+        slot, half, _, place = self.place(step)
+        return remote(
+            self.part.at[slot, half],
+            self.side.at[place, half],
+            self.send.at[step],
+            self.side_sem.at[place, half],
+            self.sib,
+        )
+
+    def side_wait(self, place, half):
+        remote(
+            self.side.at[place, half],
+            self.side.at[place, half],
+            self.send.at[0],
+            self.side_sem.at[place, half],
+            self.sib,
+        ).wait_recv()
+
+    def relay_copy(self, step, way):
+        return remote(
+            self.part.at[self.diag, way],
+            self.relay.at[way],
+            self.send.at[step],
+            self.relay_sem.at[way],
+            (self.xn, self.yn)[way],
+        )
+
+    def final_copy(self, step, way, half):
+        return remote(
+            self.part.at[(self.xn, self.yn)[way], half],
+            self.final.at[way, half],
+            self.send.at[step],
+            self.final_sem.at[way, half],
+            (self.xn, self.yn)[way],
+        )
+
+    def depart(self, step):
+        slot, half, other, place = self.place(step)
+
+        @pl.when(other == 1)
+        def _():
+            self.side_copy(step).start()
+
+        for way in (0, 1):
+
+            @pl.when(step == 2 + way)
+            def _():
+                self.side_wait(3, way)
+                add_rows(self.part.at[self.diag, way], (self.side.at[3, way],))
+                self.relay_copy(2 + way, way).start()
+
+            peer = (self.xn, self.yn)[way]
+
+            @pl.when(step == 6 + way)
+            def _():
+                self.side_wait(1 + way, way)
+                add_rows(self.part.at[peer, way], (self.side.at[1 + way, way],))
+                self.final_copy(6 + way, way, way).start()
+
+            @pl.when(step == 15)
+            def _():
+                self.side_wait(1 + way, 1 - way)
+                self.relay_copy(3 - way, 1 - way).wait_recv()
+                add_rows(
+                    self.part.at[peer, 1 - way], (self.side.at[1 + way, 1 - way], self.relay.at[1 - way])
+                )
+                self.final_copy(10 + way, way, 1 - way).start()
+
+    def finish(self, out):
+        half_rows = out.shape[1]
+        chunk = 64
+        for half in (0, 1):
+            self.side_wait(0, half)
+            self.final_copy(0, 0, half).wait_recv()
+            self.final_copy(0, 1, half).wait_recv()
+
+            def one(index, carry):
+                rows = pl.ds(pl.multiple_of(index * chunk, chunk), chunk)
+                total = self.part[self.me, half, rows, :].astype(jnp.float32)
+                total = total + self.side[0, half, rows, :].astype(jnp.float32)
+                total = total + self.final[0, half, rows, :].astype(jnp.float32)
+                total = total + self.final[1, half, rows, :].astype(jnp.float32)
+                out[half, rows, :] = total
+                return carry
+
+            lax.fori_loop(0, half_rows // chunk, one, 0)
+        for way in (0, 1):
+            self.relay_copy(2 + way, way).wait_send()
+            self.final_copy(6 + way, way, way).wait_send()
+            self.final_copy(10 + way, way, 1 - way).wait_send()
+
+        def drain(step, carry):
+            @pl.when(self.place(step)[2] == 1)
+            def _():
+                self.side_copy(step).wait_send()
+
+            return carry
+
+        lax.fori_loop(0, 16, drain, 0)
+
+
+def scatter_scratch(half, columns):
+    bf = jnp.bfloat16
+    return [
+        pltpu.VMEM((8, 2, half, columns), bf),
+        pltpu.VMEM((4, 2, half, columns), bf),
+        pltpu.VMEM((2, half, columns), bf),
+        pltpu.VMEM((2, 2, half, columns), bf),
+        pltpu.SemaphoreType.DMA((16,)),
+        pltpu.SemaphoreType.DMA((4, 2)),
+        pltpu.SemaphoreType.DMA((2,)),
+        pltpu.SemaphoreType.DMA((2, 2)),
+    ]
+
+
+def expert_out_kernel(gua_hbm, down_hbm, out, act, down_w, load, part, side, relay, final, send, side_sem, relay_sem, final_sem):
+    hidden = down_w.shape[0]
+    scatter = Scatter(part, side, relay, final, send, side_sem, relay_sem, final_sem)
+    down_load = pltpu.make_async_copy(down_hbm, down_w, load.at[16])
+    down_load.start()
+
+    def act_load(step):
+        slot, half, _, _ = scatter.place(step)
+        return pltpu.make_async_copy(
+            gua_hbm.at[slot, half, :, pl.ds(2 * hidden, hidden)], act.at[slot, half], load.at[step]
+        )
+
+    def fetch(step, carry):
+        act_load(step).start()
+        return carry
+
+    lax.fori_loop(0, 16, fetch, 0)
+    scatter.begin()
+    down_load.wait()
+
+    def one(step, carry):
+        slot, half, _, _ = scatter.place(step)
+        act_load(step).wait()
+        part[slot, half] = nn_dot(act[slot, half], down_w[...]).astype(jnp.bfloat16)
+        scatter.depart(step)
+        return carry
+
+    lax.fori_loop(0, 16, one, 0)
+    scatter.finish(out)
+
+
+def expert_out(gua, down_w):
+    half = gua.shape[2]
+    hidden, width = down_w.shape
+    return pl.pallas_call(
+        expert_out_kernel,
+        out_shape=jax.ShapeDtypeStruct((2, half, width), jnp.float32),
+        in_specs=[ANY] * 2,
+        out_specs=pl.BlockSpec(memory_space=pltpu.VMEM),
+        scratch_shapes=[
+            pltpu.VMEM((8, 2, half, hidden), jnp.bfloat16),
+            pltpu.VMEM((hidden, width), jnp.bfloat16),
+            pltpu.SemaphoreType.DMA((17,)),
+        ]
+        + scatter_scratch(half, width),
+        compiler_params=pltpu.CompilerParams(
+            collective_id=2, has_side_effects=True, vmem_limit_bytes=VMEM_BYTES
+        ),
+        name="expert_out",
+    )(gua, down_w)
+
+
+def expert_back_kernel(own, rows_hbm, gua_hbm, gate_hbm, up_hbm, down_hbm, grads_out, dgu_out, part_out, buf, gu, tails, part, gate_w, up_w, down_w, send, recv, load, load_gu, load_tail, store_a, store_b, store_c):
+    width, hidden = gate_w.shape
+    gather = Gather(own, buf, send, recv)
+    loads = (
+        pltpu.make_async_copy(down_hbm, down_w, load.at[0]),
+        pltpu.make_async_copy(own.at[0], buf.at[gather.me, 0], load.at[1]),
+        pltpu.make_async_copy(own.at[1], buf.at[gather.me, 1], load.at[2]),
+        pltpu.make_async_copy(gate_hbm, gate_w, load.at[3]),
+        pltpu.make_async_copy(up_hbm, up_w, load.at[4]),
+    )
+    for copy in loads:
+        copy.start()
+
+    def block_loads(step):
+        slot, half, _ = gather.place(step)
+        return (
+            pltpu.make_async_copy(
+                gua_hbm.at[slot, half, :, pl.ds(0, 2 * hidden)], gu.at[slot, half], load_gu.at[step]
+            ),
+            pltpu.make_async_copy(
+                rows_hbm.at[slot, half, :, pl.ds(width, 128)], tails.at[slot, half], load_tail.at[step]
+            ),
+        )
+
+    def fetch(step, carry):
+        for copy in block_loads(step):
+            copy.start()
+        return carry
+
+    lax.fori_loop(0, 16, fetch, 0)
+    gather.begin()
+    for copy in loads:
+        copy.wait()
+
+    def stores(step):
+        slot, half, _ = gather.place(step)
+        return (
+            pltpu.make_async_copy(buf.at[slot, half], grads_out.at[slot, half], store_a.at[step]),
+            pltpu.make_async_copy(gu.at[slot, half], dgu_out.at[slot, half], store_b.at[step]),
+            pltpu.make_async_copy(part.at[slot, half], part_out.at[slot, half], store_c.at[step]),
+        )
+
+    def one(step, carry):
+        slot, half = gather.arrive(step)
+        store_rows, store_dgu, store_part = stores(step)
+        store_rows.start()
+        for copy in block_loads(step):
+            copy.wait()
+        lanes = lax.broadcasted_iota(jnp.int32, (buf.shape[2], 128), 1)
+        tail = tails[slot, half].astype(jnp.float32)
+        weight = jnp.sum(jnp.where(lanes == gather.me, tail, 0.0), axis=1, keepdims=True)
+        grad_act = nt_dot(buf[slot, half], down_w[...])
+        gate_val = gu[slot, half, :, :hidden].astype(jnp.float32)
+        up_val = gu[slot, half, :, hidden:].astype(jnp.float32)
+        gate_relu = jnp.maximum(gate_val, 0.0)
+        grad_comb = jnp.sum(gate_relu * up_val * grad_act, axis=1, keepdims=True)
+        grad_act = grad_act * weight
+        grad_gate = jnp.where(gate_val > 0, grad_act * up_val, 0.0).astype(jnp.bfloat16)
+        grad_up = (grad_act * gate_relu).astype(jnp.bfloat16)
+        gu[slot, half, :, :hidden] = grad_gate
+        gu[slot, half, :, hidden:] = grad_up
+        store_dgu.start()
+        part[slot, half, :, :width] = (
+            nt_dot(grad_gate, gate_w[...]) + nt_dot(grad_up, up_w[...])
+        ).astype(jnp.bfloat16)
+        part[slot, half, :, width:] = jnp.where(lanes == gather.me, grad_comb, 0.0).astype(
+            jnp.bfloat16
+        )
+        store_part.start()
+        return carry
+
+    lax.fori_loop(0, 16, one, 0)
+    gather.finish()
+
+    def drain(step, carry):
+        for copy in stores(step):
+            copy.wait()
+        return carry
+
+    lax.fori_loop(0, 16, drain, 0)
+
+
+def expert_back(own, rows_all, gua, gate_w, up_w, down_w):
+    _, half, columns = rows_all.shape[1:]
+    width, hidden = gate_w.shape
+    bf = jnp.bfloat16
+    return pl.pallas_call(
+        expert_back_kernel,
+        out_shape=(
+            jax.ShapeDtypeStruct((8, 2, half, width), bf),
+            jax.ShapeDtypeStruct((8, 2, half, 2 * hidden), bf),
+            jax.ShapeDtypeStruct((8, 2, half, columns), bf),
+        ),
+        in_specs=[ANY] * 6,
+        out_specs=(ANY,) * 3,
+        scratch_shapes=[
+            pltpu.VMEM((8, 2, half, width), bf),
+            pltpu.VMEM((8, 2, half, 2 * hidden), bf),
+            pltpu.VMEM((8, 2, half, 128), bf),
+            pltpu.VMEM((8, 2, half, columns), bf),
+            pltpu.VMEM((width, hidden), bf),
+            pltpu.VMEM((width, hidden), bf),
+            pltpu.VMEM((hidden, width), bf),
+            pltpu.SemaphoreType.DMA((14,)),
+            pltpu.SemaphoreType.DMA((8, 2)),
+            pltpu.SemaphoreType.DMA((5,)),
+        ]
+        + [pltpu.SemaphoreType.DMA((16,))] * 5,
+        compiler_params=pltpu.CompilerParams(
+            collective_id=3, has_side_effects=True, vmem_limit_bytes=VMEM_BYTES
+        ),
+        name="expert_back",
+    )(own, rows_all, gua, gate_w, up_w, down_w)
+
+
+def scatter_kernel(part_hbm, out, load, part, side, relay, final, send, side_sem, relay_sem, final_sem):
+    scatter = Scatter(part, side, relay, final, send, side_sem, relay_sem, final_sem)
+
+    def part_load(step):
+        slot, half, _, _ = scatter.place(step)
+        return pltpu.make_async_copy(part_hbm.at[slot, half], part.at[slot, half], load.at[step])
+
+    def fetch(step, carry):
+        part_load(step).start()
+        return carry
+
+    lax.fori_loop(0, 16, fetch, 0)
+    scatter.begin()
+
+    def one(step, carry):
+        part_load(step).wait()
+        scatter.depart(step)
+        return carry
+
+    lax.fori_loop(0, 16, one, 0)
+    scatter.finish(out)
+
+
+def plane_scatter(part, ident):
+    _, _, half, columns = part.shape
+    return pl.pallas_call(
+        scatter_kernel,
+        out_shape=jax.ShapeDtypeStruct((2, half, columns), jnp.float32),
+        in_specs=[ANY],
+        out_specs=pl.BlockSpec(memory_space=pltpu.VMEM),
+        scratch_shapes=[pltpu.SemaphoreType.DMA((16,))] + scatter_scratch(half, columns),
+        compiler_params=pltpu.CompilerParams(
+            collective_id=ident, has_side_effects=True, vmem_limit_bytes=VMEM_BYTES
+        ),
+        name="plane_scatter",
+    )(part)
+
+
+def body_plane(
+    tokens,
+    targets,
+    valid_count,
+    segments,
+    routes,
+    gain_attn,
+    w_query,
+    w_key,
+    w_value,
+    w_out,
+    gain_moe,
+    w_router,
+    w_gate,
+    w_up,
+    w_down,
+):
+    bf = jnp.bfloat16
+    num_rows, width = tokens.shape
+    half = num_rows // 2
+    q_cols, k_cols = w_query.shape[1], w_key.shape[1]
+    qkv_cols = q_cols + 2 * k_cols
+    dense_cols = qkv_cols + w_out.shape[1]
+    num_experts = w_router.shape[1]
+    num_heads = q_cols // HD
+    kv_heads = k_cols // HD
+    group_size = num_heads // kv_heads
+    pad_cols = 128 - 2 - num_experts
+    dense_own = jnp.concatenate(
+        [
+            w_query,
+            w_key,
+            w_value,
+            w_out,
+            gain_attn[:, None],
+            gain_moe[:, None],
+            w_router,
+            jnp.zeros((gain_attn.shape[0], pad_cols), bf),
+        ],
+        axis=1,
+    )
+    dense_w = lax.all_gather(dense_own, ("dp", "exp"), axis=0, tiled=True)
+    gate_w = lax.all_gather(w_gate, "dp", axis=1, tiled=True)[0]
+    up_w = lax.all_gather(w_up, "dp", axis=1, tiled=True)[0]
+    down_w = lax.all_gather(w_down, "dp", axis=1, tiled=True)[0]
+    qkv_w = dense_w[:, :qkv_cols]
+    out_w = dense_w[:, qkv_cols:dense_cols]
+    gain_one = dense_w[:, dense_cols].astype(jnp.float32)
+    gain_two = dense_w[:, dense_cols + 1].astype(jnp.float32)
+    router_w = dense_w[:, dense_cols + 2 : dense_cols + 2 + num_experts]
+    tok_pos = positions(segments)
+    allowed = key_mask(segments)
+    resid_in = tokens.astype(jnp.float32)
+    inv_one = lax.rsqrt(jnp.mean(resid_in * resid_in, axis=-1, keepdims=True) + EPS)
+    normed_one = resid_in * inv_one
+    hidden_one = (normed_one * gain_one).astype(bf)
+    qkv_raw = jnp.dot(hidden_one, qkv_w, preferred_element_type=jnp.float32)
+    value_b = qkv_raw[:, q_cols + k_cols :].astype(bf)
+    query_b = rotate(qkv_raw[:, :q_cols].reshape(num_rows, num_heads, HD), tok_pos, 1.0).astype(bf)
+    query_b = query_b.reshape(num_rows, kv_heads, group_size, HD)
+    key_b = rotate(
+        qkv_raw[:, q_cols : q_cols + k_cols].reshape(num_rows, kv_heads, HD), tok_pos, 1.0
+    ).astype(bf)
+    value_h = value_b.reshape(num_rows, kv_heads, HD)
+    logit_att = attention_scores(query_b, key_b, allowed)
+    row_max = jnp.max(logit_att, axis=-1, keepdims=True)
+    log_total = row_max + jnp.log(jnp.sum(jnp.exp(logit_att - row_max), axis=-1, keepdims=True))
+    probs_b = jnp.exp(logit_att - log_total).astype(bf)
+    attn_vals = jnp.einsum("kgqp,pkd->qkgd", probs_b, value_h, preferred_element_type=jnp.float32)
+    attn_vals = attn_vals.reshape(num_rows, q_cols).astype(bf)
+    resid_mid = resid_in + jnp.dot(attn_vals, out_w, preferred_element_type=jnp.float32)
+    inv_two = lax.rsqrt(jnp.mean(resid_mid * resid_mid, axis=-1, keepdims=True) + EPS)
+    normed_two = resid_mid * inv_two
+    hidden_two = (normed_two * gain_two).astype(bf)
+    router_prob = jax.nn.softmax(
+        jnp.dot(hidden_two, router_w, preferred_element_type=jnp.float32), axis=-1
+    )
+    expert_ids = jnp.arange(num_experts, dtype=jnp.int32)
+    route_hot = routes[:, :, None] == expert_ids[None, None, :]
+    chosen = jnp.sum(jnp.where(route_hot, router_prob[:, None, :], 0.0), axis=-1)
+    weight_sum = jnp.sum(chosen, axis=1, keepdims=True)
+    combine = chosen / weight_sum
+    weight_full = jnp.sum(jnp.where(route_hot, combine[:, :, None], 0.0), axis=1)
+    rows_own = jnp.concatenate(
+        [hidden_two, jnp.pad(weight_full.astype(bf), ((0, 0), (0, 128 - num_experts)))], axis=1
+    )
+    rows_all, gua = expert_in(rows_own.reshape(2, half, width + 128), gate_w, up_w)
+    moe_out = expert_out(gua, down_w).reshape(num_rows, width)
+    resid_out = resid_mid + moe_out
+    layer_out = resid_out.astype(bf)
+    total_rows = num_rows * lax.axis_size(("dp", "exp"))
+    global_row = lax.axis_index(("dp", "exp")) * num_rows + jnp.arange(num_rows, dtype=jnp.int32)
+    loss_scale = total_rows / valid_count[0].astype(jnp.float32)
+    grad_out = jnp.where(
+        (global_row < valid_count[0])[:, None],
+        (resid_out - targets.astype(jnp.float32)) * loss_scale,
+        0.0,
+    )
+    grads_all, dgu, part = expert_back(
+        grad_out.astype(bf).reshape(2, half, width), rows_all, gua, gate_w, up_w, down_w
+    )
+    back = plane_scatter(part, 4).reshape(num_rows, width + 128)
+    hidden = gate_w.shape[1]
+    flat_rows = rows_all.reshape(-1, width + 128)[:, :width]
+    flat_grads = grads_all.reshape(-1, width)
+    grad_gate_up = jnp.einsum(
+        "rd,rf->df", flat_rows, dgu.reshape(-1, 2 * hidden), preferred_element_type=jnp.float32
+    ).astype(bf)
+    grad_down_w = jnp.einsum(
+        "rf,rd->fd",
+        gua.reshape(-1, 3 * hidden)[:, 2 * hidden :],
+        flat_grads,
+        preferred_element_type=jnp.float32,
+    ).astype(bf)
+    expert_sums = tuple(
+        lax.psum_scatter(grad[None], "dp", scatter_dimension=1, tiled=True).astype(jnp.float32)
+        for grad in (grad_gate_up[:, :hidden], grad_gate_up[:, hidden:], grad_down_w)
+    )
+    grad_hidden_two = back[:, :width]
+    grad_comb = jnp.sum(
+        jnp.where(route_hot, back[:, None, width : width + num_experts], 0.0), axis=-1
+    )
+    grad_chosen = (grad_comb - jnp.sum(grad_comb * combine, axis=1, keepdims=True)) / weight_sum
+    grad_prob = jnp.sum(jnp.where(route_hot, grad_chosen[:, :, None], 0.0), axis=1)
+    grad_logit = router_prob * (
+        grad_prob - jnp.sum(router_prob * grad_prob, axis=-1, keepdims=True)
+    )
+    grad_hidden_two = grad_hidden_two + jnp.einsum(
+        "re,de->rd", grad_logit, router_w.astype(jnp.float32), precision=HIGH
+    )
+    grad_router = jnp.einsum(
+        "rd,re->de", hidden_two.astype(jnp.float32), grad_logit, precision=HIGH
+    )
+    grad_gain_two = jnp.sum(grad_hidden_two * normed_two, axis=0)
+    grad_norm_two = grad_hidden_two * gain_two
+    grad_mid = grad_out + inv_two * (
+        grad_norm_two - normed_two * jnp.mean(grad_norm_two * normed_two, axis=-1, keepdims=True)
+    )
+    grad_proj_b = grad_mid.astype(bf)
+    grad_out_w = jnp.einsum("rh,rd->hd", attn_vals, grad_proj_b, preferred_element_type=jnp.float32)
+    grad_vals_b = jnp.einsum(
+        "rd,hd->rh", grad_proj_b, out_w, preferred_element_type=jnp.float32
+    ).astype(bf)
+    grad_vals_b = grad_vals_b.reshape(num_rows, kv_heads, group_size, HD)
+    logit_att = attention_scores(query_b, key_b, allowed)
+    probs = jnp.exp(logit_att - log_total)
+    probs_b = probs.astype(bf)
+    grad_value = jnp.einsum(
+        "kgqp,qkgd->pkd", probs_b, grad_vals_b, preferred_element_type=jnp.float32
+    )
+    grad_prob_att = jnp.einsum(
+        "qkgd,pkd->kgqp", grad_vals_b, value_h, preferred_element_type=jnp.float32
+    )
+    delta_row = jnp.sum(probs * grad_prob_att, axis=-1, keepdims=True)
+    grad_score_b = (probs * (grad_prob_att - delta_row)).astype(bf)
+    grad_query = jnp.einsum(
+        "kgqp,pkd->qkgd", grad_score_b, key_b, preferred_element_type=jnp.float32
+    ) * HD ** (-0.5)
+    grad_key = jnp.einsum(
+        "kgqp,qkgd->pkd", grad_score_b, query_b, preferred_element_type=jnp.float32
+    ) * HD ** (-0.5)
+    grad_query_b = rotate(grad_query.reshape(num_rows, num_heads, HD), tok_pos, -1.0).astype(bf)
+    grad_key_b = rotate(grad_key, tok_pos, -1.0).astype(bf)
+    grad_qkv_b = jnp.concatenate(
+        [
+            grad_query_b.reshape(num_rows, q_cols),
+            grad_key_b.reshape(num_rows, k_cols),
+            grad_value.astype(bf).reshape(num_rows, k_cols),
+        ],
+        axis=1,
+    )
+    grad_qkv_w = jnp.einsum("rd,rh->dh", hidden_one, grad_qkv_b, preferred_element_type=jnp.float32)
+    grad_hidden_one = jnp.einsum("rh,dh->rd", grad_qkv_b, qkv_w, preferred_element_type=jnp.float32)
+    grad_gain_one = jnp.sum(grad_hidden_one * normed_one, axis=0)
+    grad_norm_one = grad_hidden_one * gain_one
+    grad_in = grad_mid + inv_one * (
+        grad_norm_one - normed_one * jnp.mean(grad_norm_one * normed_one, axis=-1, keepdims=True)
+    )
+    dense_grad = jnp.concatenate(
+        [
+            grad_qkv_w.astype(bf),
+            grad_out_w.astype(bf),
+            jnp.pad(
+                jnp.concatenate([grad_gain_one[:, None], grad_gain_two[:, None], grad_router], axis=1),
+                ((0, 0), (0, pad_cols)),
+            ).astype(bf),
+        ],
+        axis=1,
+    )
+    dense_sum = lax.psum_scatter(
+        dense_grad, ("dp", "exp"), scatter_dimension=0, tiled=True
+    ).astype(jnp.float32)
+    return (
+        layer_out,
+        grad_in,
+        dense_sum[:, dense_cols],
+        dense_sum[:, :q_cols],
+        dense_sum[:, q_cols : q_cols + k_cols],
+        dense_sum[:, q_cols + k_cols : qkv_cols],
+        dense_sum[:, qkv_cols:dense_cols],
+        dense_sum[:, dense_cols + 1],
+        dense_sum[:, dense_cols + 2 : dense_cols + 2 + num_experts],
+        *expert_sums,
+    )
+
+
 def solution(mesh):
     in_specs = (
         P(("dp", "exp"), None),
@@ -338,4 +1145,5 @@
         P("exp", "dp", None),
         P("exp", "dp", None),
     )
+    body = body_plane if mesh.shape["exp"] == 8 else body_general
     return jax.shard_map(body, mesh=mesh, in_specs=in_specs, out_specs=out_specs, check_vma=False)

time: 1380 us -> 799 us (0.58)
  waiting for transfers between devices: 614 us -> 300 us
  blocking collectives: 283 us -> 0 us
  Pallas kernels: 0 us -> 259 us
  local copies, waits for them, and re-layouts: 139 us -> 39.5 us
  matrix products: 194 us -> 121 us
  other arithmetic: 112 us -> 56.8 us
  starting transfers between devices: 20.7 us -> 0.57 us
    pallas_call x0 -> x4, Pallas kernels: none -> 259 us  [the longest x1 67.3 us: expert_back(): pl.pallas_call(expert_back_kernel, out_shape=(jax.ShapeDtypeStruct((8, 2,...]
    all_to_all x4 -> x0, waiting for transfers between devices: 227 us -> none  [the longest x1 87.2 us: body(): lax.all_to_all(send_rows, 'exp', split_axis=0, concat_axis=0, tiled=True)]
    reduce_scatter x7 -> x4, waiting for transfers between devices: 383 us -> 164 us  [the longest x1 150 us: body_plane(): lax.psum_scatter(dense_grad, ('dp', 'exp'), scatter_dimension=0, tiled=True)]
    all_gather x3 -> x0, blocking collectives: 203 us -> none  [the longest x1 118 us: body(): lax.all_gather(w_router, ('dp', 'exp'), axis=0, tiled=True)]
    all_gather x5 -> x4, waiting for transfers between devices: 0.05 us -> 134 us  [the longest x1 85.8 us: body_plane(): dense_w = lax.all_gather(dense_own, ('dp', 'exp'), axis=0, tiled=True)]
    unnamed x2 -> x0, blocking collectives: 79.5 us -> none
    dot_general x28 -> x16, matrix products: 185 us -> 118 us  [the longest x1 26.1 us: body_plane(): jnp.einsum('rd,rf->df', flat_rows, dgu.reshape(-1, 2 * hidden), preferred...]
    reduce_sum x11 -> x9, other arithmetic: 60.4 us -> 5.97 us  [the longest x1 2.65 us: body_plane(): jnp.sum(jnp.exp(logit_att - row_max), axis=-1, keepdims=True)]
  transfers between devices with their start and end apart: 17 -> 8, of which waited for: 6 -> 4; matrix products, arithmetic and copies ran while one was open for 23% -> 21% of each run, Pallas kernels for 0% -> 16%
where the time goes in v1:
time: 799 us; the launch traced here: 793 us
  waiting for transfers between devices  300 us (38%)
  Pallas kernels  259 us (32%)
  matrix products  121 us (15%)
  other arithmetic  56.8 us (7%)
  local copies, waits for them, and re-layouts  39.5 us (5%)
  between operations  16.2 us (2%)
    reduce_scatter x1, waiting for transfers between devices, body_plane(): lax.psum_scatter(dense_grad, ('dp', 'exp'), scatter_dimension=0, tiled=True)  150 us
    all_gather x1, waiting for transfers between devices, body_plane(): dense_w = lax.all_gather(dense_own, ('dp', 'exp'), axis=0, tiled=True)  85.8 us
    pallas_call x1, Pallas kernels, expert_back(): pl.pallas_call(expert_back_kernel, out_shape=(jax.ShapeDtypeStruct((8, 2,...  67.3 us
    pallas_call x1, Pallas kernels, expert_in(): pl.pallas_call(expert_in_kernel, out_shape=(jax.ShapeDtypeStruct((8, 2, h...  65.5 us
    pallas_call x1, Pallas kernels, plane_scatter(): pl.pallas_call(scatter_kernel, out_shape=jax.ShapeDtypeStruct((2, half, c...  64.3 us
    pallas_call x1, Pallas kernels, expert_out(): pl.pallas_call(expert_out_kernel, out_shape=jax.ShapeDtypeStruct((2, half...  61.8 us
    all_gather x1, waiting for transfers between devices, body_plane(): up_w = lax.all_gather(w_up, 'dp', axis=1, tiled=True)[0]  48.5 us
    dot_general x1, matrix products, body_plane(): jnp.einsum('rd,rf->df', flat_rows, dgu.reshape(-1, 2 * hidden), preferred...  26.1 us
  transfers between devices with their start and end apart: 8, of which 4 were waited for; matrix products, arithmetic and copies ran while one was open for 21% of the time, Pallas kernels for 16%

profile of v1, /device:TPU:0, one launch (start us, length us, event | category | flops | bytes accessed | tf_op | source)
XLA Modules:
  0.0 793.4 jit_solution(8598796491489929469)
XLA Ops:
  18.6 85.8 %all-gather.5.cloned.1.call-done = bf16[1536,3712]{1,0:T(8,128)(2,1)} async-done(((bf16[48,3712]{1,0:T(8,128)(2,1)}), bf16[1536,3712]{1,0:T(8,128)(2,1)}) %all-gather.5.cloned.1.call-update) | async-done | bytes 11403280 | tf_op jit(solution)/shard_map/all_gather | solution.py:951
  106.0 5.6 fusion.16
  115.6 2.7 fusion.76
  120.7 3.3 subtract_convert_fusion.1
  129.3 3.4 fusion.11
  132.8 2.6 exponential_reduce_fusion
  137.3 8.1 %convolution_convert_fusion.3 = bf16[2,128,6,512]{3,1,2,0:T(8,128)(2,1)S(1)} fusion(bf16[512,2,128,1]{2,1,0,3:T(2,128)(2,1)S(1)} %bitcast.125, f32[2,512,512,6]{2,1,3,0:T(8,128)} %copy-done, f32[2,6,512]{2,1,0:T(8,128)S(1)} %log_add_fusion, pred[512,512]{0,1:T(8,128)(4,1)S(1)} %fusion.51), kind=kOutput, calls=%fused_computation.62 | convolution fusion | flops 818675712 | bytes 14704640 | tf_op jit(solution)/shard_map/kgqp,pkd->qkgd/dot_general | solution.py:978
  145.4 5.4 multiply_reduce_fusion.2
  156.5 48.5 %all-gather.9.cloned.1.call-done = bf16[1,1536,768]{2,1,0:T(8,128)(2,1)} async-done(((bf16[1,384,768]{2,1,0:T(8,128)(2,1)}), bf16[1,1536,768]{2,1,0:T(8,128)(2,1)}) %all-gather.9.cloned.1.call-update) | async-done | bytes 2359312 | tf_op jit(solution)/shard_map/all_gather | solution.py:953
  205.0 65.5 %expert_in.1 = (bf16[8,2,256,1664]{3,2,1,0:T(8,128)(2,1)}, bf16[8,2,256,2304]{3,2,1,0:T(8,128)(2,1)}) custom-call(bf16[2,256,1664]{2,1,0:T(8,128)(2,1)} %bitcast.119, bf16[1536,768]{1,0:T(8,128)(2,1)} %bitcast.115, bf16[1536,768]{1,0:T(8,128)(2,1)} %bitcast.117), custom_call_target="tpu_custom_call" | custom-call | tf_op jit(solution)/shard_map/expert_in/pallas_call | solution.py:526
  270.5 61.8 %expert_out.1 = f32[2,256,1536]{2,1,0:T(8,128)} custom-call(bf16[8,2,256,2304]{3,2,1,0:T(8,128)(2,1)} %get-tuple-element.17.gua_hbm, bf16[768,1536]{1,0:T(8,128)(2,1)} %bitcast.113), custom_call_target="tpu_custom_call" | custom-call | tf_op jit(solution)/shard_map/expert_out/pallas_call | solution.py:739
  332.3 5.1 fusion.45
  337.3 67.3 %expert_back.1 = (bf16[8,2,256,1536]{3,2,1,0:T(8,128)(2,1)}, bf16[8,2,256,1536]{3,2,1,0:T(8,128)(2,1)}, bf16[8,2,256,1664]{3,2,1,0:T(8,128)(2,1)}) custom-call(bf16[2,256,1536]{2,1,0:T(8,128)(2,1)} %bitcast.120, bf16[8,2,256,1664]{3,2,1,0:T(8,128)(2,1)} %get-tuple-element.18.rows_hbm, bf16[8,2,256,2304]{3,2,1,0:T(8,128)(2,1)} %get-tuple-element.17.gua_hbm, ...), custom_call_target="tpu_custom_call" | custom-call | tf_op jit(solution)/shard_map/expert_back/pallas_call | solution.py:843
  404.6 26.1 %fusion.8 = bf16[1536,1536]{1,0:T(8,128)(2,1)S(1)} fusion(bf16[4096,1536]{1,0:T(8,128)(2,1)} %bitcast.134, bf16[4096,1664]{1,0:T(8,128)(2,1)} %bitcast.108), kind=kOutput, calls=%fused_computation.14 | convolution fusion | flops 19329712128 | bytes 29884416 | tf_op jit(solution)/shard_map/rd,rf->df/dot_general | solution.py:1015
  434.1 64.3 %plane_scatter.1 = f32[2,256,1664]{2,1,0:T(8,128)} custom-call(bf16[8,2,256,1664]{3,2,1,0:T(8,128)(2,1)} %get-tuple-element.19.part_hbm), custom_call_target="tpu_custom_call" | custom-call | tf_op jit(solution)/shard_map/plane_scatter/pallas_call | solution.py:897
  503.1 5.8 multiply_reduce_fusion
  508.9 2.8 multiply_add_fusion
  513.4 6.0 fusion.42
  519.5 2.7 copy.153
  522.1 10.0 %fusion.3 = (f32[2,6,512]{2,1,0:T(8,128)S(1)}, f32[2,512,512,6]{2,1,3,0:T(8,128)}) fusion(f32[2,512,512,6]{2,1,3,0:T(8,128)} %copy-done, f32[2,6,512]{2,1,0:T(8,128)S(1)} %log_add_fusion, pred[512,512]{0,1:T(8,128)(4,1)S(1)} %fusion.51, bf16[512,2,6,128]{0,3,2,1:T(8,128)(2,1)} %bitcast.121, bf16[512,2,128,1]{2,1,0,3:T(2,128)(2,1)S(1)} %bitcast.126), kind=kOutput, calls=%fused_computation.6 | convolution fusion | flops 821028864 | bytes 27312128 | tf_op jit(solution)/shard_map/qkgd,pkd->kgqp/dot_general | solution.py:1060
  532.2 10.9 %fusion.5 = bf16[2,6,512,512]{2,3,1,0:T(8,128)(2,1)S(1)} fusion(f32[2,512,512,6]{2,1,3,0:T(8,128)} %get-tuple-element.123, f32[2,512,512,6]{2,1,3,0:T(8,128)} %copy-done, f32[2,6,512]{2,1,0:T(8,128)S(1)} %get-tuple-element.122, f32[2,6,512]{2,1,0:T(8,128)S(1)} %log_add_fusion, pred[512,512]{0,1:T(8,128)(4,1)S(1)} %fusion.51), kind=kLoop, calls=%fused_computation.8 | loop fusion | flops 18874368 | bytes 31768576 | tf_op jit(solution)/shard_map/convert_element_type | solution.py:1064
  546.8 5.9 convolution_multiply_fusion
  552.7 8.1 %fusion.49 = bf16[2,128,512]{2,1,0:T(8,128)(2,1)S(1)} fusion(bf16[512,2,6,128]{0,3,2,1:T(8,128)(2,1)S(1)} %bitcast.122, f32[2,512,512,6]{2,1,3,0:T(8,128)} %copy-done, f32[2,6,512]{2,1,0:T(8,128)S(1)} %log_add_fusion, pred[512,512]{0,1:T(8,128)(4,1)S(1)} %fusion.51), kind=kOutput, calls=%fused_computation.73 | convolution fusion | flops 818020352 | bytes 14704640 | tf_op jit(solution)/shard_map/kgqp,qkgd->pkd/dot_general | solution.py:1057
  560.9 12.8 %fusion.39 = bf16[1,768,1536]{2,1,0:T(8,128)(2,1)} fusion(bf16[4096,1536]{1,0:T(8,128)(2,1)S(1)} %bitcast.133, bf16[4096,2304]{1,0:T(8,128)(2,1)} %bitcast.103), kind=kOutput, calls=%fused_computation.53 | convolution fusion | flops 9664856064 | bytes 21233664 | tf_op jit(solution)/shard_map/rf,rd->fd/dot_general | solution.py:1018
  574.1 2.6 subtract_convert_fusion
  576.8 9.3 %fusion.35 = (bf16[1536]{0:T(1024)(128)(2,1)S(1)}, f32[512]{0:T(512)S(1)}, f32[512,1536]{1,0:T(8,128)}) fusion(bf16[512,1536]{1,0:T(8,128)(2,1)S(1)} %copy-done.14, f32[512]{0:T(512)S(1)} %copy-done.44, f32[1536]{0:T(1024)S(1)} %copy-done.39, bf16[1536,3712]{1,0:T(8,128)(2,1)} %all-gather.5.cloned.1.call-done, bf16[512,256]{0,1:T(8,128)(2,1)S(1)} %bitcast.137, ...), kind=kOutput, calls=%fused_computation.44 | convolution fusion | flops 3233019904 | bytes 13120512 | tf_op jit(solution)/shard_map/rh,dh->rd/dot_general | solution.py:1082
  587.2 5.1 convolution_convert_fusion
  592.3 5.4 convolution_convert_fusion.1
  597.7 5.0 fusion.6
  604.5 4.9 fusion.34
  613.7 13.9 %reduce-scatter.11.cloned.1.call-done = bf16[1,192,1536]{2,1,0:T(8,128)(2,1)} async-done(((bf16[1,768,1536]{2,1,0:T(8,128)(2,1)}), bf16[1,192,1536]{2,1,0:T(8,128)(2,1)}) %reduce-scatter.11.cloned.1.call-update) | async-done | bytes 589840 | tf_op jit(solution)/shard_map/reduce_scatter | solution.py:1025
  629.9 149.8 %reduce-scatter.5.cloned.1.call-done = bf16[48,3712]{1,0:T(8,128)(2,1)} async-done(((bf16[1536,3712]{1,0:T(8,128)(2,1)}), bf16[48,3712]{1,0:T(8,128)(2,1)}) %reduce-scatter.5.cloned.1.call-update) | async-done | bytes 356368 | tf_op jit(solution)/shard_map/reduce_scatter | solution.py:1099
  (188 shorter events, 60.8 us)
Async XLA Ops:
  7.2 6.5 copy-start.12
  7.2 6.9 copy-start.35
  7.2 97.2 %all-gather.5.cloned.1.call-start = ((), (), s32[]{:S(2)}) async-start(), calls=%async_computation.4 | async-start | bytes 11759616 | tf_op jit(solution)/shard_map/all_gather | solution.py:951
  11.5 145.0 %all-gather.7.cloned.1.call-start = ((), (), s32[]{:S(2)}) async-start(), calls=%async_computation.5 | async-start | bytes 2949120 | tf_op jit(solution)/shard_map/all_gather | solution.py:952
  12.3 192.7 %all-gather.9.cloned.1.call-start = ((), (), s32[]{:S(2)}) async-start(), calls=%async_computation.6 | async-start | bytes 2949120 | tf_op jit(solution)/shard_map/all_gather | solution.py:953
  13.0 257.5 %all-gather.11.cloned.1.call-start = ((), (), s32[]{:S(2)}) async-start(), calls=%async_computation.7 | async-start | bytes 2949120 | tf_op jit(solution)/shard_map/all_gather | solution.py:954
  13.6 595.8 %reduce-scatter.7.cloned.1.call-start = ((), (), s32[]{:S(2)}) async-start(), calls=%async_computation.9 | async-start | bytes 2949120 | tf_op jit(solution)/shard_map/reduce_scatter | solution.py:1025
  14.0 97.6 %copy-start.43 = (f32[512]{0:T(512)}, f32[512]{0:T(512)S(1)}, u32[]{:S(2)}) copy-start(f32[512]{0:T(512)S(1)} %add_rsqrt_fusion.1) | copy-start | bytes 6148
  15.5 96.1 %copy-start.26 = (f32[512,64]{0,1:T(8,128)}, f32[512,64]{0,1:T(8,128)S(1)}, u32[]{:S(2)}) copy-start(f32[512,64]{0,1:T(8,128)S(1)} %get-tuple-element.113) | copy-start | bytes 393220
  106.0 5.7 copy-start.38
  106.0 44.9 %copy-start.32 = (f32[1536]{0:T(1024)}, f32[1536]{0:T(1024)S(1)}, u32[]{:S(2)}) copy-start(f32[1536]{0:T(1024)S(1)} %get-tuple-element.82) | copy-start | bytes 18436
  124.8 7.9 copy-start.5
  127.2 5.6 copy-start.7
  137.3 8.1 %copy-start.27 = (bf16[512,2,128]{2,1,0:T(2,128)(2,1)}, bf16[512,2,128]{2,1,0:T(2,128)(2,1)S(1)}, u32[]{:S(2)}) copy-start(bf16[512,2,128]{2,1,0:T(2,128)(2,1)S(1)} %reshape.318) | copy-start | bytes 786436
  137.3 8.1 %copy-start.13 = (bf16[512,1536]{1,0:T(8,128)(2,1)S(1)}, bf16[512,1536]{1,0:T(8,128)(2,1)}, u32[]{:S(2)}) copy-start(bf16[512,1536]{1,0:T(8,128)(2,1)} %param.15) | copy-start | bytes 4718596
  433.2 178.3 %reduce-scatter.9.cloned.1.call-start = ((), (), s32[]{:S(2)}) async-start(), calls=%async_computation.10 | async-start | bytes 2949120 | tf_op jit(solution)/shard_map/reduce_scatter | solution.py:1025
  503.0 5.9 copy-start.3
  503.0 5.9 copy-start.4
  503.0 5.9 copy-start.11
  503.1 5.9 copy-start.33
  503.1 5.8 copy-start.41
  503.1 5.8 copy-start.45
  532.1 95.5 %reduce-scatter.11.cloned.1.call-start = ((), (), s32[]{:S(2)}) async-start(), calls=%async_computation.11 | async-start | bytes 2949120 | tf_op jit(solution)/shard_map/reduce_scatter | solution.py:1025
  532.2 10.9 %copy-start.6 = (bf16[512,12,64]{2,0,1:T(8,128)(2,1)S(1)}, bf16[512,12,64]{2,0,1:T(8,128)(2,1)}, u32[]{:S(2)}) copy-start(bf16[512,12,64]{2,0,1:T(8,128)(2,1)} %copy-done.5) | copy-start | bytes 2359300
  532.2 10.9 %copy-start.8 = (bf16[512,12,64]{2,0,1:T(8,128)(2,1)S(1)}, bf16[512,12,64]{2,0,1:T(8,128)(2,1)}, u32[]{:S(2)}) copy-start(bf16[512,12,64]{2,0,1:T(8,128)(2,1)} %copy-done.7) | copy-start | bytes 2359300
  546.8 5.9 copy-start.16
  546.8 14.1 %slice-start = ((s8[12582912]{0:T(1024)(128)(4,1)}), s8[4194304]{0:T(1024)(128)(4,1)S(1)}, s32[]{:S(2)}) async-start(s8[12582912]{0:T(1024)(128)(4,1)} %bitcast.131), calls=%async_computation.12 | async-start | bytes 8388608
  552.7 8.1 %slice-start.1 = ((s8[12582912]{0:T(1024)(128)(4,1)}), s8[4194304]{0:T(1024)(128)(4,1)S(1)}, s32[]{:S(2)}) async-start(s8[12582912]{0:T(1024)(128)(4,1)} %bitcast.131), calls=%async_computation.13 | async-start | bytes 8388608
  552.7 8.2 %slice-start.2 = ((s8[12582912]{0:T(1024)(128)(4,1)}), s8[4194304]{0:T(1024)(128)(4,1)S(1)}, s32[]{:S(2)}) async-start(s8[12582912]{0:T(1024)(128)(4,1)} %bitcast.131), calls=%async_computation.14 | async-start | bytes 8388608
  560.9 13.1 %copy-start.25 = (f32[512,64]{0,1:T(8,128)S(1)}, f32[512,64]{0,1:T(8,128)}, u32[]{:S(2)}) copy-start(f32[512,64]{0,1:T(8,128)} %get-tuple-element.112) | copy-start | bytes 393220
  573.7 206.0 %reduce-scatter.5.cloned.1.call-start = ((), (), s32[]{:S(2)}) async-start(), calls=%async_computation.8 | async-start | bytes 11759616 | tf_op jit(solution)/shard_map/reduce_scatter | solution.py:1099
  576.8 9.3 %copy-start.22 = (bf16[512,12,128]{0,2,1:T(8,128)(2,1)}, bf16[512,12,128]{0,2,1:T(8,128)(2,1)S(1)}, u32[]{:S(2)}) copy-start(bf16[512,12,128]{0,2,1:T(8,128)(2,1)S(1)} %pad_maximum_fusion.2) | copy-start | bytes 4718596
  (26 other events, 67.1 us)
Sparse Core Ops, SparseCore 0:
  11.6 92.7 all-gather.4
  106.0 48.5 all-gather.6
  156.2 48.7 all-gather.8
  206.4 48.7 all-gather.10
  433.4 45.5 reduce-scatter.6
  532.3 45.9 reduce-scatter.8
  580.5 47.0 reduce-scatter.10
  633.7 145.9 reduce-scatter.4

commit v2 on v1

--- a/solution.py
+++ b/solution.py
@@ -312,6 +312,7 @@
 
 MESH = pl.DeviceIdType.MESH
 ANY = pl.BlockSpec(memory_space=pl.ANY)
+VMEM = pl.BlockSpec(memory_space=pltpu.VMEM)
 VMEM_BYTES = 62 * 2**20
 
 
@@ -322,6 +323,12 @@
 def nt_dot(left, right):
     return lax.dot_general(
         left, right, (((1,), (1,)), ((), ())), preferred_element_type=jnp.float32
+    )
+
+
+def tn_dot(left, right):
+    return lax.dot_general(
+        left, right, (((0,), (0,)), ((), ())), preferred_element_type=jnp.float32
     )
 
 
@@ -549,28 +556,35 @@
     )(own, gate_w, up_w)
 
 
-def add_rows(target, others, chunk=64):
-    def one(index, carry):
-        rows = pl.ds(pl.multiple_of(index * chunk, chunk), chunk)
-        total = target[rows, :].astype(jnp.float32)
-        for other in others:
-            total = total + other[rows, :].astype(jnp.float32)
-        target[rows, :] = total.astype(target.dtype)
-        return carry
-
-    lax.fori_loop(0, target.shape[0] // chunk, one, 0)
+def row_chunk(rows):
+    return 64 if rows % 64 == 0 else 16
+
+
+def add_rows(target, others):
+    parts, rows_all, _ = target.shape
+    chunk = row_chunk(rows_all)
+    for part in range(parts):
+
+        def one(index, carry):
+            rows = pl.ds(pl.multiple_of(index * chunk, chunk), chunk)
+            total = target[part, rows, :].astype(jnp.float32)
+            for other in others:
+                total = total + other[part, rows, :].astype(jnp.float32)
+            target[part, rows, :] = total.astype(target.dtype)
+            return carry
+
+        lax.fori_loop(0, rows_all // chunk, one, 0)
 
 
 class Scatter:
-    def __init__(self, part, side, relay, final, send, side_sem, relay_sem, final_sem):
-        self.part, self.side, self.relay, self.final = part, side, relay, final
-        self.send, self.side_sem = send, side_sem
-        self.relay_sem, self.final_sem = relay_sem, final_sem
+    def __init__(self, theirs, scratch):
+        self.theirs = theirs
+        self.mine, self.side, self.relay, self.final = scratch[:4]
+        self.send, self.side_sem, self.relay_sem, self.final_sem = scratch[4:]
         self.me, self.sib, self.xn, self.yn = plane_peers()
-        self.diag = self.xn + self.yn - self.me
-
-    def begin(self):
-        plane_barrier((self.sib, self.xn, self.yn))
+
+    def peers(self):
+        return self.sib, self.xn, self.yn
 
     def place(self, step):
         quad = lax.div(step, 4)
@@ -589,7 +603,7 @@
     def side_copy(self, step):
         slot, half, _, place = self.place(step)
         return remote(
-            self.part.at[slot, half],
+            self.theirs(place, slot, half),
             self.side.at[place, half],
             self.send.at[step],
             self.side_sem.at[place, half],
@@ -607,7 +621,7 @@
 
     def relay_copy(self, step, way):
         return remote(
-            self.part.at[self.diag, way],
+            self.mine.at[3, way],
             self.relay.at[way],
             self.send.at[step],
             self.relay_sem.at[way],
@@ -616,7 +630,7 @@
 
     def final_copy(self, step, way, half):
         return remote(
-            self.part.at[(self.xn, self.yn)[way], half],
+            self.mine.at[1 + way, half],
             self.final.at[way, half],
             self.send.at[step],
             self.final_sem.at[way, half],
@@ -624,9 +638,7 @@
         )
 
     def depart(self, step):
-        slot, half, other, place = self.place(step)
-
-        @pl.when(other == 1)
+        @pl.when(self.place(step)[2] == 1)
         def _():
             self.side_copy(step).start()
 
@@ -635,66 +647,71 @@
             @pl.when(step == 2 + way)
             def _():
                 self.side_wait(3, way)
-                add_rows(self.part.at[self.diag, way], (self.side.at[3, way],))
+                add_rows(self.mine.at[3, way], (self.side.at[3, way],))
                 self.relay_copy(2 + way, way).start()
-
-            peer = (self.xn, self.yn)[way]
 
             @pl.when(step == 6 + way)
             def _():
                 self.side_wait(1 + way, way)
-                add_rows(self.part.at[peer, way], (self.side.at[1 + way, way],))
+                add_rows(self.mine.at[1 + way, way], (self.side.at[1 + way, way],))
                 self.final_copy(6 + way, way, way).start()
 
-            @pl.when(step == 15)
-            def _():
-                self.side_wait(1 + way, 1 - way)
-                self.relay_copy(3 - way, 1 - way).wait_recv()
-                add_rows(
-                    self.part.at[peer, 1 - way], (self.side.at[1 + way, 1 - way], self.relay.at[1 - way])
-                )
-                self.final_copy(10 + way, way, 1 - way).start()
-
-    def finish(self, out):
-        half_rows = out.shape[1]
-        chunk = 64
+    def forward(self):
+        for way in (0, 1):
+            self.side_wait(1 + way, 1 - way)
+            self.relay_copy(3 - way, 1 - way).wait_recv()
+            add_rows(
+                self.mine.at[1 + way, 1 - way],
+                (self.side.at[1 + way, 1 - way], self.relay.at[1 - way]),
+            )
+            self.final_copy(10 + way, way, 1 - way).start()
+
+    def finish(self, write):
+        parts, rows_all = self.mine.shape[2:4]
+        chunk = row_chunk(rows_all)
         for half in (0, 1):
             self.side_wait(0, half)
             self.final_copy(0, 0, half).wait_recv()
             self.final_copy(0, 1, half).wait_recv()
-
-            def one(index, carry):
-                rows = pl.ds(pl.multiple_of(index * chunk, chunk), chunk)
-                total = self.part[self.me, half, rows, :].astype(jnp.float32)
-                total = total + self.side[0, half, rows, :].astype(jnp.float32)
-                total = total + self.final[0, half, rows, :].astype(jnp.float32)
-                total = total + self.final[1, half, rows, :].astype(jnp.float32)
-                out[half, rows, :] = total
-                return carry
-
-            lax.fori_loop(0, half_rows // chunk, one, 0)
+            for part in range(parts):
+
+                def one(index, carry):
+                    rows = pl.ds(pl.multiple_of(index * chunk, chunk), chunk)
+                    total = self.mine[0, half, part, rows, :].astype(jnp.float32)
+                    total = total + self.side[0, half, part, rows, :].astype(jnp.float32)
+                    total = total + self.final[0, half, part, rows, :].astype(jnp.float32)
+                    total = total + self.final[1, half, part, rows, :].astype(jnp.float32)
+                    write(half, part, rows, total)
+                    return carry
+
+                lax.fori_loop(0, rows_all // chunk, one, 0)
+
+    def drain(self):
         for way in (0, 1):
             self.relay_copy(2 + way, way).wait_send()
             self.final_copy(6 + way, way, way).wait_send()
             self.final_copy(10 + way, way, 1 - way).wait_send()
 
-        def drain(step, carry):
+        def one(step, carry):
             @pl.when(self.place(step)[2] == 1)
             def _():
                 self.side_copy(step).wait_send()
 
             return carry
 
-        lax.fori_loop(0, 16, drain, 0)
-
-
-def scatter_scratch(half, columns):
+        lax.fori_loop(0, 16, one, 0)
+
+
+SCATTER_REFS = 8
+
+
+def scatter_scratch(parts, rows, columns):
     bf = jnp.bfloat16
     return [
-        pltpu.VMEM((8, 2, half, columns), bf),
-        pltpu.VMEM((4, 2, half, columns), bf),
-        pltpu.VMEM((2, half, columns), bf),
-        pltpu.VMEM((2, 2, half, columns), bf),
+        pltpu.VMEM((4, 2, parts, rows, columns), bf),
+        pltpu.VMEM((4, 2, parts, rows, columns), bf),
+        pltpu.VMEM((2, parts, rows, columns), bf),
+        pltpu.VMEM((2, 2, parts, rows, columns), bf),
         pltpu.SemaphoreType.DMA((16,)),
         pltpu.SemaphoreType.DMA((4, 2)),
         pltpu.SemaphoreType.DMA((2,)),
@@ -702,9 +719,10 @@
     ]
 
 
-def expert_out_kernel(gua_hbm, down_hbm, out, act, down_w, load, part, side, relay, final, send, side_sem, relay_sem, final_sem):
+def expert_out_kernel(gua_hbm, down_hbm, out, act, down_w, away, load, *scratch):
     hidden = down_w.shape[0]
-    scatter = Scatter(part, side, relay, final, send, side_sem, relay_sem, final_sem)
+    scatter = Scatter(lambda place, slot, half: away.at[place, half], scratch)
+    mine = scatter.mine
     down_load = pltpu.make_async_copy(down_hbm, down_w, load.at[16])
     down_load.start()
 
@@ -719,18 +737,33 @@
         return carry
 
     lax.fori_loop(0, 16, fetch, 0)
-    scatter.begin()
+    plane_barrier(scatter.peers())
     down_load.wait()
 
     def one(step, carry):
-        slot, half, _, _ = scatter.place(step)
+        slot, half, other, place = scatter.place(step)
         act_load(step).wait()
-        part[slot, half] = nn_dot(act[slot, half], down_w[...]).astype(jnp.bfloat16)
+        partial = nn_dot(act[slot, half], down_w[...]).astype(jnp.bfloat16)
+
+        @pl.when(other == 1)
+        def _():
+            away[place, half, 0] = partial
+
+        @pl.when(other == 0)
+        def _():
+            mine[place, half, 0] = partial
+
         scatter.depart(step)
         return carry
 
     lax.fori_loop(0, 16, one, 0)
-    scatter.finish(out)
+    scatter.forward()
+
+    def write(half, part, rows, total):
+        out[half, rows, :] = total
+
+    scatter.finish(write)
+    scatter.drain()
 
 
 def expert_out(gua, down_w):
@@ -740,13 +773,14 @@
         expert_out_kernel,
         out_shape=jax.ShapeDtypeStruct((2, half, width), jnp.float32),
         in_specs=[ANY] * 2,
-        out_specs=pl.BlockSpec(memory_space=pltpu.VMEM),
+        out_specs=VMEM,
         scratch_shapes=[
             pltpu.VMEM((8, 2, half, hidden), jnp.bfloat16),
             pltpu.VMEM((hidden, width), jnp.bfloat16),
+            pltpu.VMEM((4, 2, 1, half, width), jnp.bfloat16),
             pltpu.SemaphoreType.DMA((17,)),
         ]
-        + scatter_scratch(half, width),
+        + scatter_scratch(1, half, width),
         compiler_params=pltpu.CompilerParams(
             collective_id=2, has_side_effects=True, vmem_limit_bytes=VMEM_BYTES
         ),
@@ -869,42 +903,389 @@
     )(own, rows_all, gua, gate_w, up_w, down_w)
 
 
-def scatter_kernel(part_hbm, out, load, part, side, relay, final, send, side_sem, relay_sem, final_sem):
-    scatter = Scatter(part, side, relay, final, send, side_sem, relay_sem, final_sem)
+def expert_grads_kernel(part_hbm, rows_hbm, dgu_hbm, gua_hbm, grads_hbm, out, gate_out, up_out, down_out, rows, dgu, act, grads, gate_up_acc, down_acc, load, block_load, *scratch):
+    hidden, width = down_acc.shape
+    scatter = Scatter(lambda place, slot, half: part_hbm.at[slot, half], scratch)
 
     def part_load(step):
-        slot, half, _, _ = scatter.place(step)
-        return pltpu.make_async_copy(part_hbm.at[slot, half], part.at[slot, half], load.at[step])
+        slot, half, _, place = scatter.place(step)
+        return pltpu.make_async_copy(
+            part_hbm.at[slot, half], scatter.mine.at[place, half], load.at[step]
+        )
 
     def fetch(step, carry):
-        part_load(step).start()
+        @pl.when(scatter.place(step)[2] == 0)
+        def _():
+            part_load(step).start()
+
         return carry
 
+    def block_copies(block):
+        slot = lax.rem(block, 2)
+        return (
+            pltpu.make_async_copy(
+                rows_hbm.at[block, :, :, pl.ds(0, width)], rows.at[slot], block_load.at[slot, 0]
+            ),
+            pltpu.make_async_copy(dgu_hbm.at[block], dgu.at[slot], block_load.at[slot, 1]),
+            pltpu.make_async_copy(
+                gua_hbm.at[block, :, :, pl.ds(2 * hidden, hidden)], act.at[slot], block_load.at[slot, 2]
+            ),
+            pltpu.make_async_copy(grads_hbm.at[block], grads.at[slot], block_load.at[slot, 3]),
+        )
+
     lax.fori_loop(0, 16, fetch, 0)
-    scatter.begin()
+    plane_barrier(scatter.peers())
 
     def one(step, carry):
-        part_load(step).wait()
+        @pl.when(scatter.place(step)[2] == 0)
+        def _():
+            part_load(step).wait()
+
         scatter.depart(step)
         return carry
 
     lax.fori_loop(0, 16, one, 0)
-    scatter.finish(out)
-
-
-def plane_scatter(part, ident):
+    for copy in block_copies(0):
+        copy.start()
+    tile = 256
+
+    def accumulate(block, carry):
+        for copy in block_copies(block):
+            copy.wait()
+
+        @pl.when(block < 7)
+        def _():
+            for copy in block_copies(block + 1):
+                copy.start()
+
+        slot = lax.rem(block, 2)
+
+        def add_tile(acc, left, right, index):
+            cols = pl.ds(pl.multiple_of(index * tile, tile), tile)
+            total = tn_dot(
+                left[slot, :, :, cols].reshape(-1, tile), right[slot].reshape(-1, width)
+            )
+
+            @pl.when(block == 0)
+            def _():
+                acc[cols, :] = total
+
+            @pl.when(block > 0)
+            def _():
+                acc[cols, :] = acc[cols, :] + total
+
+        def gate_up_tile(index, carry):
+            add_tile(gate_up_acc, rows, dgu, index)
+            return carry
+
+        def down_tile(index, carry):
+            add_tile(down_acc, act, grads, index)
+            return carry
+
+        lax.fori_loop(0, width // tile, gate_up_tile, 0)
+        lax.fori_loop(0, hidden // tile, down_tile, 0)
+        return carry
+
+    def blocks(index, carry):
+        @pl.when(index == 3)
+        def _():
+            scatter.forward()
+
+        return accumulate(index, carry)
+
+    lax.fori_loop(0, 8, blocks, 0)
+
+    def round_tile(index, carry):
+        cols = pl.ds(pl.multiple_of(index * 64, 64), 64)
+        gate_out[cols, :] = gate_up_acc[cols, :hidden].astype(jnp.bfloat16)
+        up_out[cols, :] = gate_up_acc[cols, hidden:].astype(jnp.bfloat16)
+        return carry
+
+    lax.fori_loop(0, width // 64, round_tile, 0)
+
+    def round_down(index, carry):
+        cols = pl.ds(pl.multiple_of(index * 64, 64), 64)
+        down_out[cols, :] = down_acc[cols, :].astype(jnp.bfloat16)
+        return carry
+
+    lax.fori_loop(0, hidden // 64, round_down, 0)
+
+    def write(half, part, rows, total):
+        out[half, rows, :] = total
+
+    scatter.finish(write)
+    scatter.drain()
+
+
+def expert_grads(part, rows_all, dgu, gua, grads_all):
     _, _, half, columns = part.shape
+    width = grads_all.shape[3]
+    hidden = dgu.shape[3] // 2
+    bf = jnp.bfloat16
     return pl.pallas_call(
-        scatter_kernel,
-        out_shape=jax.ShapeDtypeStruct((2, half, columns), jnp.float32),
+        expert_grads_kernel,
+        out_shape=(
+            jax.ShapeDtypeStruct((2, half, columns), jnp.float32),
+            jax.ShapeDtypeStruct((width, hidden), bf),
+            jax.ShapeDtypeStruct((width, hidden), bf),
+            jax.ShapeDtypeStruct((hidden, width), bf),
+        ),
+        in_specs=[ANY] * 5,
+        out_specs=(VMEM,) * 4,
+        scratch_shapes=[
+            pltpu.VMEM((2, 2, half, width), bf),
+            pltpu.VMEM((2, 2, half, 2 * hidden), bf),
+            pltpu.VMEM((2, 2, half, hidden), bf),
+            pltpu.VMEM((2, 2, half, width), bf),
+            pltpu.VMEM((width, 2 * hidden), jnp.float32),
+            pltpu.VMEM((hidden, width), jnp.float32),
+            pltpu.SemaphoreType.DMA((16,)),
+            pltpu.SemaphoreType.DMA((2, 4)),
+        ]
+        + scatter_scratch(1, half, columns),
+        compiler_params=pltpu.CompilerParams(
+            collective_id=4, has_side_effects=True, vmem_limit_bytes=VMEM_BYTES
+        ),
+        name="expert_grads",
+    )(part.reshape(8, 2, 1, half, columns), rows_all, dgu, gua, grads_all)
+
+
+def line_peers():
+    line = lax.axis_index("dp")
+    return (
+        line,
+        line + 1 - 2 * lax.rem(line, 2),
+        line + 2 - 4 * lax.div(line, 2),
+        3 - line,
+    )
+
+
+def line_remote(src, dst, send_sem, recv_sem, peer):
+    return pltpu.make_async_remote_copy(
+        src_ref=src,
+        dst_ref=dst,
+        send_sem=send_sem,
+        recv_sem=recv_sem,
+        device_id={"dp": peer},
+        device_id_type=MESH,
+    )
+
+
+def full_barrier(plane, line):
+    barrier = pltpu.get_barrier_semaphore()
+    for peer in plane:
+        pl.semaphore_signal(barrier, inc=1, device_id={"exp": peer}, device_id_type=MESH)
+    for peer in line:
+        pl.semaphore_signal(barrier, inc=1, device_id={"dp": peer}, device_id_type=MESH)
+    pl.semaphore_wait(barrier, len(plane) + len(line))
+
+
+def dense_gather_kernel(own, everything, stage, send, recv, local):
+    me, sib, xn, yn = plane_peers()
+    diag = xn + yn - me
+    line = line_peers()
+    into = pltpu.make_async_copy(own, stage, local.at[0])
+    into.start()
+    full_barrier((sib, xn, yn), line[1:])
+    started = []
+
+    def put(src, slot, turn, peer):
+        copy = remote(
+            src, everything.at[line[turn], slot], send.at[len(started)], recv.at[line[turn], slot], peer
+        )
+        copy.start()
+        started.append(copy)
+
+    def pass_on(slot, turn, peer):
+        put(everything.at[line[turn], slot], slot, turn, peer)
+
+    def wait(slot, turn):
+        ref = everything.at[line[turn], slot]
+        remote(ref, ref, send.at[0], recv.at[line[turn], slot], sib).wait_recv()
+
+    put(own, me, 0, xn)
+    put(own, me, 0, yn)
+    for turn in (1, 2, 3):
+        copy = line_remote(
+            own, everything.at[line[0], me], send.at[len(started)], recv.at[line[0], me], line[turn]
+        )
+        copy.start()
+        started.append(copy)
+    put(own, me, 0, sib)
+    into.wait()
+    out = pltpu.make_async_copy(stage, everything.at[line[0], me], local.at[1])
+    out.start()
+    for turn in (0, 1, 2, 3):
+        if turn > 0:
+            wait(me, turn)
+            for peer in (xn, yn, sib):
+                pass_on(me, turn, peer)
+        wait(xn, turn)
+        if turn % 2 == 0:
+            pass_on(xn, turn, yn)
+        pass_on(xn, turn, sib)
+        wait(yn, turn)
+        if turn % 2 == 1:
+            pass_on(yn, turn, xn)
+        pass_on(yn, turn, sib)
+        if turn > 0:
+            wait(diag, turn - 1)
+            pass_on(diag, turn - 1, sib)
+    wait(diag, 3)
+    pass_on(diag, 3, sib)
+    for turn in (0, 1, 2, 3):
+        for slot in (sib, xn + sib - me, yn + sib - me, diag + sib - me):
+            wait(slot, turn)
+    out.wait()
+    for copy in started:
+        copy.wait_send()
+
+
+def dense_gather(own):
+    rows, columns = own.shape
+    return pl.pallas_call(
+        dense_gather_kernel,
+        out_shape=jax.ShapeDtypeStruct((4, 8, rows, columns), own.dtype),
         in_specs=[ANY],
-        out_specs=pl.BlockSpec(memory_space=pltpu.VMEM),
-        scratch_shapes=[pltpu.SemaphoreType.DMA((16,))] + scatter_scratch(half, columns),
+        out_specs=ANY,
+        scratch_shapes=[
+            pltpu.VMEM((rows, columns), own.dtype),
+            pltpu.SemaphoreType.DMA((32,)),
+            pltpu.SemaphoreType.DMA((4, 8)),
+            pltpu.SemaphoreType.DMA((2,)),
+        ],
         compiler_params=pltpu.CompilerParams(
-            collective_id=ident, has_side_effects=True, vmem_limit_bytes=VMEM_BYTES
+            collective_id=5, has_side_effects=True, vmem_limit_bytes=48 * 2**20
         ),
-        name="plane_scatter",
-    )(part)
+        name="dense_gather",
+    )(own).reshape(32 * rows, columns)
+
+
+class LineScatter:
+    def __init__(self, scratch):
+        self.sums, self.other, self.send, self.recv = scratch
+        self.line = line_peers()
+
+    def copy(self, turn):
+        target = self.line[turn]
+        return line_remote(
+            self.sums.at[target],
+            self.other.at[turn - 1],
+            self.send.at[turn - 1],
+            self.recv.at[turn - 1],
+            target,
+        )
+
+    def write(self, half, part, rows, total):
+        self.sums[2 * half + part, rows, :] = total.astype(self.sums.dtype)
+
+    def begin(self):
+        for turn in (1, 2, 3):
+            self.copy(turn).start()
+
+    def finish(self, out, first):
+        rows_all, columns = out.shape[0], self.sums.shape[2]
+        for turn in (1, 2, 3):
+            self.copy(turn).wait_recv()
+
+        def one(index, carry):
+            rows = pl.ds(pl.multiple_of(index * 16, 16), 16)
+            total = self.sums[self.line[0], rows, :].astype(jnp.float32)
+            for turn in (0, 1, 2):
+                total = total + self.other[turn, rows, :].astype(jnp.float32)
+            out[rows, pl.ds(first, columns)] = total
+            return carry
+
+        lax.fori_loop(0, rows_all // 16, one, 0)
+        for turn in (1, 2, 3):
+            self.copy(turn).wait_send()
+
+
+LINE_REFS = 4
+
+
+def line_scratch(rows, columns):
+    bf = jnp.bfloat16
+    return [
+        pltpu.VMEM((4, rows, columns), bf),
+        pltpu.VMEM((3, rows, columns), bf),
+        pltpu.SemaphoreType.DMA((3,)),
+        pltpu.SemaphoreType.DMA((3,)),
+    ]
+
+
+def dense_scatter_kernel(groups, *refs):
+    parts, out, refs = refs[:groups], refs[groups], refs[groups + 1 :]
+    step_refs = 1 + SCATTER_REFS + LINE_REFS
+    loads, planes, lines = [], [], []
+    for index, part in enumerate(parts):
+        some = refs[index * step_refs : (index + 1) * step_refs]
+        plane = Scatter(
+            lambda place, slot, half, part=part: part.at[half, :, slot], some[1 : 1 + SCATTER_REFS]
+        )
+
+        def load(step, part=part, plane=plane, sem=some[0]):
+            slot, half, _, place = plane.place(step)
+            return pltpu.make_async_copy(
+                part.at[half, :, slot], plane.mine.at[place, half], sem.at[step]
+            )
+
+        loads.append(load)
+        planes.append(plane)
+        lines.append(LineScatter(some[1 + SCATTER_REFS :]))
+
+    for plane, load in zip(planes, loads):
+
+        def fetch(step, carry, plane=plane, load=load):
+            @pl.when(plane.place(step)[2] == 0)
+            def _():
+                load(step).start()
+
+            return carry
+
+        lax.fori_loop(0, 16, fetch, 0)
+    full_barrier(planes[0].peers(), lines[0].line[1:])
+    for plane, load in zip(planes, loads):
+
+        def one(step, carry, plane=plane, load=load):
+            @pl.when(plane.place(step)[2] == 0)
+            def _():
+                load(step).wait()
+
+            plane.depart(step)
+            return carry
+
+        lax.fori_loop(0, 16, one, 0)
+    for plane in planes:
+        plane.forward()
+    for plane, line in zip(planes, lines):
+        plane.finish(line.write)
+        line.begin()
+    first = 0
+    for plane, line in zip(planes, lines):
+        line.finish(out, first)
+        first += line.sums.shape[2]
+        plane.drain()
+
+
+def dense_scatter(parts):
+    rows = parts[0].shape[0] // 32
+    scratch = []
+    for part in parts:
+        scratch += [pltpu.SemaphoreType.DMA((16,))]
+        scratch += scatter_scratch(2, rows, part.shape[1]) + line_scratch(rows, part.shape[1])
+    columns = sum(part.shape[1] for part in parts)
+    return pl.pallas_call(
+        functools.partial(dense_scatter_kernel, len(parts)),
+        out_shape=jax.ShapeDtypeStruct((rows, columns), jnp.float32),
+        in_specs=[ANY] * len(parts),
+        out_specs=VMEM,
+        scratch_shapes=scratch,
+        compiler_params=pltpu.CompilerParams(
+            collective_id=6, has_side_effects=True, vmem_limit_bytes=VMEM_BYTES
+        ),
+        name="dense_scatter",
+    )(*(part.reshape(2, 2, 8, rows, part.shape[1]) for part in parts))
 
 
 def body_plane(
@@ -948,7 +1329,7 @@
         ],
         axis=1,
     )
-    dense_w = lax.all_gather(dense_own, ("dp", "exp"), axis=0, tiled=True)
+    dense_w = dense_gather(dense_own)
     gate_w = lax.all_gather(w_gate, "dp", axis=1, tiled=True)[0]
     up_w = lax.all_gather(w_up, "dp", axis=1, tiled=True)[0]
     down_w = lax.all_gather(w_down, "dp", axis=1, tiled=True)[0]
@@ -1008,22 +1389,11 @@
     grads_all, dgu, part = expert_back(
         grad_out.astype(bf).reshape(2, half, width), rows_all, gua, gate_w, up_w, down_w
     )
-    back = plane_scatter(part, 4).reshape(num_rows, width + 128)
-    hidden = gate_w.shape[1]
-    flat_rows = rows_all.reshape(-1, width + 128)[:, :width]
-    flat_grads = grads_all.reshape(-1, width)
-    grad_gate_up = jnp.einsum(
-        "rd,rf->df", flat_rows, dgu.reshape(-1, 2 * hidden), preferred_element_type=jnp.float32
-    ).astype(bf)
-    grad_down_w = jnp.einsum(
-        "rf,rd->fd",
-        gua.reshape(-1, 3 * hidden)[:, 2 * hidden :],
-        flat_grads,
-        preferred_element_type=jnp.float32,
-    ).astype(bf)
+    back, *expert_parts = expert_grads(part, rows_all, dgu, gua, grads_all)
+    back = back.reshape(num_rows, width + 128)
     expert_sums = tuple(
         lax.psum_scatter(grad[None], "dp", scatter_dimension=1, tiled=True).astype(jnp.float32)
-        for grad in (grad_gate_up[:, :hidden], grad_gate_up[:, hidden:], grad_down_w)
+        for grad in expert_parts
     )
     grad_hidden_two = back[:, :width]
     grad_comb = jnp.sum(
@@ -1085,10 +1455,9 @@
     grad_in = grad_mid + inv_one * (
         grad_norm_one - normed_one * jnp.mean(grad_norm_one * normed_one, axis=-1, keepdims=True)
     )
-    dense_grad = jnp.concatenate(
+    qkv_part = jnp.concatenate(
         [
             grad_qkv_w.astype(bf),
-            grad_out_w.astype(bf),
             jnp.pad(
                 jnp.concatenate([grad_gain_one[:, None], grad_gain_two[:, None], grad_router], axis=1),
                 ((0, 0), (0, pad_cols)),
@@ -1096,19 +1465,18 @@
         ],
         axis=1,
     )
-    dense_sum = lax.psum_scatter(
-        dense_grad, ("dp", "exp"), scatter_dimension=0, tiled=True
-    ).astype(jnp.float32)
+    dense_sum = dense_scatter((grad_out_w.astype(bf), qkv_part))
+    out_sum, qkv_sum = dense_sum[:, :width], dense_sum[:, width:]
     return (
         layer_out,
         grad_in,
-        dense_sum[:, dense_cols],
-        dense_sum[:, :q_cols],
-        dense_sum[:, q_cols : q_cols + k_cols],
-        dense_sum[:, q_cols + k_cols : qkv_cols],
-        dense_sum[:, qkv_cols:dense_cols],
-        dense_sum[:, dense_cols + 1],
-        dense_sum[:, dense_cols + 2 : dense_cols + 2 + num_experts],
+        qkv_sum[:, qkv_cols],
+        qkv_sum[:, :q_cols],
+        qkv_sum[:, q_cols : q_cols + k_cols],
+        qkv_sum[:, q_cols + k_cols : qkv_cols],
+        out_sum,
+        qkv_sum[:, qkv_cols + 1],
+        qkv_sum[:, qkv_cols + 2 : qkv_cols + 2 + num_experts],
         *expert_sums,
     )
 
@@ -1145,5 +1513,5 @@
         P("exp", "dp", None),
         P("exp", "dp", None),
     )
-    body = body_plane if mesh.shape["exp"] == 8 else body_general
+    body = body_plane if (mesh.shape["dp"], mesh.shape["exp"]) == (4, 8) else body_general
     return jax.shard_map(body, mesh=mesh, in_specs=in_specs, out_specs=out_specs, check_vma=False)

time: 799 us -> 636 us (0.80)
  waiting for transfers between devices: 300 us -> 2.14 us
  Pallas kernels: 259 us -> 433 us
  matrix products: 121 us -> 84.6 us
  other arithmetic: 56.8 us -> 48.1 us
    pallas_call x1 -> x3, Pallas kernels: 64.3 us -> 238 us  [the longest x1 86 us: dense_gather(): pl.pallas_call(dense_gather_kernel, out_shape=jax.ShapeDtypeStruct((4, 8,...]
    reduce_scatter x1 -> x0, waiting for transfers between devices: 150 us -> none  [body_plane(): lax.psum_scatter(dense_grad, ('dp', 'exp'), scatter_dimension=0, tiled=True)]
    all_gather x1 -> x0, waiting for transfers between devices: 85.8 us -> none  [body_plane(): dense_w = lax.all_gather(dense_own, ('dp', 'exp'), axis=0, tiled=True)]
    all_gather x1, waiting for transfers between devices: 48.5 us -> 0.01 us  [body_plane(): up_w = lax.all_gather(w_up, 'dp', axis=1, tiled=True)[0]]
    dot_general x2 -> x0, matrix products: 38.9 us -> none  [the longest x1 26.1 us: body_plane(): jnp.einsum('rd,rf->df', flat_rows, dgu.reshape(-1, 2 * hidden), preferred...]
    reduce_scatter x3, waiting for transfers between devices: 13.9 us -> 0.01 us  [body_plane(): lax.psum_scatter(grad[None], 'dp', scatter_dimension=1, tiled=True)]
  transfers between devices with their start and end apart: 8 -> 6, of which waited for: 4 -> 0; matrix products, arithmetic and copies ran while one was open for 21% -> 25% of each run, Pallas kernels for 16% -> 37%
where the time goes in v2:
time: 636 us; the launch traced here: 628 us
  Pallas kernels  433 us (68%)
  matrix products  84.6 us (13%)
  other arithmetic  48.1 us (8%)
  local copies, waits for them, and re-layouts  43.9 us (7%)
  between operations  16 us (3%)
    pallas_call x1, Pallas kernels, dense_gather(): pl.pallas_call(dense_gather_kernel, out_shape=jax.ShapeDtypeStruct((4, 8,...  86 us
    pallas_call x1, Pallas kernels, dense_scatter(): pl.pallas_call(functools.partial(dense_scatter_kernel, len(parts)), out_s...  79.4 us
    pallas_call x1, Pallas kernels, expert_grads(): pl.pallas_call(expert_grads_kernel, out_shape=(jax.ShapeDtypeStruct((2, h...  72.7 us
    pallas_call x1, Pallas kernels, expert_back(): pl.pallas_call(expert_back_kernel, out_shape=(jax.ShapeDtypeStruct((8, 2,...  67.1 us
    pallas_call x1, Pallas kernels, expert_in(): pl.pallas_call(expert_in_kernel, out_shape=(jax.ShapeDtypeStruct((8, 2, h...  65.4 us
    pallas_call x1, Pallas kernels, expert_out(): pl.pallas_call(expert_out_kernel, out_shape=jax.ShapeDtypeStruct((2, half...  62.3 us
  transfers between devices with their start and end apart: 6, of which 0 were waited for; matrix products, arithmetic and copies ran while one was open for 25% of the time, Pallas kernels for 37%

profile of v2, /device:TPU:0, one launch (start us, length us, event | category | flops | bytes accessed | tf_op | source)
XLA Modules:
  0.0 627.8 jit_solution(9505175952066349121)
XLA Ops:
  12.9 86.0 %dense_gather.1 = bf16[4,8,48,3712]{3,2,1,0:T(8,128)(2,1)} custom-call(bf16[48,3712]{1,0:T(8,128)(2,1)S(1)} %concatenate.37.own), custom_call_target="tpu_custom_call" | custom-call | tf_op jit(solution)/shard_map/dense_gather/pallas_call | solution.py:1146
  98.9 2.2 fusion.63
  101.7 5.6 fusion.9
  110.2 2.2 reshape.320
  112.5 2.7 fusion.66
  118.3 2.4 copy.149
  120.7 3.3 subtract_convert_fusion.1
  124.9 2.3 copy.151
  129.2 3.4 fusion.6
  132.7 2.6 exponential_reduce_fusion
  137.3 9.2 %convolution_convert_fusion.3 = bf16[2,128,6,512]{3,1,2,0:T(8,128)(2,1)} fusion(bf16[512,2,128,1]{2,1,0,3:T(2,128)(2,1)S(1)} %bitcast.133, f32[2,512,512,6]{2,1,3,0:T(8,128)} %copy-done, f32[2,6,512]{2,1,0:T(8,128)S(1)} %log_add_fusion, pred[512,512]{0,1:T(8,128)(4,1)S(1)} %fusion.38), kind=kOutput, calls=%fused_computation.53 | convolution fusion | flops 818675712 | bytes 14704640 | tf_op jit(solution)/shard_map/kgqp,pkd->qkgd/dot_general | solution.py:1359
  146.8 5.9 multiply_reduce_fusion.2
  159.8 65.4 %expert_in.1 = (bf16[8,2,256,1664]{3,2,1,0:T(8,128)(2,1)}, bf16[8,2,256,2304]{3,2,1,0:T(8,128)(2,1)}) custom-call(bf16[2,256,1664]{2,1,0:T(8,128)(2,1)} %bitcast.121, bf16[1536,768]{1,0:T(8,128)(2,1)} %bitcast.117, bf16[1536,768]{1,0:T(8,128)(2,1)} %bitcast.119), custom_call_target="tpu_custom_call" | custom-call | tf_op jit(solution)/shard_map/expert_in/pallas_call | solution.py:533
  225.2 62.3 %expert_out.1 = f32[2,256,1536]{2,1,0:T(8,128)} custom-call(bf16[8,2,256,2304]{3,2,1,0:T(8,128)(2,1)} %get-tuple-element.21.gua_hbm, bf16[768,1536]{1,0:T(8,128)(2,1)} %bitcast.115), custom_call_target="tpu_custom_call" | custom-call | tf_op jit(solution)/shard_map/expert_out/pallas_call | solution.py:772
  287.5 4.6 fusion.32
  292.1 67.1 %expert_back.1 = (bf16[8,2,256,1536]{3,2,1,0:T(8,128)(2,1)}, bf16[8,2,256,1536]{3,2,1,0:T(8,128)(2,1)}, bf16[8,2,256,1664]{3,2,1,0:T(8,128)(2,1)}) custom-call(bf16[2,256,1536]{2,1,0:T(8,128)(2,1)} %bitcast.122, bf16[8,2,256,1664]{3,2,1,0:T(8,128)(2,1)} %get-tuple-element.22.rows_hbm, bf16[8,2,256,2304]{3,2,1,0:T(8,128)(2,1)} %get-tuple-element.21.gua_hbm, ...), custom_call_target="tpu_custom_call" | custom-call | tf_op jit(solution)/shard_map/expert_back/pallas_call | solution.py:877
  359.2 72.7 %expert_grads.1 = (f32[2,256,1664]{2,1,0:T(8,128)}, bf16[1536,768]{1,0:T(8,128)(2,1)}, bf16[1536,768]{1,0:T(8,128)(2,1)}, bf16[768,1536]{1,0:T(8,128)(2,1)}) custom-call(bf16[8,2,1,256,1664]{4,3,2,1,0:T(8,128)(2,1)} %bitcast.112, bf16[8,2,256,1664]{3,2,1,0:T(8,128)(2,1)} %get-tuple-element.22.rows_hbm, bf16[8,2,256,1536]{3,2,1,0:T(8,128)(2,1)} %get-tuple-element.24.dgu_hbm, ...), custom_call_target="tpu_custom_call" | custom-call | tf_op jit(solution)/shard_map/expert_grads/pallas_call | solution.py:1025
  440.9 5.2 multiply_reduce_fusion
  446.2 2.9 multiply_add_fusion
  450.8 5.0 fusion.29
  456.7 11.0 %fusion.1 = (f32[2,6,512]{2,1,0:T(8,128)S(1)}, f32[2,512,512,6]{2,1,3,0:T(8,128)}) fusion(f32[2,512,512,6]{2,1,3,0:T(8,128)} %copy-done, f32[2,6,512]{2,1,0:T(8,128)} %copy-done.31, pred[512,512]{0,1:T(8,128)(4,1)S(1)} %fusion.38, bf16[512,2,6,128]{0,3,2,1:T(8,128)(2,1)S(1)} %bitcast.123, bf16[512,2,128,1]{2,1,0,3:T(2,128)(2,1)} %bitcast.134), kind=kOutput, calls=%fused_computation.4 | convolution fusion | flops 821028864 | bytes 27312128 | tf_op jit(solution)/shard_map/qkgd,pkd->kgqp/dot_general | solution.py:1430
  469.5 7.2 %fusion.3 = bf16[2,6,512,512]{2,3,1,0:T(8,128)(2,1)S(1)} fusion(f32[2,512,512,6]{2,1,3,0:T(8,128)} %get-tuple-element.129, f32[2,512,512,6]{2,1,3,0:T(8,128)S(1)} %bitcast.99, f32[2,6,512]{2,1,0:T(8,128)S(1)} %get-tuple-element.128, f32[2,6,512]{2,1,0:T(8,128)S(1)} %copy-done.32, pred[512,512]{0,1:T(8,128)(4,1)S(1)} %fusion.38), kind=kLoop, calls=%fused_computation.6 | loop fusion | flops 18874368 | bytes 31768576 | tf_op jit(solution)/shard_map/convert_element_type | solution.py:1434
  480.7 4.0 convolution_multiply_fusion
  486.8 8.6 %fusion.36 = bf16[2,128,512]{2,1,0:T(8,128)(2,1)} fusion(bf16[512,2,6,128]{0,3,2,1:T(8,128)(2,1)S(1)} %bitcast.124, f32[2,512,512,6]{2,1,3,0:T(8,128)} %copy-done, f32[2,6,512]{2,1,0:T(8,128)S(1)} %copy-done.33, pred[512,512]{0,1:T(8,128)(4,1)S(1)} %fusion.38), kind=kOutput, calls=%fused_computation.64 | convolution fusion | flops 818020352 | bytes 14704640 | tf_op jit(solution)/shard_map/kgqp,qkgd->pkd/dot_general | solution.py:1427
  495.5 10.4 %fusion.25 = (bf16[1536]{0:T(1024)(128)(2,1)S(1)}, f32[512]{0:T(512)}, f32[512,1536]{1,0:T(8,128)}) fusion(bf16[512,1536]{1,0:T(8,128)(2,1)} %param.15, f32[512]{0:T(512)S(1)} %copy-done.55, f32[1536]{0:T(1024)S(1)} %copy-done.46, bf16[1536,3712]{1,0:T(8,128)(2,1)} %bitcast.107, bf16[512,256]{0,1:T(8,128)(2,1)} %bitcast.141, ...), kind=kOutput, calls=%fused_computation.38 | convolution fusion | flops 3233019904 | bytes 13120512 | tf_op jit(solution)/shard_map/rh,dh->rd/dot_general | solution.py:1452
  508.4 6.2 convolution_convert_fusion.1
  514.7 5.4 convolution_convert_fusion
  520.0 3.2 fusion.5
  523.2 79.4 %dense_scatter.1 = f32[48,3712]{1,0:T(8,128)} custom-call(bf16[2,2,8,48,1536]{4,3,2,1,0:T(8,128)(2,1)} %bitcast.125, bf16[2,2,8,48,2176]{4,3,2,1,0:T(8,128)(2,1)} %bitcast.100), custom_call_target="tpu_custom_call" | custom-call | tf_op jit(solution)/shard_map/dense_scatter/pallas_call | solution.py:1278
  609.0 5.3 fusion.24
  616.4 2.2 convert_element_type.141
  618.6 2.2 convert_element_type.142
  (213 shorter events, 53.7 us)
Async XLA Ops:
  7.2 152.6 %all-gather.4.cloned.1.call-start = ((), (), s32[]{:S(2)}) async-start(), calls=%async_computation.3 | async-start | bytes 2949120 | tf_op jit(solution)/shard_map/all_gather | solution.py:1333
  7.9 151.9 %all-gather.6.cloned.1.call-start = ((), (), s32[]{:S(2)}) async-start(), calls=%async_computation.4 | async-start | bytes 2949120 | tf_op jit(solution)/shard_map/all_gather | solution.py:1334
  8.7 216.6 %all-gather.8.cloned.1.call-start = ((), (), s32[]{:S(2)}) async-start(), calls=%async_computation.5 | async-start | bytes 2949120 | tf_op jit(solution)/shard_map/all_gather | solution.py:1335
  9.4 604.8 %reduce-scatter.4.cloned.1.call-start = ((), (), s32[]{:S(2)}) async-start(), calls=%async_computation.6 | async-start | bytes 2949120 | tf_op jit(solution)/shard_map/reduce_scatter | solution.py:1395
  12.9 88.4 %copy-start.16 = (bf16[512,1536]{1,0:T(8,128)(2,1)S(1)}, bf16[512,1536]{1,0:T(8,128)(2,1)}, u32[]{:S(2)}) copy-start(bf16[512,1536]{1,0:T(8,128)(2,1)} %param.15) | copy-start | bytes 4718596
  110.2 8.1 %slice-start.3 = ((f32[512,2048]{1,0:T(8,128)}), f32[512,1536]{1,0:T(8,128)S(1)}, s32[]{:S(2)}) async-start(f32[512,2048]{1,0:T(8,128)} %copy-done.11), calls=%async_computation.12 | async-start | bytes 6291456 | tf_op jit(solution)/shard_map/slice | solution.py:1349
  124.8 7.8 %copy-start.7 = (bf16[512,12,64]{2,0,1:T(8,128)(2,1)}, bf16[512,12,64]{2,0,1:T(8,128)(2,1)S(1)}, u32[]{:S(2)}) copy-start(bf16[512,12,64]{2,0,1:T(8,128)(2,1)S(1)} %copy.150) | copy-start | bytes 2359300
  137.2 9.3 %copy-start.31 = (f32[2,6,512]{2,1,0:T(8,128)}, f32[2,6,512]{2,1,0:T(8,128)S(1)}, u32[]{:S(2)}) copy-start(f32[2,6,512]{2,1,0:T(8,128)S(1)} %log_add_fusion) | copy-start | bytes 73732
  137.3 9.2 %copy-start.28 = (bf16[512,2,128]{2,1,0:T(2,128)(2,1)}, bf16[512,2,128]{2,1,0:T(2,128)(2,1)S(1)}, u32[]{:S(2)}) copy-start(bf16[512,2,128]{2,1,0:T(2,128)(2,1)S(1)} %reshape.319) | copy-start | bytes 786436
  137.3 9.2 %copy-start.26 = (bf16[1536,1]{1,0:T(8,128)(2,1)S(1)}, bf16[1536,1]{1,0:T(8,128)(2,1)}, u32[]{:S(2)}) copy-start(bf16[1536,1]{1,0:T(8,128)(2,1)} %get-tuple-element.100) | copy-start | bytes 9220
  137.3 9.4 %copy-start.17 = (bf16[512,1536]{1,0:T(8,128)(2,1)S(1)}, bf16[512,1536]{1,0:T(8,128)(2,1)}, u32[]{:S(2)}) copy-start(bf16[512,1536]{1,0:T(8,128)(2,1)} %param.15) | copy-start | bytes 4718596
  158.5 129.1 %copy-start.57 = (pred[512]{0:T(512)(128)(4,1)}, pred[512]{0:T(512)(128)(4,1)S(1)}, u32[]{:S(2)}) copy-start(pred[512]{0:T(512)(128)(4,1)S(1)} %add_compare_fusion) | copy-start | bytes 1540
  225.2 62.3 %copy-start.14 = (bf16[512,1536]{1,0:T(8,128)(2,1)S(1)}, bf16[512,1536]{1,0:T(8,128)(2,1)}, u32[]{:S(2)}) copy-start(bf16[512,1536]{1,0:T(8,128)(2,1)} %param.16) | copy-start | bytes 4718596
  431.9 9.0 %copy-start.3 = (f32[512,1536]{1,0:T(8,128)S(1)}, f32[512,1536]{1,0:T(8,128)}, u32[]{:S(2)}) copy-start(f32[512,1536]{1,0:T(8,128)} %copy-done.2) | copy-start | bytes 9437188
  431.9 184.4 %reduce-scatter.6.cloned.1.call-start = ((), (), s32[]{:S(2)}) async-start(), calls=%async_computation.7 | async-start | bytes 2949120 | tf_op jit(solution)/shard_map/reduce_scatter | solution.py:1395
  456.6 162.0 %reduce-scatter.8.cloned.1.call-start = ((), (), s32[]{:S(2)}) async-start(), calls=%async_computation.8 | async-start | bytes 2949120 | tf_op jit(solution)/shard_map/reduce_scatter | solution.py:1395
  456.6 11.1 %slice-start = ((s8[12582912]{0:T(1024)(128)(4,1)}), s8[4194304]{0:T(1024)(128)(4,1)S(1)}, s32[]{:S(2)}) async-start(s8[12582912]{0:T(1024)(128)(4,1)} %bitcast.98), calls=%async_computation.9 | async-start | bytes 8388608
  456.7 11.1 %slice-start.1 = ((s8[12582912]{0:T(1024)(128)(4,1)}), s8[4194304]{0:T(1024)(128)(4,1)S(1)}, s32[]{:S(2)}) async-start(s8[12582912]{0:T(1024)(128)(4,1)} %bitcast.98), calls=%async_computation.10 | async-start | bytes 8388608
  456.7 12.8 %slice-start.2 = ((s8[12582912]{0:T(1024)(128)(4,1)}), s8[4194304]{0:T(1024)(128)(4,1)S(1)}, s32[]{:S(2)}) async-start(s8[12582912]{0:T(1024)(128)(4,1)} %bitcast.98), calls=%async_computation.11 | async-start | bytes 8388608
  456.7 12.8 %copy-start.32 = (f32[2,6,512]{2,1,0:T(8,128)S(1)}, f32[2,6,512]{2,1,0:T(8,128)}, u32[]{:S(2)}) copy-start(f32[2,6,512]{2,1,0:T(8,128)} %copy-done.31) | copy-start | bytes 73732
  469.5 7.2 %copy-start.8 = (bf16[512,12,64]{2,0,1:T(8,128)(2,1)S(1)}, bf16[512,12,64]{2,0,1:T(8,128)(2,1)}, u32[]{:S(2)}) copy-start(bf16[512,12,64]{2,0,1:T(8,128)(2,1)} %copy-done.7) | copy-start | bytes 2359300
  469.5 7.3 %copy-start.10 = (bf16[512,12,64]{2,0,1:T(8,128)(2,1)S(1)}, bf16[512,12,64]{2,0,1:T(8,128)(2,1)}, u32[]{:S(2)}) copy-start(bf16[512,12,64]{2,0,1:T(8,128)(2,1)} %copy-done.9) | copy-start | bytes 2359300
  486.8 8.6 %copy-start.46 = (f32[1536]{0:T(1024)S(1)}, f32[1536]{0:T(1024)}, u32[]{:S(2)}) copy-start(f32[1536]{0:T(1024)} %copy-done.45) | copy-start | bytes 18436
  486.8 8.6 %copy-start.55 = (f32[512]{0:T(512)S(1)}, f32[512]{0:T(512)}, u32[]{:S(2)}) copy-start(f32[512]{0:T(512)} %copy-done.54) | copy-start | bytes 6148
  495.4 10.4 %copy-start.53 = (bf16[1536]{0:T(1024)(128)(2,1)S(1)}, bf16[1536]{0:T(1024)(128)(2,1)}, u32[]{:S(2)}) copy-start(bf16[1536]{0:T(1024)(128)(2,1)} %get-tuple-element.90) | copy-start | bytes 9220
  495.4 10.4 %copy-start.6 = (bf16[512,1536]{1,0:T(8,128)(2,1)S(1)}, bf16[512,1536]{1,0:T(8,128)(2,1)}, u32[]{:S(2)}) copy-start(bf16[512,1536]{1,0:T(8,128)(2,1)} %copy-done.5) | copy-start | bytes 4718596
  495.4 10.4 %copy-start.35 = (f32[512,8]{0,1:T(8,128)S(1)}, f32[512,8]{0,1:T(8,128)}, u32[]{:S(2)}) copy-start(f32[512,8]{0,1:T(8,128)} %copy-done.34) | copy-start | bytes 49156
  495.5 10.4 %copy-start.52 = (f32[512]{0:T(512)S(1)}, f32[512]{0:T(512)}, u32[]{:S(2)}) copy-start(f32[512]{0:T(512)} %copy-done.51) | copy-start | bytes 6148
  495.5 12.9 %copy-start.13 = (f32[512,1536]{1,0:T(8,128)S(1)}, f32[512,1536]{1,0:T(8,128)}, u32[]{:S(2)}) copy-start(f32[512,1536]{1,0:T(8,128)} %copy-done.12) | copy-start | bytes 9437188
  508.4 6.3 %copy-start.18 = (bf16[512,1536]{1,0:T(8,128)(2,1)S(1)}, bf16[512,1536]{1,0:T(8,128)(2,1)}, u32[]{:S(2)}) copy-start(bf16[512,1536]{1,0:T(8,128)(2,1)} %param.15) | copy-start | bytes 4718596
  523.2 82.4 %copy-start.59 = (f32[512]{0:T(512)S(1)}, f32[512]{0:T(512)}, u32[]{:S(2)}) copy-start(f32[512]{0:T(512)} %get-tuple-element.93) | copy-start | bytes 6148
  523.2 85.7 %copy-start.19 = (bf16[512,1536]{1,0:T(8,128)(2,1)S(1)}, bf16[512,1536]{1,0:T(8,128)(2,1)}, u32[]{:S(2)}) copy-start(bf16[512,1536]{1,0:T(8,128)(2,1)} %param.15) | copy-start | bytes 4718596
  (39 other events, 150.2 us)
Sparse Core Ops, SparseCore 0:
  9.6 78.3 all-gather.3
  89.5 49.9 all-gather.5
  141.1 48.7 all-gather.7
  432.1 44.9 reduce-scatter.3
  479.2 47.0 reduce-scatter.5
  528.4 52.2 reduce-scatter.7

commit v3 on v2

--- a/solution.py
+++ b/solution.py
@@ -719,7 +719,7 @@
     ]
 
 
-def expert_out_kernel(gua_hbm, down_hbm, out, act, down_w, away, load, *scratch):
+def expert_out_kernel(gua_hbm, down_hbm, resid, targets, scales, layer, grad, grad_b, act, down_w, away, load, *scratch):
     hidden = down_w.shape[0]
     scatter = Scatter(lambda place, slot, half: away.at[place, half], scratch)
     mine = scatter.mine
@@ -760,20 +760,28 @@
     scatter.forward()
 
     def write(half, part, rows, total):
-        out[half, rows, :] = total
+        value = resid[half, rows, :] + total
+        layer[half, rows, :] = value.astype(layer.dtype)
+        error = (value - targets[half, rows, :].astype(jnp.float32)) * scales[half, rows, 0:1]
+        grad[half, rows, :] = error
+        grad_b[half, rows, :] = error.astype(grad_b.dtype)
 
     scatter.finish(write)
     scatter.drain()
 
 
-def expert_out(gua, down_w):
+def expert_out(gua, down_w, resid, targets, scales):
     half = gua.shape[2]
     hidden, width = down_w.shape
     return pl.pallas_call(
         expert_out_kernel,
-        out_shape=jax.ShapeDtypeStruct((2, half, width), jnp.float32),
-        in_specs=[ANY] * 2,
-        out_specs=VMEM,
+        out_shape=(
+            jax.ShapeDtypeStruct((2, half, width), jnp.bfloat16),
+            jax.ShapeDtypeStruct((2, half, width), jnp.float32),
+            jax.ShapeDtypeStruct((2, half, width), jnp.bfloat16),
+        ),
+        in_specs=[ANY] * 2 + [VMEM] * 3,
+        out_specs=(VMEM,) * 3,
         scratch_shapes=[
             pltpu.VMEM((8, 2, half, hidden), jnp.bfloat16),
             pltpu.VMEM((hidden, width), jnp.bfloat16),
@@ -785,7 +793,13 @@
             collective_id=2, has_side_effects=True, vmem_limit_bytes=VMEM_BYTES
         ),
         name="expert_out",
-    )(gua, down_w)
+    )(
+        gua,
+        down_w,
+        resid.reshape(2, half, width),
+        targets.reshape(2, half, width),
+        scales.reshape(2, half, 128),
+    )
 
 
 def expert_back_kernel(own, rows_hbm, gua_hbm, gate_hbm, up_hbm, down_hbm, grads_out, dgu_out, part_out, buf, gu, tails, part, gate_w, up_w, down_w, send, recv, load, load_gu, load_tail, store_a, store_b, store_c):
@@ -1183,8 +1197,8 @@
         for turn in (1, 2, 3):
             self.copy(turn).start()
 
-    def finish(self, out, first):
-        rows_all, columns = out.shape[0], self.sums.shape[2]
+    def finish(self, outs):
+        rows_all = outs[0].shape[0]
         for turn in (1, 2, 3):
             self.copy(turn).wait_recv()
 
@@ -1193,7 +1207,10 @@
             total = self.sums[self.line[0], rows, :].astype(jnp.float32)
             for turn in (0, 1, 2):
                 total = total + self.other[turn, rows, :].astype(jnp.float32)
-            out[rows, pl.ds(first, columns)] = total
+            first = 0
+            for out in outs:
+                out[rows, :] = total[:, first : first + out.shape[1]]
+                first += out.shape[1]
             return carry
 
         lax.fori_loop(0, rows_all // 16, one, 0)
@@ -1214,8 +1231,9 @@
     ]
 
 
-def dense_scatter_kernel(groups, *refs):
-    parts, out, refs = refs[:groups], refs[groups], refs[groups + 1 :]
+def dense_scatter_kernel(splits, *refs):
+    groups, count = len(splits), sum(len(split) for split in splits)
+    parts, outs, refs = refs[:groups], refs[groups : groups + count], refs[groups + count :]
     step_refs = 1 + SCATTER_REFS + LINE_REFS
     loads, planes, lines = [], [], []
     for index, part in enumerate(parts):
@@ -1261,31 +1279,352 @@
     for plane, line in zip(planes, lines):
         plane.finish(line.write)
         line.begin()
-    first = 0
-    for plane, line in zip(planes, lines):
-        line.finish(out, first)
-        first += line.sums.shape[2]
+    for plane, line, split in zip(planes, lines, splits):
+        line.finish(outs[: len(split)])
+        outs = outs[len(split) :]
         plane.drain()
 
 
-def dense_scatter(parts):
+def dense_scatter(parts, splits):
     rows = parts[0].shape[0] // 32
     scratch = []
     for part in parts:
         scratch += [pltpu.SemaphoreType.DMA((16,))]
         scratch += scatter_scratch(2, rows, part.shape[1]) + line_scratch(rows, part.shape[1])
-    columns = sum(part.shape[1] for part in parts)
+    shapes = [
+        jax.ShapeDtypeStruct((rows, columns), jnp.float32) for split in splits for columns in split
+    ]
     return pl.pallas_call(
-        functools.partial(dense_scatter_kernel, len(parts)),
-        out_shape=jax.ShapeDtypeStruct((rows, columns), jnp.float32),
+        functools.partial(dense_scatter_kernel, splits),
+        out_shape=shapes,
         in_specs=[ANY] * len(parts),
-        out_specs=VMEM,
+        out_specs=[VMEM] * len(shapes),
         scratch_shapes=scratch,
         compiler_params=pltpu.CompilerParams(
             collective_id=6, has_side_effects=True, vmem_limit_bytes=VMEM_BYTES
         ),
         name="dense_scatter",
     )(*(part.reshape(2, 2, 8, rows, part.shape[1]) for part in parts))
+
+
+def rope(values, cosine, sine):
+    return values * cosine + pltpu.roll(values, HD // 2, 1) * sine
+
+
+def gain_rows(misc, out):
+    for index in range(misc.shape[0] // 128):
+        rows = pl.ds(index * 128, 128)
+        out[:, rows] = jnp.transpose(misc[rows, :].astype(jnp.float32))
+
+
+def inverse_rms(values):
+    return lax.rsqrt(jnp.mean(values * values, axis=1, keepdims=True) + EPS)
+
+
+def row_loop(count, chunk, body):
+    def one(index, carry):
+        body(pl.ds(pl.multiple_of(index * chunk, chunk), chunk))
+        return carry
+
+    lax.fori_loop(0, count // chunk, one, 0)
+
+
+def tile_loop(count, tile, body):
+    row_loop(count, tile, body)
+
+
+ROW_CHUNK = 16
+TILE = 256
+
+
+def attend_kernel(q_heads, kv_heads, experts, tokens, dense_hbm, cosine, sine, bias, picked, rows_out, resid, heads, mixed, lse, prob, qkv_w, rest_w, gains, hidden, load):
+    num_rows, width = tokens.shape
+    group = q_heads // kv_heads
+    q_cols = q_heads * HD
+    loads = (
+        pltpu.make_async_copy(dense_hbm.at[:, pl.ds(0, qkv_w.shape[1])], qkv_w, load.at[0]),
+        pltpu.make_async_copy(
+            dense_hbm.at[:, pl.ds(qkv_w.shape[1], rest_w.shape[1])], rest_w, load.at[1]
+        ),
+    )
+    for copy in loads:
+        copy.start()
+    loads[1].wait()
+    misc = rest_w.at[:, pl.ds(width, 128)]
+    gain_rows(misc, gains)
+
+    def norm_one(rows):
+        value = tokens[rows, :].astype(jnp.float32)
+        normed = value * inverse_rms(value)
+        hidden[rows, :] = (normed * gains[experts : experts + 1, :]).astype(jnp.bfloat16)
+
+    row_loop(num_rows, ROW_CHUNK, norm_one)
+    loads[0].wait()
+
+    def project(index, carry):
+        cols = pl.ds(pl.multiple_of(index * TILE, TILE), TILE)
+        raw = nn_dot(hidden[...], qkv_w[:, cols])
+        turned = index < (q_heads + kv_heads) // 2
+        cos_now = jnp.where(turned, cosine[...], 1.0)
+        sin_now = jnp.where(turned, sine[...], 0.0)
+        for part in (0, 1):
+            value = rope(raw[:, part * HD : (part + 1) * HD], cos_now, sin_now)
+            heads[2 * index + part] = value.astype(jnp.bfloat16)
+        return carry
+
+    lax.fori_loop(0, (q_heads + 2 * kv_heads) // 2, project, 0)
+    lse[...] = jnp.zeros_like(lse)
+
+    def head_step(head, carry):
+        kv_head = q_heads + lax.div(head, group)
+        cols = pl.ds(pl.multiple_of(head * HD, HD), HD)
+        for first, keys in ((0, PROMPT), (PROMPT, num_rows)):
+            rows = pl.ds(first, keys - first)
+            query = heads[head, rows, :]
+            score = nt_dot(query, heads[kv_head, :keys, :]) * HD ** (-0.5) + bias[rows, :keys]
+            top = jnp.max(score, axis=1, keepdims=True)
+            weight = jnp.exp(score - top)
+            total = jnp.sum(weight, axis=1, keepdims=True)
+            value = nn_dot(weight.astype(jnp.bfloat16), heads[kv_head + kv_heads, :keys, :])
+            mixed[rows, cols] = (value / total).astype(jnp.bfloat16)
+            lanes = lax.broadcasted_iota(jnp.int32, (keys - first, 128), 1)
+            lse[rows, :] = jnp.where(lanes == head, top + jnp.log(total), lse[rows, :])
+        return carry
+
+    lax.fori_loop(0, q_heads, head_step, 0)
+
+    def out_tile(cols):
+        resid[:, cols] = tokens[:, cols].astype(jnp.float32) + nn_dot(mixed[...], rest_w[:, cols])
+
+    tile_loop(width, TILE, out_tile)
+
+    def norm_two(rows):
+        value = resid[rows, :]
+        normed = value * inverse_rms(value)
+        rows_out[rows, :width] = (normed * gains[experts + 1 : experts + 2, :]).astype(jnp.bfloat16)
+
+    row_loop(num_rows, ROW_CHUNK, norm_two)
+    logits = nn_dot(rows_out[:, :width], misc[...])
+    lanes = lax.broadcasted_iota(jnp.int32, logits.shape, 1)
+    logits = jnp.where(lanes < experts, logits, NEG_BIG)
+    weight = jnp.exp(logits - jnp.max(logits, axis=1, keepdims=True))
+    value = weight / jnp.sum(weight, axis=1, keepdims=True)
+    prob[...] = value
+    chosen = value * picked[...]
+    rows_out[:, width:] = (chosen / jnp.sum(chosen, axis=1, keepdims=True)).astype(jnp.bfloat16)
+
+
+def attend(tokens, dense_w, cosine, sine, bias, picked, q_heads, kv_heads, experts):
+    num_rows, width = tokens.shape
+    bf = jnp.bfloat16
+    all_heads = q_heads + 2 * kv_heads
+    return pl.pallas_call(
+        functools.partial(attend_kernel, q_heads, kv_heads, experts),
+        out_shape=(
+            jax.ShapeDtypeStruct((num_rows, width + 128), bf),
+            jax.ShapeDtypeStruct((num_rows, width), jnp.float32),
+            jax.ShapeDtypeStruct((all_heads, num_rows, HD), bf),
+            jax.ShapeDtypeStruct((num_rows, q_heads * HD), bf),
+            jax.ShapeDtypeStruct((num_rows, 128), jnp.float32),
+            jax.ShapeDtypeStruct((num_rows, 128), jnp.float32),
+        ),
+        in_specs=[VMEM, ANY] + [VMEM] * 4,
+        out_specs=(VMEM,) * 6,
+        scratch_shapes=[
+            pltpu.VMEM((width, all_heads * HD), bf),
+            pltpu.VMEM((q_heads * HD, width + 128), bf),
+            pltpu.VMEM((128, width), jnp.float32),
+            pltpu.VMEM((num_rows, width), bf),
+            pltpu.SemaphoreType.DMA((2,)),
+        ],
+        compiler_params=pltpu.CompilerParams(vmem_limit_bytes=VMEM_BYTES),
+        name="attend",
+    )(tokens, dense_w, cosine, sine, bias, picked)
+
+
+def attend_back_kernel(q_heads, kv_heads, experts, back_hbm, grad_hbm, resid_hbm, rows_hbm, prob_hbm, picked_hbm, dense_hbm, mixed_hbm, heads_hbm, lse_hbm, bias_hbm, cos_hbm, sin_hbm, tokens_hbm, grad_in, out_part, qkv_part, back, grad, resid, hidden_two, prob, picked, dense, mixed, heads, lse, bias, cosine, sine, tokens, gains, gain_sums, grad_logit, grad_proj, grad_mixed, grad_qkv, grad_kv, load):
+    num_rows, width = tokens.shape
+    group = q_heads // kv_heads
+    q_cols = q_heads * HD
+    qkv_cols = q_cols + 2 * kv_heads * HD
+    bf = jnp.bfloat16
+    pairs = (
+        (prob_hbm, prob),
+        (picked_hbm, picked),
+        (back_hbm, back),
+        (dense_hbm, dense),
+        (resid_hbm, resid),
+        (grad_hbm, grad),
+        (rows_hbm, hidden_two),
+        (mixed_hbm, mixed),
+        (heads_hbm, heads),
+        (lse_hbm, lse),
+        (bias_hbm, bias),
+        (cos_hbm, cosine),
+        (sin_hbm, sine),
+        (tokens_hbm, tokens),
+    )
+    loads = [pltpu.make_async_copy(src, dst, load.at[i]) for i, (src, dst) in enumerate(pairs)]
+    for copy in loads:
+        copy.start()
+    for copy in loads[:3]:
+        copy.wait()
+    gain_sums[...] = jnp.zeros_like(gain_sums)
+
+    def router_rows(rows):
+        value = prob[rows, :]
+        chosen = value * picked[rows, :]
+        total = jnp.sum(chosen, axis=1, keepdims=True)
+        comb = chosen / total
+        grad_comb = back[rows, width:]
+        grad_chosen = (
+            picked[rows, :] * (grad_comb - jnp.sum(grad_comb * comb, axis=1, keepdims=True)) / total
+        )
+        logit = value * (grad_chosen - jnp.sum(value * grad_chosen, axis=1, keepdims=True))
+        grad_logit[rows, :] = logit.astype(bf)
+
+    row_loop(num_rows, 64, router_rows)
+    loads[3].wait()
+    misc = dense.at[:, pl.ds(qkv_cols + width, 128)]
+    gain_rows(misc, gains)
+    lanes = lax.broadcasted_iota(jnp.int32, (TILE, 128), 1)
+
+    def hidden_tile(cols):
+        router = jnp.where(lanes < experts, misc[cols, :], jnp.zeros((), bf))
+        back[:, cols] = back[:, cols] + nt_dot(grad_logit[...], router)
+
+    tile_loop(width, TILE, hidden_tile)
+    for copy in loads[4:]:
+        copy.wait()
+
+    def fold(values):
+        return jnp.sum(values.reshape(-1, 8, width), axis=0)
+
+    def norm_two(rows):
+        value = resid[rows, :]
+        inverse = inverse_rms(value)
+        normed = value * inverse
+        grad_hidden = back[rows, :width]
+        gain_sums[8:16, :] = gain_sums[8:16, :] + fold(grad_hidden * normed)
+        grad_norm = grad_hidden * gains[experts + 1 : experts + 2, :]
+        mean = jnp.mean(grad_norm * normed, axis=1, keepdims=True)
+        total = grad[rows, :] + inverse * (grad_norm - normed * mean)
+        grad[rows, :] = total
+        grad_proj[rows, :] = total.astype(bf)
+
+    row_loop(num_rows, ROW_CHUNK, norm_two)
+
+    def out_tile(cols):
+        out_part[cols, :] = tn_dot(mixed[:, cols], grad_proj[...]).astype(bf)
+        grad_mixed[:, cols] = nt_dot(
+            grad_proj[...], dense[cols, pl.ds(qkv_cols, width)]
+        ).astype(bf)
+
+    tile_loop(q_cols, TILE, out_tile)
+    scale = HD ** (-0.5)
+
+    def head_step(head, carry):
+        kv_head = lax.div(head, group)
+        cols = pl.ds(pl.multiple_of(head * HD, HD), HD)
+
+        @pl.when(lax.rem(head, group) == 0)
+        def _():
+            grad_kv[...] = jnp.zeros_like(grad_kv)
+
+        for first, keys in ((0, PROMPT), (PROMPT, num_rows)):
+            rows = pl.ds(first, keys - first)
+            key = heads[q_heads + kv_head, :keys, :]
+            query = heads[head, rows, :]
+            up = grad_mixed[rows, cols]
+            lane = lax.broadcasted_iota(jnp.int32, (keys - first, 128), 1)
+            total = jnp.sum(jnp.where(lane == head, lse[rows, :], 0.0), axis=1, keepdims=True)
+            weight = jnp.exp(nt_dot(query, key) * scale + bias[rows, :keys] - total)
+            grad_weight = nt_dot(up, heads[q_heads + kv_heads + kv_head, :keys, :])
+            delta = jnp.sum(weight * grad_weight, axis=1, keepdims=True)
+            score = (weight * (grad_weight - delta)).astype(bf)
+            grad_kv[1, :keys, :] = grad_kv[1, :keys, :] + tn_dot(weight.astype(bf), up)
+            grad_kv[0, :keys, :] = grad_kv[0, :keys, :] + tn_dot(score, query) * scale
+            value = rope(nn_dot(score, key) * scale, cosine[rows, :], -sine[rows, :])
+            grad_qkv[rows, cols] = value.astype(bf)
+
+        @pl.when(lax.rem(head, group) == group - 1)
+        def _():
+            key_cols = pl.ds(pl.multiple_of(q_cols + kv_head * HD, HD), HD)
+            value_cols = pl.ds(pl.multiple_of(q_cols + (kv_heads + kv_head) * HD, HD), HD)
+            grad_qkv[:, key_cols] = rope(grad_kv[0], cosine[...], -sine[...]).astype(bf)
+            grad_qkv[:, value_cols] = grad_kv[1].astype(bf)
+
+        return carry
+
+    lax.fori_loop(0, q_heads, head_step, 0)
+    hidden = grad_mixed
+
+    def norm_one(rows):
+        value = tokens[rows, :].astype(jnp.float32)
+        normed = value * inverse_rms(value)
+        hidden[rows, :] = (normed * gains[experts : experts + 1, :]).astype(bf)
+
+    row_loop(num_rows, ROW_CHUNK, norm_one)
+
+    def hidden_back_tile(cols):
+        back[:, cols] = nt_dot(grad_qkv[...], dense[cols, pl.ds(0, qkv_cols)])
+
+    tile_loop(width, TILE, hidden_back_tile)
+
+    def last_rows(rows):
+        value = tokens[rows, :].astype(jnp.float32)
+        inverse = inverse_rms(value)
+        normed = value * inverse
+        grad_hidden = back[rows, :width]
+        gain_sums[0:8, :] = gain_sums[0:8, :] + fold(grad_hidden * normed)
+        grad_norm = grad_hidden * gains[experts : experts + 1, :]
+        mean = jnp.mean(grad_norm * normed, axis=1, keepdims=True)
+        grad_in[rows, :] = grad[rows, :] + inverse * (grad_norm - normed * mean)
+
+    row_loop(num_rows, ROW_CHUNK, last_rows)
+    gains[0:16, :] = gain_sums[...]
+
+    def weight_tile(cols):
+        qkv_part[cols, :qkv_cols] = tn_dot(hidden[:, cols], grad_qkv[...]).astype(bf)
+        router = tn_dot(hidden_two[:, cols], grad_logit[...])
+        one = jnp.sum(gains[0:8, cols], axis=0, keepdims=True)
+        two = jnp.sum(gains[8:16, cols], axis=0, keepdims=True)
+        place = lax.broadcasted_iota(jnp.int32, (128, TILE), 0)
+        block = jnp.where(place == experts, one, jnp.where(place == experts + 1, two, 0.0))
+        qkv_part[cols, qkv_cols:] = (router + jnp.transpose(block)).astype(bf)
+
+    tile_loop(width, TILE, weight_tile)
+
+
+def attend_back(back, grad, resid, rows_own, prob, picked, dense_w, mixed, heads, lse, bias, cosine, sine, tokens, q_heads, kv_heads, experts):
+    num_rows, width = tokens.shape
+    bf = jnp.bfloat16
+    arrays = (back, grad, resid, rows_own, prob, picked, dense_w, mixed, heads, lse, bias, cosine, sine, tokens)
+    qkv_cols = (q_heads + 2 * kv_heads) * HD
+    q_cols = q_heads * HD
+    return pl.pallas_call(
+        functools.partial(attend_back_kernel, q_heads, kv_heads, experts),
+        out_shape=(
+            jax.ShapeDtypeStruct((num_rows, width), jnp.float32),
+            jax.ShapeDtypeStruct((q_cols, width), bf),
+            jax.ShapeDtypeStruct((width, qkv_cols + 128), bf),
+        ),
+        in_specs=[ANY] * len(arrays),
+        out_specs=(VMEM,) * 3,
+        scratch_shapes=[pltpu.VMEM(array.shape, array.dtype) for array in arrays]
+        + [
+            pltpu.VMEM((128, width), jnp.float32),
+            pltpu.VMEM((16, width), jnp.float32),
+            pltpu.VMEM((num_rows, 128), bf),
+            pltpu.VMEM((num_rows, width), bf),
+            pltpu.VMEM((num_rows, q_cols), bf),
+            pltpu.VMEM((num_rows, qkv_cols), bf),
+            pltpu.VMEM((2, num_rows, HD), jnp.float32),
+            pltpu.SemaphoreType.DMA((len(arrays),)),
+        ],
+        compiler_params=pltpu.CompilerParams(vmem_limit_bytes=63 * 2**20),
+        name="attend_back",
+    )(*arrays)
 
 
 def body_plane(
@@ -1309,12 +1648,9 @@
     num_rows, width = tokens.shape
     half = num_rows // 2
     q_cols, k_cols = w_query.shape[1], w_key.shape[1]
-    qkv_cols = q_cols + 2 * k_cols
-    dense_cols = qkv_cols + w_out.shape[1]
     num_experts = w_router.shape[1]
     num_heads = q_cols // HD
     kv_heads = k_cols // HD
-    group_size = num_heads // kv_heads
     pad_cols = 128 - 2 - num_experts
     dense_own = jnp.concatenate(
         [
@@ -1322,9 +1658,9 @@
             w_key,
             w_value,
             w_out,
+            w_router,
             gain_attn[:, None],
             gain_moe[:, None],
-            w_router,
             jnp.zeros((gain_attn.shape[0], pad_cols), bf),
         ],
         axis=1,
@@ -1333,150 +1669,65 @@
     gate_w = lax.all_gather(w_gate, "dp", axis=1, tiled=True)[0]
     up_w = lax.all_gather(w_up, "dp", axis=1, tiled=True)[0]
     down_w = lax.all_gather(w_down, "dp", axis=1, tiled=True)[0]
-    qkv_w = dense_w[:, :qkv_cols]
-    out_w = dense_w[:, qkv_cols:dense_cols]
-    gain_one = dense_w[:, dense_cols].astype(jnp.float32)
-    gain_two = dense_w[:, dense_cols + 1].astype(jnp.float32)
-    router_w = dense_w[:, dense_cols + 2 : dense_cols + 2 + num_experts]
     tok_pos = positions(segments)
-    allowed = key_mask(segments)
-    resid_in = tokens.astype(jnp.float32)
-    inv_one = lax.rsqrt(jnp.mean(resid_in * resid_in, axis=-1, keepdims=True) + EPS)
-    normed_one = resid_in * inv_one
-    hidden_one = (normed_one * gain_one).astype(bf)
-    qkv_raw = jnp.dot(hidden_one, qkv_w, preferred_element_type=jnp.float32)
-    value_b = qkv_raw[:, q_cols + k_cols :].astype(bf)
-    query_b = rotate(qkv_raw[:, :q_cols].reshape(num_rows, num_heads, HD), tok_pos, 1.0).astype(bf)
-    query_b = query_b.reshape(num_rows, kv_heads, group_size, HD)
-    key_b = rotate(
-        qkv_raw[:, q_cols : q_cols + k_cols].reshape(num_rows, kv_heads, HD), tok_pos, 1.0
-    ).astype(bf)
-    value_h = value_b.reshape(num_rows, kv_heads, HD)
-    logit_att = attention_scores(query_b, key_b, allowed)
-    row_max = jnp.max(logit_att, axis=-1, keepdims=True)
-    log_total = row_max + jnp.log(jnp.sum(jnp.exp(logit_att - row_max), axis=-1, keepdims=True))
-    probs_b = jnp.exp(logit_att - log_total).astype(bf)
-    attn_vals = jnp.einsum("kgqp,pkd->qkgd", probs_b, value_h, preferred_element_type=jnp.float32)
-    attn_vals = attn_vals.reshape(num_rows, q_cols).astype(bf)
-    resid_mid = resid_in + jnp.dot(attn_vals, out_w, preferred_element_type=jnp.float32)
-    inv_two = lax.rsqrt(jnp.mean(resid_mid * resid_mid, axis=-1, keepdims=True) + EPS)
-    normed_two = resid_mid * inv_two
-    hidden_two = (normed_two * gain_two).astype(bf)
-    router_prob = jax.nn.softmax(
-        jnp.dot(hidden_two, router_w, preferred_element_type=jnp.float32), axis=-1
-    )
-    expert_ids = jnp.arange(num_experts, dtype=jnp.int32)
-    route_hot = routes[:, :, None] == expert_ids[None, None, :]
-    chosen = jnp.sum(jnp.where(route_hot, router_prob[:, None, :], 0.0), axis=-1)
-    weight_sum = jnp.sum(chosen, axis=1, keepdims=True)
-    combine = chosen / weight_sum
-    weight_full = jnp.sum(jnp.where(route_hot, combine[:, :, None], 0.0), axis=1)
-    rows_own = jnp.concatenate(
-        [hidden_two, jnp.pad(weight_full.astype(bf), ((0, 0), (0, 128 - num_experts)))], axis=1
+    bias = jnp.where(key_mask(segments), 0.0, NEG_BIG)
+    freq = THETA ** (-2.0 * jnp.arange(HD // 2, dtype=jnp.float32) / HD)
+    angle = tok_pos.astype(jnp.float32)[:, None] * freq[None, :]
+    cosine, sine_part = jnp.cos(angle), jnp.sin(angle)
+    cosine = jnp.concatenate([cosine, cosine], axis=1)
+    sine = jnp.concatenate([-sine_part, sine_part], axis=1)
+    lane_ids = jnp.arange(128, dtype=jnp.int32)
+    picked = jnp.sum((routes[:, :, None] == lane_ids[None, None, :]).astype(jnp.float32), axis=1)
+    rows_own, resid_mid, heads, mixed, lse, prob = attend(
+        tokens, dense_w, cosine, sine, bias, picked, num_heads, kv_heads, num_experts
     )
     rows_all, gua = expert_in(rows_own.reshape(2, half, width + 128), gate_w, up_w)
-    moe_out = expert_out(gua, down_w).reshape(num_rows, width)
-    resid_out = resid_mid + moe_out
-    layer_out = resid_out.astype(bf)
     total_rows = num_rows * lax.axis_size(("dp", "exp"))
     global_row = lax.axis_index(("dp", "exp")) * num_rows + jnp.arange(num_rows, dtype=jnp.int32)
     loss_scale = total_rows / valid_count[0].astype(jnp.float32)
-    grad_out = jnp.where(
-        (global_row < valid_count[0])[:, None],
-        (resid_out - targets.astype(jnp.float32)) * loss_scale,
-        0.0,
-    )
-    grads_all, dgu, part = expert_back(
-        grad_out.astype(bf).reshape(2, half, width), rows_all, gua, gate_w, up_w, down_w
-    )
+    scales = jnp.broadcast_to(
+        jnp.where(global_row < valid_count[0], loss_scale, 0.0)[:, None], (num_rows, 128)
+    )
+    layer_out, grad_out, grad_out_b = expert_out(gua, down_w, resid_mid, targets, scales)
+    layer_out = layer_out.reshape(num_rows, width)
+    grads_all, dgu, part = expert_back(grad_out_b, rows_all, gua, gate_w, up_w, down_w)
     back, *expert_parts = expert_grads(part, rows_all, dgu, gua, grads_all)
-    back = back.reshape(num_rows, width + 128)
     expert_sums = tuple(
         lax.psum_scatter(grad[None], "dp", scatter_dimension=1, tiled=True).astype(jnp.float32)
         for grad in expert_parts
     )
-    grad_hidden_two = back[:, :width]
-    grad_comb = jnp.sum(
-        jnp.where(route_hot, back[:, None, width : width + num_experts], 0.0), axis=-1
-    )
-    grad_chosen = (grad_comb - jnp.sum(grad_comb * combine, axis=1, keepdims=True)) / weight_sum
-    grad_prob = jnp.sum(jnp.where(route_hot, grad_chosen[:, :, None], 0.0), axis=1)
-    grad_logit = router_prob * (
-        grad_prob - jnp.sum(router_prob * grad_prob, axis=-1, keepdims=True)
-    )
-    grad_hidden_two = grad_hidden_two + jnp.einsum(
-        "re,de->rd", grad_logit, router_w.astype(jnp.float32), precision=HIGH
-    )
-    grad_router = jnp.einsum(
-        "rd,re->de", hidden_two.astype(jnp.float32), grad_logit, precision=HIGH
-    )
-    grad_gain_two = jnp.sum(grad_hidden_two * normed_two, axis=0)
-    grad_norm_two = grad_hidden_two * gain_two
-    grad_mid = grad_out + inv_two * (
-        grad_norm_two - normed_two * jnp.mean(grad_norm_two * normed_two, axis=-1, keepdims=True)
-    )
-    grad_proj_b = grad_mid.astype(bf)
-    grad_out_w = jnp.einsum("rh,rd->hd", attn_vals, grad_proj_b, preferred_element_type=jnp.float32)
-    grad_vals_b = jnp.einsum(
-        "rd,hd->rh", grad_proj_b, out_w, preferred_element_type=jnp.float32
-    ).astype(bf)
-    grad_vals_b = grad_vals_b.reshape(num_rows, kv_heads, group_size, HD)
-    logit_att = attention_scores(query_b, key_b, allowed)
-    probs = jnp.exp(logit_att - log_total)
-    probs_b = probs.astype(bf)
-    grad_value = jnp.einsum(
-        "kgqp,qkgd->pkd", probs_b, grad_vals_b, preferred_element_type=jnp.float32
-    )
-    grad_prob_att = jnp.einsum(
-        "qkgd,pkd->kgqp", grad_vals_b, value_h, preferred_element_type=jnp.float32
-    )
-    delta_row = jnp.sum(probs * grad_prob_att, axis=-1, keepdims=True)
-    grad_score_b = (probs * (grad_prob_att - delta_row)).astype(bf)
-    grad_query = jnp.einsum(
-        "kgqp,pkd->qkgd", grad_score_b, key_b, preferred_element_type=jnp.float32
-    ) * HD ** (-0.5)
-    grad_key = jnp.einsum(
-        "kgqp,qkgd->pkd", grad_score_b, query_b, preferred_element_type=jnp.float32
-    ) * HD ** (-0.5)
-    grad_query_b = rotate(grad_query.reshape(num_rows, num_heads, HD), tok_pos, -1.0).astype(bf)
-    grad_key_b = rotate(grad_key, tok_pos, -1.0).astype(bf)
-    grad_qkv_b = jnp.concatenate(
-        [
-            grad_query_b.reshape(num_rows, q_cols),
-            grad_key_b.reshape(num_rows, k_cols),
-            grad_value.astype(bf).reshape(num_rows, k_cols),
-        ],
-        axis=1,
-    )
-    grad_qkv_w = jnp.einsum("rd,rh->dh", hidden_one, grad_qkv_b, preferred_element_type=jnp.float32)
-    grad_hidden_one = jnp.einsum("rh,dh->rd", grad_qkv_b, qkv_w, preferred_element_type=jnp.float32)
-    grad_gain_one = jnp.sum(grad_hidden_one * normed_one, axis=0)
-    grad_norm_one = grad_hidden_one * gain_one
-    grad_in = grad_mid + inv_one * (
-        grad_norm_one - normed_one * jnp.mean(grad_norm_one * normed_one, axis=-1, keepdims=True)
-    )
-    qkv_part = jnp.concatenate(
-        [
-            grad_qkv_w.astype(bf),
-            jnp.pad(
-                jnp.concatenate([grad_gain_one[:, None], grad_gain_two[:, None], grad_router], axis=1),
-                ((0, 0), (0, pad_cols)),
-            ).astype(bf),
-        ],
-        axis=1,
-    )
-    dense_sum = dense_scatter((grad_out_w.astype(bf), qkv_part))
-    out_sum, qkv_sum = dense_sum[:, :width], dense_sum[:, width:]
+    grad_in, out_part, qkv_part = attend_back(
+        back.reshape(num_rows, width + 128),
+        grad_out.reshape(num_rows, width),
+        resid_mid,
+        rows_own,
+        prob,
+        picked,
+        dense_w,
+        mixed,
+        heads,
+        lse,
+        bias,
+        cosine,
+        sine,
+        tokens,
+        num_heads,
+        kv_heads,
+        num_experts,
+    )
+    out_sum, q_sum, k_sum, v_sum, misc_sum = dense_scatter(
+        (out_part, qkv_part), ((width,), (q_cols, k_cols, k_cols, 128))
+    )
     return (
         layer_out,
         grad_in,
-        qkv_sum[:, qkv_cols],
-        qkv_sum[:, :q_cols],
-        qkv_sum[:, q_cols : q_cols + k_cols],
-        qkv_sum[:, q_cols + k_cols : qkv_cols],
+        misc_sum[:, num_experts],
+        q_sum,
+        k_sum,
+        v_sum,
         out_sum,
-        qkv_sum[:, qkv_cols + 1],
-        qkv_sum[:, qkv_cols + 2 : qkv_cols + 2 + num_experts],
+        misc_sum[:, num_experts + 1],
+        misc_sum[:, :num_experts],
         *expert_sums,
     )
 

time: 636 us -> 608 us (0.956)
  Pallas kernels: 433 us -> 554 us
  matrix products: 84.6 us -> 0 us
  other arithmetic: 48.1 us -> 11.1 us
  local copies, waits for them, and re-layouts: 43.9 us -> 11 us
    pallas_call x2 -> x4, Pallas kernels: 142 us -> 263 us  [the longest x1 99.1 us: dense_scatter(): pl.pallas_call(functools.partial(dense_scatter_kernel, splits), out_shape...]
    dot_general x15 -> x0, matrix products: 84.6 us -> none  [the longest x1 11 us: body_plane(): jnp.einsum('qkgd,pkd->kgqp', grad_vals_b, value_h, preferred_element_type...]
    slice x13 -> x1, local copies, waits for them, and re-layouts: 17.9 us -> 1.52 us  [body_plane(): misc_sum[:, num_experts + 1]]
    convert_element_type x6 -> x1, other arithmetic: 12.2 us -> 0.01 us  [body_plane(): angle = tok_pos.astype(jnp.float32)[:, None] * freq[None, :]]
    add x3 -> x0, other arithmetic: 8.22 us -> none  [the longest x1 5.28 us: body_plane(): grad_mid + inv_one * (grad_norm_one - normed_one * jnp.mean(grad_norm_one...]
  transfers between devices with their start and end apart: 6 -> 6, of which waited for: 0 -> 1; matrix products, arithmetic and copies ran while one was open for 25% -> 3% of each run, Pallas kernels for 37% -> 58%
where the time goes in v3:
time: 608 us; the launch traced here: 597 us
  Pallas kernels  554 us (91%)
  between operations  15 us (2%)
  other arithmetic  11.1 us (2%)
  local copies, waits for them, and re-layouts  11 us (2%)
    pallas_call x1, Pallas kernels, dense_scatter(): pl.pallas_call(functools.partial(dense_scatter_kernel, splits), out_shape...  99.1 us
    pallas_call x1, Pallas kernels, dense_gather(): pl.pallas_call(dense_gather_kernel, out_shape=jax.ShapeDtypeStruct((4, 8,...  85.6 us
    pallas_call x1, Pallas kernels, expert_grads(): pl.pallas_call(expert_grads_kernel, out_shape=(jax.ShapeDtypeStruct((2, h...  73 us
    pallas_call x1, Pallas kernels, expert_back(): pl.pallas_call(expert_back_kernel, out_shape=(jax.ShapeDtypeStruct((8, 2,...  67.2 us
    pallas_call x1, Pallas kernels, expert_out(): pl.pallas_call(expert_out_kernel, out_shape=(jax.ShapeDtypeStruct((2, hal...  66.7 us
    pallas_call x1, Pallas kernels, expert_in(): pl.pallas_call(expert_in_kernel, out_shape=(jax.ShapeDtypeStruct((8, 2, h...  65.5 us
    pallas_call x1, Pallas kernels, attend_back(): pl.pallas_call(functools.partial(attend_back_kernel, q_heads, kv_heads, e...  62.7 us
    pallas_call x1, Pallas kernels, attend(): pl.pallas_call(functools.partial(attend_kernel, q_heads, kv_heads, expert...  34.6 us
  transfers between devices with their start and end apart: 6, of which 1 were waited for; matrix products, arithmetic and copies ran while one was open for 3% of the time, Pallas kernels for 58%

profile of v3, /device:TPU:0, one launch (start us, length us, event | category | flops | bytes accessed | tf_op | source)
XLA Modules:
  0.0 596.8 jit_solution(7180825594876173316)
XLA Ops:
  7.2 0.7 all-gather.4.cloned.1.call-update
  8.0 0.7 all-gather.6.cloned.1.call-update
  8.7 0.7 all-gather.8.cloned.1.call-update
  10.1 0.8 copy.38
  10.8 0.8 copy.39
  11.6 0.8 copy.37
  12.4 1.1 concatenate.9.own
  13.5 85.6 %dense_gather.1 = bf16[4,8,48,3712]{3,2,1,0:T(8,128)(2,1)} custom-call(bf16[48,3712]{1,0:T(8,128)(2,1)S(1)} %concatenate.9.own), custom_call_target="tpu_custom_call" | custom-call | tf_op jit(solution)/shard_map/dense_gather/pallas_call | solution.py:1160
  99.4 1.0 fusion.2
  100.4 1.0 pad_maximum_fusion
  101.4 1.0 convert_reduce_fusion.picked.picked_hbm
  102.4 1.2 fusion.1.bias.bias_hbm
  103.6 34.6 %attend.1 = (bf16[512,1664]{1,0:T(8,128)(2,1)}, f32[512,1536]{1,0:T(8,128)}, bf16[16,512,128]{2,1,0:T(8,128)(2,1)}, bf16[512,1536]{1,0:T(8,128)(2,1)}, f32[512,128]{1,0:T(8,128)}, /*index=5*/f32[512,128]{1,0:T(8,128)}) custom-call(bf16[512,1536]{1,0:T(8,128)(2,1)} %tokens_hbm.1, bf16[1536,3712]{1,0:T(8,128)(2,1)} %bitcast.22, ...), custom_call_target="tpu_custom_call" | custom-call | tf_op jit(solution)/shard_map/attend/pallas_call | solution.py:1421
  138.3 1.9 all-gather.6.cloned.1.call-done
  140.2 65.5 %expert_in.1 = (bf16[8,2,256,1664]{3,2,1,0:T(8,128)(2,1)}, bf16[8,2,256,2304]{3,2,1,0:T(8,128)(2,1)}) custom-call(bf16[2,256,1664]{2,1,0:T(8,128)(2,1)} %bitcast.32, bf16[1536,768]{1,0:T(8,128)(2,1)} %bitcast.28, bf16[1536,768]{1,0:T(8,128)(2,1)} %bitcast.30), custom_call_target="tpu_custom_call" | custom-call | tf_op jit(solution)/shard_map/expert_in/pallas_call | solution.py:533
  205.7 0.8 broadcast_in_dim.88.scales
  206.6 66.7 %expert_out.1 = (bf16[2,256,1536]{2,1,0:T(8,128)(2,1)}, f32[2,256,1536]{2,1,0:T(8,128)}, bf16[2,256,1536]{2,1,0:T(8,128)(2,1)}) custom-call(bf16[8,2,256,2304]{3,2,1,0:T(8,128)(2,1)} %get-tuple-element.39.gua_hbm, bf16[768,1536]{1,0:T(8,128)(2,1)} %bitcast.26, f32[2,256,1536]{2,1,0:T(8,128)} %bitcast.25, bf16[2,256,1536]{2,1,0:T(8,128)(2,1)} %bitcast.40, ...), custom_call_target="tpu_custom_call" | custom-call | tf_op jit(solution)/shard_map/expert_out/pallas_call | solution.py:776
  273.3 67.2 %expert_back.1 = (bf16[8,2,256,1536]{3,2,1,0:T(8,128)(2,1)}, bf16[8,2,256,1536]{3,2,1,0:T(8,128)(2,1)}, bf16[8,2,256,1664]{3,2,1,0:T(8,128)(2,1)}) custom-call(bf16[2,256,1536]{2,1,0:T(8,128)(2,1)} %get-tuple-element.42.own, bf16[8,2,256,1664]{3,2,1,0:T(8,128)(2,1)} %get-tuple-element.43.rows_hbm, bf16[8,2,256,2304]{3,2,1,0:T(8,128)(2,1)} %get-tuple-element.39.gua_hbm, ...), custom_call_target="tpu_custom_call" | custom-call | tf_op jit(solution)/shard_map/expert_back/pallas_call | solution.py:891
  340.5 73.0 %expert_grads.1 = (f32[2,256,1664]{2,1,0:T(8,128)}, bf16[1536,768]{1,0:T(8,128)(2,1)}, bf16[1536,768]{1,0:T(8,128)(2,1)}, bf16[768,1536]{1,0:T(8,128)(2,1)}) custom-call(bf16[8,2,1,256,1664]{4,3,2,1,0:T(8,128)(2,1)} %bitcast.24, bf16[8,2,256,1664]{3,2,1,0:T(8,128)(2,1)} %get-tuple-element.43.rows_hbm, bf16[8,2,256,1536]{3,2,1,0:T(8,128)(2,1)} %get-tuple-element.45.dgu_hbm, ...), custom_call_target="tpu_custom_call" | custom-call | tf_op jit(solution)/shard_map/expert_grads/pallas_call | solution.py:1039
  413.6 0.5 reduce-scatter.6.cloned.1.call-update
  414.7 62.7 %attend_back.1 = (f32[512,1536]{1,0:T(8,128)}, bf16[1536,1536]{1,0:T(8,128)(2,1)}, bf16[1536,2176]{1,0:T(8,128)(2,1)}) custom-call(f32[512,1664]{1,0:T(8,128)} %bitcast.35, f32[512,1536]{1,0:T(8,128)} %bitcast.36, f32[512,1536]{1,0:T(8,128)} %get-tuple-element.40.resid_hbm, bf16[512,1664]{1,0:T(8,128)(2,1)} %get-tuple-element.38.rows_hbm, ...), custom_call_target="tpu_custom_call" | custom-call | tf_op jit(solution)/shard_map/attend_back/pallas_call | solution.py:1605
  477.4 99.1 %dense_scatter.1 = (f32[48,1536]{1,0:T(8,128)}, f32[48,1536]{1,0:T(8,128)}, f32[48,256]{1,0:T(8,128)}, f32[48,256]{1,0:T(8,128)}, f32[48,128]{1,0:T(8,128)}) custom-call(bf16[2,2,8,48,1536]{4,3,2,1,0:T(8,128)(2,1)} %bitcast.34, bf16[2,2,8,48,2176]{4,3,2,1,0:T(8,128)(2,1)} %bitcast.33), custom_call_target="tpu_custom_call" | custom-call | tf_op jit(solution)/shard_map/dense_scatter/pallas_call | solution.py:1297
  576.5 1.4 copy.40
  577.9 1.5 slice_reduce_fusion
  579.4 2.3 convert_element_type.23
  581.7 2.2 convert_element_type.22
  583.9 2.2 convert_element_type.21
  586.1 1.1 copy.47
  587.2 0.7 copy.48
  588.0 0.6 copy.49
  588.6 0.6 copy.50
  589.2 0.7 copy.51
  (33 shorter events, 1.1 us)
Async XLA Ops:
  7.2 131.1 %all-gather.4.cloned.1.call-start = ((), (), s32[]{:S(2)}) async-start(), calls=%async_computation.3 | async-start | bytes 2949120 | tf_op jit(solution)/shard_map/all_gather | solution.py:1669
  7.9 132.3 %all-gather.6.cloned.1.call-start = ((), (), s32[]{:S(2)}) async-start(), calls=%async_computation.4 | async-start | bytes 2949120 | tf_op jit(solution)/shard_map/all_gather | solution.py:1670
  8.7 197.0 %all-gather.8.cloned.1.call-start = ((), (), s32[]{:S(2)}) async-start(), calls=%async_computation.5 | async-start | bytes 2949120 | tf_op jit(solution)/shard_map/all_gather | solution.py:1671
  9.4 570.0 %reduce-scatter.8.cloned.1.call-start = ((), (), s32[]{:S(2)}) async-start(), calls=%async_computation.8 | async-start | bytes 2949120 | tf_op jit(solution)/shard_map/reduce_scatter | solution.py:1696
  13.5 85.7 %copy-start.3 = (s32[512]{0:T(512)S(1)}, s32[512]{0:T(512)}, u32[]{:S(2)}) copy-start(s32[512]{0:T(512)} %param.18) | copy-start | bytes 6148
  13.5 87.9 %copy-start.6 = (s32[512,4]{0,1:T(4,128)S(1)}, s32[512,4]{0,1:T(4,128)}, u32[]{:S(2)}) copy-start(s32[512,4]{0,1:T(4,128)} %param.19) | copy-start | bytes 24580
  413.6 168.2 %reduce-scatter.6.cloned.1.call-start = ((), (), s32[]{:S(2)}) async-start(), calls=%async_computation.7 | async-start | bytes 2949120 | tf_op jit(solution)/shard_map/reduce_scatter | solution.py:1696
  414.2 169.7 %reduce-scatter.4.cloned.1.call-start = ((), (), s32[]{:S(2)}) async-start(), calls=%async_computation.6 | async-start | bytes 2949120 | tf_op jit(solution)/shard_map/reduce_scatter | solution.py:1696
  579.4 6.7 %copy-start = (bf16[2,256,1536]{2,1,0:T(8,128)(2,1)S(1)}, bf16[2,256,1536]{2,1,0:T(8,128)(2,1)}, u32[]{:S(2)}) copy-start(bf16[2,256,1536]{2,1,0:T(8,128)(2,1)} %get-tuple-element.41) | copy-start | bytes 4718596
  583.9 3.4 copy-start.2
  583.9 4.1 copy-start.5
  586.1 2.5 copy-start.4
  586.1 3.1 copy-start.1
Sparse Core Ops, SparseCore 0:
  9.6 78.9 all-gather.3
  90.2 49.9 all-gather.5
  141.8 48.7 all-gather.7
  413.7 46.4 reduce-scatter.7
  462.3 47.0 reduce-scatter.5
  511.6 70.0 reduce-scatter.3

commit v4 on v3

--- a/solution.py
+++ b/solution.py
@@ -577,11 +577,15 @@
 
 
 class Scatter:
-    def __init__(self, theirs, scratch):
-        self.theirs = theirs
-        self.mine, self.side, self.relay, self.final = scratch[:4]
-        self.send, self.side_sem, self.relay_sem, self.final_sem = scratch[4:]
+    def __init__(self, mine, theirs, scratch):
+        self.mine_of, self.theirs = mine, theirs
+        self.side, self.relay, self.final = scratch[:3]
+        self.send, self.side_sem, self.relay_sem, self.final_sem = scratch[3:]
         self.me, self.sib, self.xn, self.yn = plane_peers()
+
+    def mine(self, place, half):
+        slot = (self.me, self.xn, self.yn, self.xn + self.yn - self.me)[place]
+        return self.mine_of(place, slot, half)
 
     def peers(self):
         return self.sib, self.xn, self.yn
@@ -621,7 +625,7 @@
 
     def relay_copy(self, step, way):
         return remote(
-            self.mine.at[3, way],
+            self.mine(3, way),
             self.relay.at[way],
             self.send.at[step],
             self.relay_sem.at[way],
@@ -630,7 +634,7 @@
 
     def final_copy(self, step, way, half):
         return remote(
-            self.mine.at[1 + way, half],
+            self.mine(1 + way, half),
             self.final.at[way, half],
             self.send.at[step],
             self.final_sem.at[way, half],
@@ -647,13 +651,13 @@
             @pl.when(step == 2 + way)
             def _():
                 self.side_wait(3, way)
-                add_rows(self.mine.at[3, way], (self.side.at[3, way],))
+                add_rows(self.mine(3, way), (self.side.at[3, way],))
                 self.relay_copy(2 + way, way).start()
 
             @pl.when(step == 6 + way)
             def _():
                 self.side_wait(1 + way, way)
-                add_rows(self.mine.at[1 + way, way], (self.side.at[1 + way, way],))
+                add_rows(self.mine(1 + way, way), (self.side.at[1 + way, way],))
                 self.final_copy(6 + way, way, way).start()
 
     def forward(self):
@@ -661,23 +665,24 @@
             self.side_wait(1 + way, 1 - way)
             self.relay_copy(3 - way, 1 - way).wait_recv()
             add_rows(
-                self.mine.at[1 + way, 1 - way],
+                self.mine(1 + way, 1 - way),
                 (self.side.at[1 + way, 1 - way], self.relay.at[1 - way]),
             )
             self.final_copy(10 + way, way, 1 - way).start()
 
     def finish(self, write):
-        parts, rows_all = self.mine.shape[2:4]
+        parts, rows_all = self.relay.shape[1:3]
         chunk = row_chunk(rows_all)
         for half in (0, 1):
+            home = self.mine(0, half)
             self.side_wait(0, half)
             self.final_copy(0, 0, half).wait_recv()
             self.final_copy(0, 1, half).wait_recv()
             for part in range(parts):
 
-                def one(index, carry):
+                def one(index, carry, half=half, home=home, part=part):
                     rows = pl.ds(pl.multiple_of(index * chunk, chunk), chunk)
-                    total = self.mine[0, half, part, rows, :].astype(jnp.float32)
+                    total = home[part, rows, :].astype(jnp.float32)
                     total = total + self.side[0, half, part, rows, :].astype(jnp.float32)
                     total = total + self.final[0, half, part, rows, :].astype(jnp.float32)
                     total = total + self.final[1, half, part, rows, :].astype(jnp.float32)
@@ -702,13 +707,12 @@
         lax.fori_loop(0, 16, one, 0)
 
 
-SCATTER_REFS = 8
+SCATTER_REFS = 7
 
 
 def scatter_scratch(parts, rows, columns):
     bf = jnp.bfloat16
     return [
-        pltpu.VMEM((4, 2, parts, rows, columns), bf),
         pltpu.VMEM((4, 2, parts, rows, columns), bf),
         pltpu.VMEM((2, parts, rows, columns), bf),
         pltpu.VMEM((2, 2, parts, rows, columns), bf),
@@ -719,10 +723,13 @@
     ]
 
 
-def expert_out_kernel(gua_hbm, down_hbm, resid, targets, scales, layer, grad, grad_b, act, down_w, away, load, *scratch):
+def expert_out_kernel(gua_hbm, down_hbm, resid, targets, scales, layer, grad, grad_b, act, down_w, mine, away, load, *scratch):
     hidden = down_w.shape[0]
-    scatter = Scatter(lambda place, slot, half: away.at[place, half], scratch)
-    mine = scatter.mine
+    scatter = Scatter(
+        lambda place, slot, half: mine.at[place, half],
+        lambda place, slot, half: away.at[place, half],
+        scratch,
+    )
     down_load = pltpu.make_async_copy(down_hbm, down_w, load.at[16])
     down_load.start()
 
@@ -786,6 +793,7 @@
             pltpu.VMEM((8, 2, half, hidden), jnp.bfloat16),
             pltpu.VMEM((hidden, width), jnp.bfloat16),
             pltpu.VMEM((4, 2, 1, half, width), jnp.bfloat16),
+            pltpu.VMEM((4, 2, 1, half, width), jnp.bfloat16),
             pltpu.SemaphoreType.DMA((17,)),
         ]
         + scatter_scratch(1, half, width),
@@ -802,7 +810,7 @@
     )
 
 
-def expert_back_kernel(own, rows_hbm, gua_hbm, gate_hbm, up_hbm, down_hbm, grads_out, dgu_out, part_out, buf, gu, tails, part, gate_w, up_w, down_w, send, recv, load, load_gu, load_tail, store_a, store_b, store_c):
+def expert_back_kernel(own, rows_hbm, gua_hbm, gate_hbm, up_hbm, down_hbm, dgu_out, part_out, down_out, buf, gua, tails, part, gate_w, up_w, down_w, down_acc, send, recv, load, load_gua, load_tail, store_b, store_c):
     width, hidden = gate_w.shape
     gather = Gather(own, buf, send, recv)
     loads = (
@@ -819,7 +827,7 @@
         slot, half, _ = gather.place(step)
         return (
             pltpu.make_async_copy(
-                gua_hbm.at[slot, half, :, pl.ds(0, 2 * hidden)], gu.at[slot, half], load_gu.at[step]
+                gua_hbm.at[slot, half], gua.at[slot, half], load_gua.at[step]
             ),
             pltpu.make_async_copy(
                 rows_hbm.at[slot, half, :, pl.ds(width, 128)], tails.at[slot, half], load_tail.at[step]
@@ -836,52 +844,100 @@
     for copy in loads:
         copy.wait()
 
-    def stores(step):
+    def dgu_store(step):
         slot, half, _ = gather.place(step)
-        return (
-            pltpu.make_async_copy(buf.at[slot, half], grads_out.at[slot, half], store_a.at[step]),
-            pltpu.make_async_copy(gu.at[slot, half], dgu_out.at[slot, half], store_b.at[step]),
-            pltpu.make_async_copy(part.at[slot, half], part_out.at[slot, half], store_c.at[step]),
-        )
+        return pltpu.make_async_copy(
+            gua.at[slot, half, :, pl.ds(0, 2 * hidden)], dgu_out.at[slot, half], store_b.at[step]
+        )
+
+    def part_store(step):
+        slot, half, _ = gather.place(step)
+        return pltpu.make_async_copy(
+            part.at[lax.rem(step, PART_SLOTS)], part_out.at[slot, half], store_c.at[step]
+        )
+
+    def grad_down(step):
+        slot_a, half_a, _ = gather.place(step - 1)
+        slot_b, half_b, _ = gather.place(step)
+
+        def tile(index, carry):
+            rows = pl.ds(pl.multiple_of(index * 256, 256), 256)
+            cols = pl.ds(pl.multiple_of(2 * hidden + index * 256, 256), 256)
+            total = tn_dot(gua[slot_a, half_a, :, cols], buf[slot_a, half_a]) + tn_dot(
+                gua[slot_b, half_b, :, cols], buf[slot_b, half_b]
+            )
+
+            @pl.when(step == 1)
+            def _():
+                down_acc[rows, :] = total
+
+            @pl.when(step > 1)
+            def _():
+                down_acc[rows, :] = down_acc[rows, :] + total
+
+            return carry
+
+        lax.fori_loop(0, hidden // 256, tile, 0)
 
     def one(step, carry):
         slot, half = gather.arrive(step)
-        store_rows, store_dgu, store_part = stores(step)
-        store_rows.start()
+
+        @pl.when(step >= PART_SLOTS)
+        def _():
+            part_store(step - PART_SLOTS).wait()
+
+        part_now = part.at[lax.rem(step, PART_SLOTS)]
         for copy in block_loads(step):
             copy.wait()
         lanes = lax.broadcasted_iota(jnp.int32, (buf.shape[2], 128), 1)
         tail = tails[slot, half].astype(jnp.float32)
         weight = jnp.sum(jnp.where(lanes == gather.me, tail, 0.0), axis=1, keepdims=True)
         grad_act = nt_dot(buf[slot, half], down_w[...])
-        gate_val = gu[slot, half, :, :hidden].astype(jnp.float32)
-        up_val = gu[slot, half, :, hidden:].astype(jnp.float32)
+        gate_val = gua[slot, half, :, :hidden].astype(jnp.float32)
+        up_val = gua[slot, half, :, hidden : 2 * hidden].astype(jnp.float32)
         gate_relu = jnp.maximum(gate_val, 0.0)
         grad_comb = jnp.sum(gate_relu * up_val * grad_act, axis=1, keepdims=True)
         grad_act = grad_act * weight
         grad_gate = jnp.where(gate_val > 0, grad_act * up_val, 0.0).astype(jnp.bfloat16)
         grad_up = (grad_act * gate_relu).astype(jnp.bfloat16)
-        gu[slot, half, :, :hidden] = grad_gate
-        gu[slot, half, :, hidden:] = grad_up
-        store_dgu.start()
-        part[slot, half, :, :width] = (
+        gua[slot, half, :, :hidden] = grad_gate
+        gua[slot, half, :, hidden : 2 * hidden] = grad_up
+        dgu_store(step).start()
+        part_now[:, :width] = (
             nt_dot(grad_gate, gate_w[...]) + nt_dot(grad_up, up_w[...])
         ).astype(jnp.bfloat16)
-        part[slot, half, :, width:] = jnp.where(lanes == gather.me, grad_comb, 0.0).astype(
+        part_now[:, width:] = jnp.where(lanes == gather.me, grad_comb, 0.0).astype(
             jnp.bfloat16
         )
-        store_part.start()
+        part_store(step).start()
+
+        @pl.when(lax.rem(step, 2) == 1)
+        def _():
+            grad_down(step)
+
         return carry
 
     lax.fori_loop(0, 16, one, 0)
     gather.finish()
 
+    def round_down(rows):
+        down_out[rows, :] = down_acc[rows, :].astype(jnp.bfloat16)
+
+    row_loop(hidden, 64, round_down)
+
     def drain(step, carry):
-        for copy in stores(step):
-            copy.wait()
+        dgu_store(step).wait()
+
+        @pl.when(step >= 16 - PART_SLOTS)
+        def _():
+            part_store(step).wait()
+
         return carry
 
     lax.fori_loop(0, 16, drain, 0)
+
+
+PART_SLOTS = 4
 
 
 def expert_back(own, rows_all, gua, gate_w, up_w, down_w):
@@ -891,25 +947,26 @@
     return pl.pallas_call(
         expert_back_kernel,
         out_shape=(
-            jax.ShapeDtypeStruct((8, 2, half, width), bf),
             jax.ShapeDtypeStruct((8, 2, half, 2 * hidden), bf),
             jax.ShapeDtypeStruct((8, 2, half, columns), bf),
+            jax.ShapeDtypeStruct((hidden, width), bf),
         ),
         in_specs=[ANY] * 6,
-        out_specs=(ANY,) * 3,
+        out_specs=(ANY, ANY, VMEM),
         scratch_shapes=[
             pltpu.VMEM((8, 2, half, width), bf),
-            pltpu.VMEM((8, 2, half, 2 * hidden), bf),
+            pltpu.VMEM((8, 2, half, 3 * hidden), bf),
             pltpu.VMEM((8, 2, half, 128), bf),
-            pltpu.VMEM((8, 2, half, columns), bf),
+            pltpu.VMEM((PART_SLOTS, half, columns), bf),
             pltpu.VMEM((width, hidden), bf),
             pltpu.VMEM((width, hidden), bf),
             pltpu.VMEM((hidden, width), bf),
+            pltpu.VMEM((hidden, width), jnp.float32),
             pltpu.SemaphoreType.DMA((14,)),
             pltpu.SemaphoreType.DMA((8, 2)),
             pltpu.SemaphoreType.DMA((5,)),
         ]
-        + [pltpu.SemaphoreType.DMA((16,))] * 5,
+        + [pltpu.SemaphoreType.DMA((16,))] * 4,
         compiler_params=pltpu.CompilerParams(
             collective_id=3, has_side_effects=True, vmem_limit_bytes=VMEM_BYTES
         ),
@@ -917,14 +974,19 @@
     )(own, rows_all, gua, gate_w, up_w, down_w)
 
 
-def expert_grads_kernel(part_hbm, rows_hbm, dgu_hbm, gua_hbm, grads_hbm, out, gate_out, up_out, down_out, rows, dgu, act, grads, gate_up_acc, down_acc, load, block_load, *scratch):
-    hidden, width = down_acc.shape
-    scatter = Scatter(lambda place, slot, half: part_hbm.at[slot, half], scratch)
+def expert_grads_kernel(part_hbm, rows_hbm, dgu_hbm, out, gate_out, up_out, rows, dgu, acc, mine, load, block_load, *scratch):
+    width = acc.shape[0]
+    hidden = acc.shape[1] // 2
+    scatter = Scatter(
+        lambda place, slot, half: mine.at[place, half],
+        lambda place, slot, half: part_hbm.at[slot, half],
+        scratch,
+    )
 
     def part_load(step):
         slot, half, _, place = scatter.place(step)
         return pltpu.make_async_copy(
-            part_hbm.at[slot, half], scatter.mine.at[place, half], load.at[step]
+            part_hbm.at[slot, half], mine.at[place, half], load.at[step]
         )
 
     def fetch(step, carry):
@@ -941,10 +1003,6 @@
                 rows_hbm.at[block, :, :, pl.ds(0, width)], rows.at[slot], block_load.at[slot, 0]
             ),
             pltpu.make_async_copy(dgu_hbm.at[block], dgu.at[slot], block_load.at[slot, 1]),
-            pltpu.make_async_copy(
-                gua_hbm.at[block, :, :, pl.ds(2 * hidden, hidden)], act.at[slot], block_load.at[slot, 2]
-            ),
-            pltpu.make_async_copy(grads_hbm.at[block], grads.at[slot], block_load.at[slot, 3]),
         )
 
     lax.fori_loop(0, 16, fetch, 0)
@@ -974,10 +1032,10 @@
 
         slot = lax.rem(block, 2)
 
-        def add_tile(acc, left, right, index):
+        def add_tile(index, carry):
             cols = pl.ds(pl.multiple_of(index * tile, tile), tile)
             total = tn_dot(
-                left[slot, :, :, cols].reshape(-1, tile), right[slot].reshape(-1, width)
+                rows[slot, :, :, cols].reshape(-1, tile), dgu[slot].reshape(-1, 2 * hidden)
             )
 
             @pl.when(block == 0)
@@ -988,16 +1046,9 @@
             def _():
                 acc[cols, :] = acc[cols, :] + total
 
-        def gate_up_tile(index, carry):
-            add_tile(gate_up_acc, rows, dgu, index)
             return carry
 
-        def down_tile(index, carry):
-            add_tile(down_acc, act, grads, index)
-            return carry
-
-        lax.fori_loop(0, width // tile, gate_up_tile, 0)
-        lax.fori_loop(0, hidden // tile, down_tile, 0)
+        lax.fori_loop(0, width // tile, add_tile, 0)
         return carry
 
     def blocks(index, carry):
@@ -1011,18 +1062,11 @@
 
     def round_tile(index, carry):
         cols = pl.ds(pl.multiple_of(index * 64, 64), 64)
-        gate_out[cols, :] = gate_up_acc[cols, :hidden].astype(jnp.bfloat16)
-        up_out[cols, :] = gate_up_acc[cols, hidden:].astype(jnp.bfloat16)
+        gate_out[cols, :] = acc[cols, :hidden].astype(jnp.bfloat16)
+        up_out[cols, :] = acc[cols, hidden:].astype(jnp.bfloat16)
         return carry
 
     lax.fori_loop(0, width // 64, round_tile, 0)
-
-    def round_down(index, carry):
-        cols = pl.ds(pl.multiple_of(index * 64, 64), 64)
-        down_out[cols, :] = down_acc[cols, :].astype(jnp.bfloat16)
-        return carry
-
-    lax.fori_loop(0, hidden // 64, round_down, 0)
 
     def write(half, part, rows, total):
         out[half, rows, :] = total
@@ -1031,9 +1075,9 @@
     scatter.drain()
 
 
-def expert_grads(part, rows_all, dgu, gua, grads_all):
+def expert_grads(part, rows_all, dgu):
     _, _, half, columns = part.shape
-    width = grads_all.shape[3]
+    width = columns - 128
     hidden = dgu.shape[3] // 2
     bf = jnp.bfloat16
     return pl.pallas_call(
@@ -1042,26 +1086,23 @@
             jax.ShapeDtypeStruct((2, half, columns), jnp.float32),
             jax.ShapeDtypeStruct((width, hidden), bf),
             jax.ShapeDtypeStruct((width, hidden), bf),
-            jax.ShapeDtypeStruct((hidden, width), bf),
         ),
-        in_specs=[ANY] * 5,
-        out_specs=(VMEM,) * 4,
+        in_specs=[ANY] * 3,
+        out_specs=(VMEM,) * 3,
         scratch_shapes=[
             pltpu.VMEM((2, 2, half, width), bf),
             pltpu.VMEM((2, 2, half, 2 * hidden), bf),
-            pltpu.VMEM((2, 2, half, hidden), bf),
-            pltpu.VMEM((2, 2, half, width), bf),
             pltpu.VMEM((width, 2 * hidden), jnp.float32),
-            pltpu.VMEM((hidden, width), jnp.float32),
+            pltpu.VMEM((4, 2, 1, half, columns), bf),
             pltpu.SemaphoreType.DMA((16,)),
-            pltpu.SemaphoreType.DMA((2, 4)),
+            pltpu.SemaphoreType.DMA((2, 2)),
         ]
         + scatter_scratch(1, half, columns),
         compiler_params=pltpu.CompilerParams(
             collective_id=4, has_side_effects=True, vmem_limit_bytes=VMEM_BYTES
         ),
         name="expert_grads",
-    )(part.reshape(8, 2, 1, half, columns), rows_all, dgu, gua, grads_all)
+    )(part.reshape(8, 2, 1, half, columns), rows_all, dgu)
 
 
 def line_peers():
@@ -1176,41 +1217,40 @@
 
 
 class LineScatter:
-    def __init__(self, scratch):
-        self.sums, self.other, self.send, self.recv = scratch
+    def __init__(self, sums, scratch):
+        self.sums = sums
+        self.other, self.send, self.recv = scratch
         self.line = line_peers()
 
     def copy(self, turn):
         target = self.line[turn]
         return line_remote(
-            self.sums.at[target],
+            self.sums(target),
             self.other.at[turn - 1],
             self.send.at[turn - 1],
             self.recv.at[turn - 1],
             target,
         )
 
-    def write(self, half, part, rows, total):
-        self.sums[2 * half + part, rows, :] = total.astype(self.sums.dtype)
-
     def begin(self):
         for turn in (1, 2, 3):
             self.copy(turn).start()
 
     def finish(self, outs):
-        rows_all = outs[0].shape[0]
+        rows_all = self.other.shape[1]
         for turn in (1, 2, 3):
             self.copy(turn).wait_recv()
+        own = self.sums(self.line[0])
 
         def one(index, carry):
             rows = pl.ds(pl.multiple_of(index * 16, 16), 16)
-            total = self.sums[self.line[0], rows, :].astype(jnp.float32)
+            total = own[rows, :].astype(jnp.float32)
             for turn in (0, 1, 2):
                 total = total + self.other[turn, rows, :].astype(jnp.float32)
             first = 0
-            for out in outs:
-                out[rows, :] = total[:, first : first + out.shape[1]]
-                first += out.shape[1]
+            for out, place, columns in outs:
+                out[rows, place : place + columns] = total[:, first : first + columns]
+                first += columns
             return carry
 
         lax.fori_loop(0, rows_all // 16, one, 0)
@@ -1218,93 +1258,49 @@
             self.copy(turn).wait_send()
 
 
-LINE_REFS = 4
-
-
-def line_scratch(rows, columns):
-    bf = jnp.bfloat16
-    return [
-        pltpu.VMEM((4, rows, columns), bf),
-        pltpu.VMEM((3, rows, columns), bf),
+class DenseScatter:
+    def __init__(self, total, scratch):
+        def block(place, slot, half):
+            return total.at[half, :, slot]
+
+        self.plane = Scatter(block, block, scratch[:SCATTER_REFS])
+        me = self.plane.me
+        self.line = LineScatter(
+            lambda line: total.at[lax.div(line, 2), lax.rem(line, 2), me], scratch[SCATTER_REFS:]
+        )
+
+    def begin(self):
+        def one(step, carry):
+            self.plane.depart(step)
+            return carry
+
+        lax.fori_loop(0, 16, one, 0)
+
+    def forward(self):
+        self.plane.forward()
+
+    def turn(self):
+        def write(half, part, rows, total):
+            home = self.plane.mine(0, half)
+            home[part, rows, :] = total.astype(home.dtype)
+
+        self.plane.finish(write)
+        self.line.begin()
+
+    def finish(self, outs):
+        self.line.finish(outs)
+        self.plane.drain()
+
+
+DENSE_REFS = SCATTER_REFS + 3
+
+
+def dense_scratch(rows, columns):
+    return scatter_scratch(2, rows, columns) + [
+        pltpu.VMEM((3, rows, columns), jnp.bfloat16),
         pltpu.SemaphoreType.DMA((3,)),
         pltpu.SemaphoreType.DMA((3,)),
     ]
-
-
-def dense_scatter_kernel(splits, *refs):
-    groups, count = len(splits), sum(len(split) for split in splits)
-    parts, outs, refs = refs[:groups], refs[groups : groups + count], refs[groups + count :]
-    step_refs = 1 + SCATTER_REFS + LINE_REFS
-    loads, planes, lines = [], [], []
-    for index, part in enumerate(parts):
-        some = refs[index * step_refs : (index + 1) * step_refs]
-        plane = Scatter(
-            lambda place, slot, half, part=part: part.at[half, :, slot], some[1 : 1 + SCATTER_REFS]
-        )
-
-        def load(step, part=part, plane=plane, sem=some[0]):
-            slot, half, _, place = plane.place(step)
-            return pltpu.make_async_copy(
-                part.at[half, :, slot], plane.mine.at[place, half], sem.at[step]
-            )
-
-        loads.append(load)
-        planes.append(plane)
-        lines.append(LineScatter(some[1 + SCATTER_REFS :]))
-
-    for plane, load in zip(planes, loads):
-
-        def fetch(step, carry, plane=plane, load=load):
-            @pl.when(plane.place(step)[2] == 0)
-            def _():
-                load(step).start()
-
-            return carry
-
-        lax.fori_loop(0, 16, fetch, 0)
-    full_barrier(planes[0].peers(), lines[0].line[1:])
-    for plane, load in zip(planes, loads):
-
-        def one(step, carry, plane=plane, load=load):
-            @pl.when(plane.place(step)[2] == 0)
-            def _():
-                load(step).wait()
-
-            plane.depart(step)
-            return carry
-
-        lax.fori_loop(0, 16, one, 0)
-    for plane in planes:
-        plane.forward()
-    for plane, line in zip(planes, lines):
-        plane.finish(line.write)
-        line.begin()
-    for plane, line, split in zip(planes, lines, splits):
-        line.finish(outs[: len(split)])
-        outs = outs[len(split) :]
-        plane.drain()
-
-
-def dense_scatter(parts, splits):
-    rows = parts[0].shape[0] // 32
-    scratch = []
-    for part in parts:
-        scratch += [pltpu.SemaphoreType.DMA((16,))]
-        scratch += scatter_scratch(2, rows, part.shape[1]) + line_scratch(rows, part.shape[1])
-    shapes = [
-        jax.ShapeDtypeStruct((rows, columns), jnp.float32) for split in splits for columns in split
-    ]
-    return pl.pallas_call(
-        functools.partial(dense_scatter_kernel, splits),
-        out_shape=shapes,
-        in_specs=[ANY] * len(parts),
-        out_specs=[VMEM] * len(shapes),
-        scratch_shapes=scratch,
-        compiler_params=pltpu.CompilerParams(
-            collective_id=6, has_side_effects=True, vmem_limit_bytes=VMEM_BYTES
-        ),
-        name="dense_scatter",
-    )(*(part.reshape(2, 2, 8, rows, part.shape[1]) for part in parts))
 
 
 def rope(values, cosine, sine):
@@ -1442,12 +1438,21 @@
     )(tokens, dense_w, cosine, sine, bias, picked)
 
 
-def attend_back_kernel(q_heads, kv_heads, experts, back_hbm, grad_hbm, resid_hbm, rows_hbm, prob_hbm, picked_hbm, dense_hbm, mixed_hbm, heads_hbm, lse_hbm, bias_hbm, cos_hbm, sin_hbm, tokens_hbm, grad_in, out_part, qkv_part, back, grad, resid, hidden_two, prob, picked, dense, mixed, heads, lse, bias, cosine, sine, tokens, gains, gain_sums, grad_logit, grad_proj, grad_mixed, grad_qkv, grad_kv, load):
+def attend_back_kernel(q_heads, kv_heads, experts, back_hbm, grad_hbm, resid_hbm, rows_hbm, prob_hbm, picked_hbm, dense_hbm, mixed_hbm, heads_hbm, lse_hbm, bias_hbm, cos_hbm, sin_hbm, tokens_hbm, grad_in, out_sum, q_sum, k_sum, v_sum, misc_sum, back, grad, resid, hidden_two, prob, picked, dense, mixed, heads, lse, bias, cosine, sine, tokens, gains, gain_sums, grad_logit, grad_proj, grad_mixed, grad_qkv, grad_kv, hidden, load, *scratch):
     num_rows, width = tokens.shape
     group = q_heads // kv_heads
     q_cols = q_heads * HD
-    qkv_cols = q_cols + 2 * kv_heads * HD
+    k_cols = kv_heads * HD
+    qkv_cols = q_cols + 2 * k_cols
+    near_cols = group * HD
     bf = jnp.bfloat16
+    parts, scatters = [], []
+    for index in range(4):
+        some = scratch[index * (1 + DENSE_REFS) : (index + 1) * (1 + DENSE_REFS)]
+        parts.append(some[0])
+        scatters.append(DenseScatter(some[0], some[1:]))
+    out_part, near_part, rest_part, misc_part = parts
+    out_scatter, near_scatter, rest_scatter, misc_scatter = scatters
     pairs = (
         (prob_hbm, prob),
         (picked_hbm, picked),
@@ -1467,6 +1472,7 @@
     loads = [pltpu.make_async_copy(src, dst, load.at[i]) for i, (src, dst) in enumerate(pairs)]
     for copy in loads:
         copy.start()
+    full_barrier(out_scatter.plane.peers(), out_scatter.line.line[1:])
     for copy in loads[:3]:
         copy.wait()
     gain_sums[...] = jnp.zeros_like(gain_sums)
@@ -1514,13 +1520,34 @@
 
     row_loop(num_rows, ROW_CHUNK, norm_two)
 
-    def out_tile(cols):
-        out_part[cols, :] = tn_dot(mixed[:, cols], grad_proj[...]).astype(bf)
+    def weight_loop(part, left, right):
+        _, _, blocks, rows_each, columns = part.shape
+        span = blocks * rows_each
+
+        def one(line, carry):
+            cols = pl.ds(pl.multiple_of(line * span, 128), span)
+            total = tn_dot(left[:, cols], right[...]).astype(bf)
+            part[lax.div(line, 2), lax.rem(line, 2)] = total.reshape(blocks, rows_each, columns)
+            return carry
+
+        lax.fori_loop(0, 4, one, 0)
+
+    weight_loop(out_part, mixed, grad_proj)
+    out_scatter.begin()
+
+    def mixed_tile(cols):
         grad_mixed[:, cols] = nt_dot(
             grad_proj[...], dense[cols, pl.ds(qkv_cols, width)]
         ).astype(bf)
 
-    tile_loop(q_cols, TILE, out_tile)
+    tile_loop(q_cols, TILE, mixed_tile)
+
+    def norm_one(rows):
+        value = tokens[rows, :].astype(jnp.float32)
+        normed = value * inverse_rms(value)
+        hidden[rows, :] = (normed * gains[experts : experts + 1, :]).astype(bf)
+
+    row_loop(num_rows, ROW_CHUNK, norm_one)
     scale = HD ** (-0.5)
 
     def head_step(head, carry):
@@ -1554,22 +1581,35 @@
             grad_qkv[:, key_cols] = rope(grad_kv[0], cosine[...], -sine[...]).astype(bf)
             grad_qkv[:, value_cols] = grad_kv[1].astype(bf)
 
+        @pl.when(head == 2)
+        def _():
+            out_scatter.forward()
+
+        @pl.when(head == group - 1)
+        def _():
+            weight_loop(near_part, hidden, grad_qkv.at[:, pl.ds(0, near_cols)])
+            near_scatter.begin()
+
+        @pl.when(head == group + 1)
+        def _():
+            out_scatter.turn()
+
+        @pl.when(head == group + 3)
+        def _():
+            near_scatter.forward()
+
         return carry
 
     lax.fori_loop(0, q_heads, head_step, 0)
-    hidden = grad_mixed
-
-    def norm_one(rows):
-        value = tokens[rows, :].astype(jnp.float32)
-        normed = value * inverse_rms(value)
-        hidden[rows, :] = (normed * gains[experts : experts + 1, :]).astype(bf)
-
-    row_loop(num_rows, ROW_CHUNK, norm_one)
+    weight_loop(rest_part, hidden, grad_qkv.at[:, pl.ds(near_cols, qkv_cols - near_cols)])
+    rest_scatter.begin()
+    near_scatter.turn()
 
     def hidden_back_tile(cols):
         back[:, cols] = nt_dot(grad_qkv[...], dense[cols, pl.ds(0, qkv_cols)])
 
     tile_loop(width, TILE, hidden_back_tile)
+    rest_scatter.forward()
 
     def last_rows(rows):
         value = tokens[rows, :].astype(jnp.float32)
@@ -1579,38 +1619,62 @@
         gain_sums[0:8, :] = gain_sums[0:8, :] + fold(grad_hidden * normed)
         grad_norm = grad_hidden * gains[experts : experts + 1, :]
         mean = jnp.mean(grad_norm * normed, axis=1, keepdims=True)
-        grad_in[rows, :] = grad[rows, :] + inverse * (grad_norm - normed * mean)
+        grad[rows, :] = grad[rows, :] + inverse * (grad_norm - normed * mean)
 
     row_loop(num_rows, ROW_CHUNK, last_rows)
+    store = pltpu.make_async_copy(grad, grad_in, load.at[0])
+    store.start()
     gains[0:16, :] = gain_sums[...]
-
-    def weight_tile(cols):
-        qkv_part[cols, :qkv_cols] = tn_dot(hidden[:, cols], grad_qkv[...]).astype(bf)
+    _, _, blocks, rows_each, _ = misc_part.shape
+    span = blocks * rows_each
+
+    def misc_line(line, carry):
+        cols = pl.ds(pl.multiple_of(line * span, 128), span)
         router = tn_dot(hidden_two[:, cols], grad_logit[...])
         one = jnp.sum(gains[0:8, cols], axis=0, keepdims=True)
         two = jnp.sum(gains[8:16, cols], axis=0, keepdims=True)
-        place = lax.broadcasted_iota(jnp.int32, (128, TILE), 0)
+        place = lax.broadcasted_iota(jnp.int32, (128, span), 0)
         block = jnp.where(place == experts, one, jnp.where(place == experts + 1, two, 0.0))
-        qkv_part[cols, qkv_cols:] = (router + jnp.transpose(block)).astype(bf)
-
-    tile_loop(width, TILE, weight_tile)
+        total = (router + jnp.transpose(block)).astype(bf)
+        misc_part[lax.div(line, 2), lax.rem(line, 2)] = total.reshape(blocks, rows_each, 128)
+        return carry
+
+    lax.fori_loop(0, 4, misc_line, 0)
+    misc_scatter.begin()
+    misc_scatter.forward()
+    rest_scatter.turn()
+    misc_scatter.turn()
+    out_scatter.finish(((out_sum, 0, width),))
+    near_scatter.finish(((q_sum, 0, near_cols),))
+    rest_scatter.finish(
+        ((q_sum, near_cols, q_cols - near_cols), (k_sum, 0, k_cols), (v_sum, 0, k_cols))
+    )
+    misc_scatter.finish(((misc_sum, 0, 128),))
+    store.wait()
 
 
 def attend_back(back, grad, resid, rows_own, prob, picked, dense_w, mixed, heads, lse, bias, cosine, sine, tokens, q_heads, kv_heads, experts):
     num_rows, width = tokens.shape
     bf = jnp.bfloat16
     arrays = (back, grad, resid, rows_own, prob, picked, dense_w, mixed, heads, lse, bias, cosine, sine, tokens)
-    qkv_cols = (q_heads + 2 * kv_heads) * HD
+    k_cols = kv_heads * HD
     q_cols = q_heads * HD
+    qkv_cols = q_cols + 2 * k_cols
+    near_cols = q_cols // kv_heads
+    block_rows = width // 32
+    scratch = []
+    for columns in (width, near_cols, qkv_cols - near_cols, 128):
+        scratch += [pltpu.VMEM((2, 2, 8, block_rows, columns), bf)]
+        scratch += dense_scratch(block_rows, columns)
     return pl.pallas_call(
         functools.partial(attend_back_kernel, q_heads, kv_heads, experts),
-        out_shape=(
-            jax.ShapeDtypeStruct((num_rows, width), jnp.float32),
-            jax.ShapeDtypeStruct((q_cols, width), bf),
-            jax.ShapeDtypeStruct((width, qkv_cols + 128), bf),
+        out_shape=(jax.ShapeDtypeStruct((num_rows, width), jnp.float32),)
+        + tuple(
+            jax.ShapeDtypeStruct((block_rows, columns), jnp.float32)
+            for columns in (width, q_cols, k_cols, k_cols, 128)
         ),
         in_specs=[ANY] * len(arrays),
-        out_specs=(VMEM,) * 3,
+        out_specs=(ANY,) + (VMEM,) * 5,
         scratch_shapes=[pltpu.VMEM(array.shape, array.dtype) for array in arrays]
         + [
             pltpu.VMEM((128, width), jnp.float32),
@@ -1620,9 +1684,13 @@
             pltpu.VMEM((num_rows, q_cols), bf),
             pltpu.VMEM((num_rows, qkv_cols), bf),
             pltpu.VMEM((2, num_rows, HD), jnp.float32),
+            pltpu.VMEM((num_rows, width), bf),
             pltpu.SemaphoreType.DMA((len(arrays),)),
-        ],
-        compiler_params=pltpu.CompilerParams(vmem_limit_bytes=63 * 2**20),
+        ]
+        + scratch,
+        compiler_params=pltpu.CompilerParams(
+            collective_id=6, has_side_effects=True, vmem_limit_bytes=67043328
+        ),
         name="attend_back",
     )(*arrays)
 
@@ -1690,13 +1758,13 @@
     )
     layer_out, grad_out, grad_out_b = expert_out(gua, down_w, resid_mid, targets, scales)
     layer_out = layer_out.reshape(num_rows, width)
-    grads_all, dgu, part = expert_back(grad_out_b, rows_all, gua, gate_w, up_w, down_w)
-    back, *expert_parts = expert_grads(part, rows_all, dgu, gua, grads_all)
+    dgu, part, down_part = expert_back(grad_out_b, rows_all, gua, gate_w, up_w, down_w)
+    back, gate_part, up_part = expert_grads(part, rows_all, dgu)
     expert_sums = tuple(
         lax.psum_scatter(grad[None], "dp", scatter_dimension=1, tiled=True).astype(jnp.float32)
-        for grad in expert_parts
-    )
-    grad_in, out_part, qkv_part = attend_back(
+        for grad in (gate_part, up_part, down_part)
+    )
+    grad_in, out_sum, q_sum, k_sum, v_sum, misc_sum = attend_back(
         back.reshape(num_rows, width + 128),
         grad_out.reshape(num_rows, width),
         resid_mid,
@@ -1715,9 +1783,6 @@
         kv_heads,
         num_experts,
     )
-    out_sum, q_sum, k_sum, v_sum, misc_sum = dense_scatter(
-        (out_part, qkv_part), ((width,), (q_cols, k_cols, k_cols, 128))
-    )
     return (
         layer_out,
         grad_in,

time: 608 us -> 554 us (0.911); the launches traced: 597 us -> 553 us
  Pallas kernels: 554 us -> 508 us
    pallas_call x1 -> x0, Pallas kernels: 99.1 us -> none  [dense_scatter(): pl.pallas_call(functools.partial(dense_scatter_kernel, splits), out_shape...]
    pallas_call x1, Pallas kernels: 62.7 us -> 117 us  [attend_back(): pl.pallas_call(functools.partial(attend_back_kernel, q_heads, kv_heads, e...]
    pallas_call x1, Pallas kernels: 73 us -> 65.8 us  [expert_grads(): pl.pallas_call(expert_grads_kernel, out_shape=(jax.ShapeDtypeStruct((2, h...]
  transfers between devices with their start and end apart: 6 -> 6, of which waited for: 1 -> 1; matrix products, arithmetic and copies ran while one was open for 3% -> 3% of each run, Pallas kernels for 58% -> 67%
where the time goes in v4:
time: 554 us; the launch traced here: 553 us
  Pallas kernels  508 us (92%)
  between operations  15 us (3%)
  local copies, waits for them, and re-layouts  14.2 us (3%)
  other arithmetic  11.1 us (2%)
    pallas_call x1, Pallas kernels, attend_back(): pl.pallas_call(functools.partial(attend_back_kernel, q_heads, kv_heads, e...  117 us
    pallas_call x1, Pallas kernels, dense_gather(): pl.pallas_call(dense_gather_kernel, out_shape=jax.ShapeDtypeStruct((4, 8,...  85.6 us
    pallas_call x1, Pallas kernels, expert_back(): pl.pallas_call(expert_back_kernel, out_shape=(jax.ShapeDtypeStruct((8, 2,...  72.8 us
    pallas_call x1, Pallas kernels, expert_out(): pl.pallas_call(expert_out_kernel, out_shape=(jax.ShapeDtypeStruct((2, hal...  66.9 us
    pallas_call x1, Pallas kernels, expert_grads(): pl.pallas_call(expert_grads_kernel, out_shape=(jax.ShapeDtypeStruct((2, h...  65.8 us
    pallas_call x1, Pallas kernels, expert_in(): pl.pallas_call(expert_in_kernel, out_shape=(jax.ShapeDtypeStruct((8, 2, h...  65.5 us
    pallas_call x1, Pallas kernels, attend(): pl.pallas_call(functools.partial(attend_kernel, q_heads, kv_heads, expert...  34.6 us
  transfers between devices with their start and end apart: 6, of which 1 were waited for; matrix products, arithmetic and copies ran while one was open for 3% of the time, Pallas kernels for 67%

profile of v4, /device:TPU:0, one launch (start us, length us, event | category | flops | bytes accessed | tf_op | source)
XLA Modules:
  0.0 553.2 jit_solution(16962147416908960421)
XLA Ops:
  7.2 0.7 all-gather.4.cloned.1.call-update
  8.0 0.7 all-gather.6.cloned.1.call-update
  8.7 0.7 all-gather.8.cloned.1.call-update
  10.1 0.8 copy.38
  10.8 0.8 copy.39
  11.6 0.8 copy.37
  12.4 1.1 concatenate.9.own
  13.5 85.6 %dense_gather.1 = bf16[4,8,48,3712]{3,2,1,0:T(8,128)(2,1)} custom-call(bf16[48,3712]{1,0:T(8,128)(2,1)S(1)} %concatenate.9.own), custom_call_target="tpu_custom_call" | custom-call | tf_op jit(solution)/shard_map/dense_gather/pallas_call | solution.py:1201
  99.4 1.0 fusion.2
  100.4 1.0 pad_maximum_fusion
  101.4 1.0 convert_reduce_fusion.picked.picked_hbm
  102.4 1.2 fusion.1.bias.bias_hbm
  103.6 34.6 %attend.1 = (bf16[512,1664]{1,0:T(8,128)(2,1)}, f32[512,1536]{1,0:T(8,128)}, bf16[16,512,128]{2,1,0:T(8,128)(2,1)}, bf16[512,1536]{1,0:T(8,128)(2,1)}, f32[512,128]{1,0:T(8,128)}, /*index=5*/f32[512,128]{1,0:T(8,128)}) custom-call(bf16[512,1536]{1,0:T(8,128)(2,1)} %tokens_hbm.1, bf16[1536,3712]{1,0:T(8,128)(2,1)} %bitcast.20, ...), custom_call_target="tpu_custom_call" | custom-call | tf_op jit(solution)/shard_map/attend/pallas_call | solution.py:1417
  138.3 1.9 all-gather.6.cloned.1.call-done
  140.2 65.5 %expert_in.1 = (bf16[8,2,256,1664]{3,2,1,0:T(8,128)(2,1)}, bf16[8,2,256,2304]{3,2,1,0:T(8,128)(2,1)}) custom-call(bf16[2,256,1664]{2,1,0:T(8,128)(2,1)} %bitcast.30, bf16[1536,768]{1,0:T(8,128)(2,1)} %bitcast.26, bf16[1536,768]{1,0:T(8,128)(2,1)} %bitcast.28), custom_call_target="tpu_custom_call" | custom-call | tf_op jit(solution)/shard_map/expert_in/pallas_call | solution.py:533
  205.7 0.9 broadcast_in_dim.88.scales
  206.6 66.9 %expert_out.1 = (bf16[2,256,1536]{2,1,0:T(8,128)(2,1)}, f32[2,256,1536]{2,1,0:T(8,128)}, bf16[2,256,1536]{2,1,0:T(8,128)(2,1)}) custom-call(bf16[8,2,256,2304]{3,2,1,0:T(8,128)(2,1)} %get-tuple-element.36.gua_hbm, bf16[768,1536]{1,0:T(8,128)(2,1)} %bitcast.24, f32[2,256,1536]{2,1,0:T(8,128)} %bitcast.23, bf16[2,256,1536]{2,1,0:T(8,128)(2,1)} %bitcast.36, ...), custom_call_target="tpu_custom_call" | custom-call | tf_op jit(solution)/shard_map/expert_out/pallas_call | solution.py:783
  273.5 72.8 %expert_back.1 = (bf16[8,2,256,1536]{3,2,1,0:T(8,128)(2,1)}, bf16[8,2,256,1664]{3,2,1,0:T(8,128)(2,1)}, bf16[768,1536]{1,0:T(8,128)(2,1)}) custom-call(bf16[2,256,1536]{2,1,0:T(8,128)(2,1)} %get-tuple-element.39.own, bf16[8,2,256,1664]{3,2,1,0:T(8,128)(2,1)} %get-tuple-element.40.rows_hbm, bf16[8,2,256,2304]{3,2,1,0:T(8,128)(2,1)} %get-tuple-element.36.gua_hbm, ...), custom_call_target="tpu_custom_call" | custom-call | tf_op jit(solution)/shard_map/expert_back/pallas_call | solution.py:947
  346.5 65.8 %expert_grads.1 = (f32[2,256,1664]{2,1,0:T(8,128)}, bf16[1536,768]{1,0:T(8,128)(2,1)}, bf16[1536,768]{1,0:T(8,128)(2,1)}) custom-call(bf16[8,2,1,256,1664]{4,3,2,1,0:T(8,128)(2,1)} %bitcast.22, bf16[8,2,256,1664]{3,2,1,0:T(8,128)(2,1)} %get-tuple-element.40.rows_hbm, bf16[8,2,256,1536]{3,2,1,0:T(8,128)(2,1)} %get-tuple-element.42.dgu_hbm), custom_call_target="tpu_custom_call" | custom-call | tf_op jit(solution)/shard_map/expert_grads/pallas_call | solution.py:1083
  412.4 0.5 reduce-scatter.4.cloned.1.call-update
  413.0 116.7 %attend_back.1 = (f32[512,1536]{1,0:T(8,128)}, f32[48,1536]{1,0:T(8,128)}, f32[48,1536]{1,0:T(8,128)}, f32[48,256]{1,0:T(8,128)}, f32[48,256]{1,0:T(8,128)}, /*index=5*/f32[48,128]{1,0:T(8,128)}) custom-call(f32[512,1664]{1,0:T(8,128)} %bitcast.31, f32[512,1536]{1,0:T(8,128)} %bitcast.32, f32[512,1536]{1,0:T(8,128)} %get-tuple-element.37.resid_hbm, ...), custom_call_target="tpu_custom_call" | custom-call | tf_op jit(solution)/shard_map/attend_back/pallas_call | solution.py:1669
  529.7 1.4 copy.40
  531.1 1.5 slice_reduce_fusion
  532.6 2.2 convert_element_type.23
  534.8 2.2 convert_element_type.22
  537.0 2.3 convert_element_type.21
  539.3 2.7 copy.48
  542.0 1.7 copy.49
  543.6 0.7 copy.50
  544.4 0.6 copy.51
  545.0 0.6 copy.52
  545.6 0.7 copy.53
  (33 shorter events, 0.8 us)
Async XLA Ops:
  7.2 131.1 %all-gather.4.cloned.1.call-start = ((), (), s32[]{:S(2)}) async-start(), calls=%async_computation.3 | async-start | bytes 2949120 | tf_op jit(solution)/shard_map/all_gather | solution.py:1737
  7.9 132.3 %all-gather.6.cloned.1.call-start = ((), (), s32[]{:S(2)}) async-start(), calls=%async_computation.4 | async-start | bytes 2949120 | tf_op jit(solution)/shard_map/all_gather | solution.py:1738
  8.7 197.0 %all-gather.8.cloned.1.call-start = ((), (), s32[]{:S(2)}) async-start(), calls=%async_computation.5 | async-start | bytes 2949120 | tf_op jit(solution)/shard_map/all_gather | solution.py:1739
  9.4 523.2 %reduce-scatter.8.cloned.1.call-start = ((), (), s32[]{:S(2)}) async-start(), calls=%async_computation.8 | async-start | bytes 2949120 | tf_op jit(solution)/shard_map/reduce_scatter | solution.py:1764
  13.5 85.7 %copy-start.3 = (s32[512]{0:T(512)S(1)}, s32[512]{0:T(512)}, u32[]{:S(2)}) copy-start(s32[512]{0:T(512)} %param.18) | copy-start | bytes 6148
  13.5 87.9 %copy-start.6 = (s32[512,4]{0,1:T(4,128)S(1)}, s32[512,4]{0,1:T(4,128)}, u32[]{:S(2)}) copy-start(s32[512,4]{0,1:T(4,128)} %param.19) | copy-start | bytes 24580
  346.3 188.5 %reduce-scatter.6.cloned.1.call-start = ((), (), s32[]{:S(2)}) async-start(), calls=%async_computation.7 | async-start | bytes 2949120 | tf_op jit(solution)/shard_map/reduce_scatter | solution.py:1764
  412.4 124.6 %reduce-scatter.4.cloned.1.call-start = ((), (), s32[]{:S(2)}) async-start(), calls=%async_computation.6 | async-start | bytes 2949120 | tf_op jit(solution)/shard_map/reduce_scatter | solution.py:1764
  537.0 5.0 copy-start
  541.9 1.7 copy-start.2
  541.9 2.4 copy-start.5
  542.0 3.0 copy-start.4
  542.0 3.6 copy-start.1
Sparse Core Ops, SparseCore 0:
  9.6 78.9 all-gather.3
  90.2 49.9 all-gather.5
  141.8 48.7 all-gather.7
  346.4 45.8 reduce-scatter.7
  412.5 46.9 reduce-scatter.5
  461.7 69.2 reduce-scatter.3

commit v5 on v4

--- a/solution.py
+++ b/solution.py
@@ -477,41 +477,79 @@
                 copy.wait_send()
 
 
-def expert_in_kernel(own, gate_hbm, up_hbm, rows_out, gua_out, buf, gua, gate_w, up_w, send, recv, load, store_a, store_b):
-    width, hidden = gate_w.shape
+def line_peers():
+    line = lax.axis_index("dp")
+    return (
+        line,
+        line + 1 - 2 * lax.rem(line, 2),
+        line + 2 - 4 * lax.div(line, 2),
+        3 - line,
+    )
+
+
+def line_remote(src, dst, send_sem, recv_sem, peer):
+    return pltpu.make_async_remote_copy(
+        src_ref=src,
+        dst_ref=dst,
+        send_sem=send_sem,
+        recv_sem=recv_sem,
+        device_id={"dp": peer},
+        device_id_type=MESH,
+    )
+
+
+def full_barrier(plane, line):
+    barrier = pltpu.get_barrier_semaphore()
+    for peer in plane:
+        pl.semaphore_signal(barrier, inc=1, device_id={"exp": peer}, device_id_type=MESH)
+    for peer in line:
+        pl.semaphore_signal(barrier, inc=1, device_id={"dp": peer}, device_id_type=MESH)
+    pl.semaphore_wait(barrier, len(plane) + len(line))
+
+
+def expert_in_kernel(own, gate_hbm, down_own, rows_out, gate_out, down_out, buf, gate, gate_w, down_stage, send, recv, load, store_a, store_b, line_send, line_recv):
+    width = gate_w.shape[0]
     gather = Gather(own, buf, send, recv)
+    line = line_peers()
     loads = (
-        pltpu.make_async_copy(gate_hbm, gate_w, load.at[0]),
-        pltpu.make_async_copy(up_hbm, up_w, load.at[1]),
-        pltpu.make_async_copy(own.at[0], buf.at[gather.me, 0], load.at[2]),
-        pltpu.make_async_copy(own.at[1], buf.at[gather.me, 1], load.at[3]),
+        pltpu.make_async_copy(own.at[0], buf.at[gather.me, 0], load.at[0]),
+        pltpu.make_async_copy(own.at[1], buf.at[gather.me, 1], load.at[1]),
+        pltpu.make_async_copy(gate_hbm, gate_w, load.at[2]),
+        pltpu.make_async_copy(down_own, down_stage, load.at[3]),
     )
     for copy in loads:
         copy.start()
-    gather.begin()
+    full_barrier((gather.sib, gather.xn, gather.yn), line[1:])
+    for copy in gather.own_copies():
+        copy.start()
+
+    def down_copy(turn):
+        return line_remote(
+            down_own,
+            down_out.at[line[0]],
+            line_send.at[turn - 1],
+            line_recv.at[turn - 1],
+            line[turn],
+        )
+
+    for turn in (1, 2, 3):
+        down_copy(turn).start()
     for copy in loads:
         copy.wait()
+    down_store = pltpu.make_async_copy(down_stage, down_out.at[line[0]], load.at[4])
+    down_store.start()
 
     def row_store(slot, half, step):
         return pltpu.make_async_copy(buf.at[slot, half], rows_out.at[slot, half], store_a.at[step])
 
-    def gua_store(slot, half, step):
-        return pltpu.make_async_copy(gua.at[slot, half], gua_out.at[slot, half], store_b.at[step])
+    def gate_store(slot, half, step):
+        return pltpu.make_async_copy(gate.at[slot, half], gate_out.at[slot, half], store_b.at[step])
 
     def one(step, carry):
         slot, half = gather.arrive(step)
         row_store(slot, half, step).start()
-        rows = buf[slot, half, :, :width]
-        lanes = lax.broadcasted_iota(jnp.int32, (buf.shape[2], 128), 1)
-        tail = buf[slot, half, :, width:].astype(jnp.float32)
-        weight = jnp.sum(jnp.where(lanes == gather.me, tail, 0.0), axis=1, keepdims=True)
-        gate_val = nn_dot(rows, gate_w[...])
-        up_val = nn_dot(rows, up_w[...])
-        gua[slot, half, :, :hidden] = gate_val.astype(jnp.bfloat16)
-        gua[slot, half, :, hidden : 2 * hidden] = up_val.astype(jnp.bfloat16)
-        act_val = jnp.maximum(gate_val, 0.0) * up_val * weight
-        gua[slot, half, :, 2 * hidden :] = act_val.astype(jnp.bfloat16)
-        gua_store(slot, half, step).start()
+        gate[slot, half] = nn_dot(buf[slot, half, :, :width], gate_w[...]).astype(jnp.bfloat16)
+        gate_store(slot, half, step).start()
         return carry
 
     lax.fori_loop(0, 16, one, 0)
@@ -520,13 +558,22 @@
     def drain(step, carry):
         slot, half, _ = gather.place(step)
         row_store(slot, half, step).wait()
-        gua_store(slot, half, step).wait()
+        gate_store(slot, half, step).wait()
         return carry
 
     lax.fori_loop(0, 16, drain, 0)
-
-
-def expert_in(own, gate_w, up_w):
+    down_store.wait()
+    for turn in (1, 2, 3):
+        line_remote(
+            down_own,
+            down_out.at[line[turn]],
+            line_send.at[turn - 1],
+            line_recv.at[turn - 1],
+            line[turn],
+        ).wait()
+
+
+def expert_in(own, gate_w, down_own):
     _, half, columns = own.shape
     width, hidden = gate_w.shape
     bf = jnp.bfloat16
@@ -534,26 +581,29 @@
         expert_in_kernel,
         out_shape=(
             jax.ShapeDtypeStruct((8, 2, half, columns), bf),
-            jax.ShapeDtypeStruct((8, 2, half, 3 * hidden), bf),
+            jax.ShapeDtypeStruct((8, 2, half, hidden), bf),
+            jax.ShapeDtypeStruct((4, *down_own.shape), bf),
         ),
         in_specs=[ANY] * 3,
-        out_specs=(ANY, ANY),
+        out_specs=(ANY, ANY, ANY),
         scratch_shapes=[
             pltpu.VMEM((8, 2, half, columns), bf),
-            pltpu.VMEM((8, 2, half, 3 * hidden), bf),
+            pltpu.VMEM((8, 2, half, hidden), bf),
             pltpu.VMEM((width, hidden), bf),
-            pltpu.VMEM((width, hidden), bf),
+            pltpu.VMEM(down_own.shape, bf),
             pltpu.SemaphoreType.DMA((14,)),
             pltpu.SemaphoreType.DMA((8, 2)),
-            pltpu.SemaphoreType.DMA((4,)),
+            pltpu.SemaphoreType.DMA((5,)),
             pltpu.SemaphoreType.DMA((16,)),
             pltpu.SemaphoreType.DMA((16,)),
+            pltpu.SemaphoreType.DMA((3,)),
+            pltpu.SemaphoreType.DMA((3,)),
         ],
         compiler_params=pltpu.CompilerParams(
             collective_id=1, has_side_effects=True, vmem_limit_bytes=VMEM_BYTES
         ),
         name="expert_in",
-    )(own, gate_w, up_w)
+    )(own, gate_w, down_own)
 
 
 def row_chunk(rows):
@@ -592,10 +642,10 @@
 
     def place(self, step):
         quad = lax.div(step, 4)
-        far_x, far_y = step_place(step, 3 - quad)
-        odd = lax.rem(step, 2)
+        odd = lax.div(lax.rem(step, 4), 2)
+        far_x, far_y = step_place(odd, 3 - quad)
         third = lax.div(quad, 2) * (1 - lax.div(quad, 3))
-        other = 1 - lax.div(lax.rem(step, 4), 2)
+        other = 1 - lax.rem(step, 2)
         slot = (
             self.me
             + far_x * (self.xn - self.me)
@@ -648,27 +698,27 @@
 
         for way in (0, 1):
 
-            @pl.when(step == 2 + way)
+            @pl.when(step == 1 + 2 * way)
             def _():
                 self.side_wait(3, way)
                 add_rows(self.mine(3, way), (self.side.at[3, way],))
-                self.relay_copy(2 + way, way).start()
-
-            @pl.when(step == 6 + way)
+                self.relay_copy(1 + 2 * way, way).start()
+
+            @pl.when(step == 5 + 2 * way)
             def _():
                 self.side_wait(1 + way, way)
                 add_rows(self.mine(1 + way, way), (self.side.at[1 + way, way],))
-                self.final_copy(6 + way, way, way).start()
+                self.final_copy(5 + 2 * way, way, way).start()
 
     def forward(self):
         for way in (0, 1):
             self.side_wait(1 + way, 1 - way)
-            self.relay_copy(3 - way, 1 - way).wait_recv()
+            self.relay_copy(0, 1 - way).wait_recv()
             add_rows(
                 self.mine(1 + way, 1 - way),
                 (self.side.at[1 + way, 1 - way], self.relay.at[1 - way]),
             )
-            self.final_copy(10 + way, way, 1 - way).start()
+            self.final_copy(9 + 2 * way, way, 1 - way).start()
 
     def finish(self, write):
         parts, rows_all = self.relay.shape[1:3]
@@ -693,9 +743,9 @@
 
     def drain(self):
         for way in (0, 1):
-            self.relay_copy(2 + way, way).wait_send()
-            self.final_copy(6 + way, way, way).wait_send()
-            self.final_copy(10 + way, way, 1 - way).wait_send()
+            self.relay_copy(1 + 2 * way, way).wait_send()
+            self.final_copy(5 + 2 * way, way, way).wait_send()
+            self.final_copy(9 + 2 * way, way, 1 - way).wait_send()
 
         def one(step, carry):
             @pl.when(self.place(step)[2] == 1)
@@ -723,42 +773,76 @@
     ]
 
 
-def expert_out_kernel(gua_hbm, down_hbm, resid, targets, scales, layer, grad, grad_b, act, down_w, mine, away, load, *scratch):
-    hidden = down_w.shape[0]
+OUT_SLOTS = 4
+
+
+def expert_out_kernel(rows_hbm, gate_hbm, up_hbm, down_hbm, resid, targets, scales, layer, grad, grad_b, ua_out, rows, gate, ua, up_w, down_w, mine, away, load_w, load_rows, load_gate, store_ua, *scratch):
+    hidden, width = down_w.shape
     scatter = Scatter(
         lambda place, slot, half: mine.at[place, half],
         lambda place, slot, half: away.at[place, half],
         scratch,
     )
-    down_load = pltpu.make_async_copy(down_hbm, down_w, load.at[16])
-    down_load.start()
-
-    def act_load(step):
+    weights = (
+        pltpu.make_async_copy(up_hbm, up_w, load_w.at[0]),
+        pltpu.make_async_copy(down_hbm, down_w, load_w.at[1]),
+    )
+
+    def loads(step):
+        slot, half, _, _ = scatter.place(step)
+        spot = lax.rem(step, OUT_SLOTS)
+        return (
+            pltpu.make_async_copy(rows_hbm.at[slot, half], rows.at[spot], load_rows.at[step]),
+            pltpu.make_async_copy(gate_hbm.at[slot, half], gate.at[spot], load_gate.at[step]),
+        )
+
+    def ua_store(step):
         slot, half, _, _ = scatter.place(step)
         return pltpu.make_async_copy(
-            gua_hbm.at[slot, half, :, pl.ds(2 * hidden, hidden)], act.at[slot, half], load.at[step]
-        )
-
-    def fetch(step, carry):
-        act_load(step).start()
-        return carry
-
-    lax.fori_loop(0, 16, fetch, 0)
+            ua.at[lax.rem(step, OUT_SLOTS)], ua_out.at[slot, half], store_ua.at[step]
+        )
+
+    weights[0].start()
+    for step in (0, 1):
+        for copy in loads(step):
+            copy.start()
+    weights[1].start()
     plane_barrier(scatter.peers())
-    down_load.wait()
+    for copy in weights:
+        copy.wait()
 
     def one(step, carry):
-        slot, half, other, place = scatter.place(step)
-        act_load(step).wait()
-        partial = nn_dot(act[slot, half], down_w[...]).astype(jnp.bfloat16)
+        _, _, other, place = scatter.place(step)
+        spot = lax.rem(step, OUT_SLOTS)
+        for copy in loads(step):
+            copy.wait()
+
+        @pl.when(step < 14)
+        def _():
+            for copy in loads(step + 2):
+                copy.start()
+
+        @pl.when(step >= OUT_SLOTS)
+        def _():
+            ua_store(step - OUT_SLOTS).wait()
+
+        lanes = lax.broadcasted_iota(jnp.int32, (rows.shape[1], 128), 1)
+        tail = rows[spot, :, width:].astype(jnp.float32)
+        weight = jnp.sum(jnp.where(lanes == scatter.me, tail, 0.0), axis=1, keepdims=True)
+        up_val = nn_dot(rows[spot, :, :width], up_w[...])
+        act_val = jnp.maximum(gate[spot].astype(jnp.float32), 0.0) * up_val * weight
+        ua[spot, :, :hidden] = up_val.astype(jnp.bfloat16)
+        ua[spot, :, hidden:] = act_val.astype(jnp.bfloat16)
+        ua_store(step).start()
+        partial = nn_dot(ua[spot, :, hidden:], down_w[...]).astype(jnp.bfloat16)
 
         @pl.when(other == 1)
         def _():
-            away[place, half, 0] = partial
+            away[place, half_of(scatter, step), 0] = partial
 
         @pl.when(other == 0)
         def _():
-            mine[place, half, 0] = partial
+            mine[place, half_of(scatter, step), 0] = partial
 
         scatter.depart(step)
         return carry
@@ -776,25 +860,43 @@
     scatter.finish(write)
     scatter.drain()
 
-
-def expert_out(gua, down_w, resid, targets, scales):
-    half = gua.shape[2]
+    def drain(step, carry):
+        ua_store(step).wait()
+        return carry
+
+    lax.fori_loop(16 - OUT_SLOTS, 16, drain, 0)
+
+
+def half_of(scatter, step):
+    return scatter.place(step)[1]
+
+
+def expert_out(rows_all, gate_val, up_w, down_w, resid, targets, scales):
+    half, columns = rows_all.shape[2:]
     hidden, width = down_w.shape
+    bf = jnp.bfloat16
     return pl.pallas_call(
         expert_out_kernel,
         out_shape=(
-            jax.ShapeDtypeStruct((2, half, width), jnp.bfloat16),
+            jax.ShapeDtypeStruct((2, half, width), bf),
             jax.ShapeDtypeStruct((2, half, width), jnp.float32),
-            jax.ShapeDtypeStruct((2, half, width), jnp.bfloat16),
+            jax.ShapeDtypeStruct((2, half, width), bf),
+            jax.ShapeDtypeStruct((8, 2, half, 2 * hidden), bf),
         ),
-        in_specs=[ANY] * 2 + [VMEM] * 3,
-        out_specs=(VMEM,) * 3,
+        in_specs=[ANY] * 4 + [VMEM] * 3,
+        out_specs=(VMEM, VMEM, VMEM, ANY),
         scratch_shapes=[
-            pltpu.VMEM((8, 2, half, hidden), jnp.bfloat16),
-            pltpu.VMEM((hidden, width), jnp.bfloat16),
-            pltpu.VMEM((4, 2, 1, half, width), jnp.bfloat16),
-            pltpu.VMEM((4, 2, 1, half, width), jnp.bfloat16),
-            pltpu.SemaphoreType.DMA((17,)),
+            pltpu.VMEM((OUT_SLOTS, half, columns), bf),
+            pltpu.VMEM((OUT_SLOTS, half, hidden), bf),
+            pltpu.VMEM((OUT_SLOTS, half, 2 * hidden), bf),
+            pltpu.VMEM((width, hidden), bf),
+            pltpu.VMEM((hidden, width), bf),
+            pltpu.VMEM((4, 2, 1, half, width), bf),
+            pltpu.VMEM((4, 2, 1, half, width), bf),
+            pltpu.SemaphoreType.DMA((2,)),
+            pltpu.SemaphoreType.DMA((16,)),
+            pltpu.SemaphoreType.DMA((16,)),
+            pltpu.SemaphoreType.DMA((16,)),
         ]
         + scatter_scratch(1, half, width),
         compiler_params=pltpu.CompilerParams(
@@ -802,7 +904,9 @@
         ),
         name="expert_out",
     )(
-        gua,
+        rows_all,
+        gate_val,
+        up_w,
         down_w,
         resid.reshape(2, half, width),
         targets.reshape(2, half, width),
@@ -810,7 +914,7 @@
     )
 
 
-def expert_back_kernel(own, rows_hbm, gua_hbm, gate_hbm, up_hbm, down_hbm, dgu_out, part_out, down_out, buf, gua, tails, part, gate_w, up_w, down_w, down_acc, send, recv, load, load_gua, load_tail, store_b, store_c):
+def expert_back_kernel(own, rows_hbm, g_hbm, ua_hbm, gate_hbm, up_hbm, down_hbm, dgu_out, part_out, down_out, buf, gua, tails, part, gate_w, up_w, down_w, down_acc, send, recv, load, load_g, load_ua, load_tail, store_b, store_c):
     width, hidden = gate_w.shape
     gather = Gather(own, buf, send, recv)
     loads = (
@@ -827,7 +931,12 @@
         slot, half, _ = gather.place(step)
         return (
             pltpu.make_async_copy(
-                gua_hbm.at[slot, half], gua.at[slot, half], load_gua.at[step]
+                g_hbm.at[slot, half], gua.at[slot, half, :, pl.ds(0, hidden)], load_g.at[step]
+            ),
+            pltpu.make_async_copy(
+                ua_hbm.at[slot, half],
+                gua.at[slot, half, :, pl.ds(hidden, 2 * hidden)],
+                load_ua.at[step],
             ),
             pltpu.make_async_copy(
                 rows_hbm.at[slot, half, :, pl.ds(width, 128)], tails.at[slot, half], load_tail.at[step]
@@ -940,7 +1049,7 @@
 PART_SLOTS = 4
 
 
-def expert_back(own, rows_all, gua, gate_w, up_w, down_w):
+def expert_back(own, rows_all, gate_val, ua, gate_w, up_w, down_w):
     _, half, columns = rows_all.shape[1:]
     width, hidden = gate_w.shape
     bf = jnp.bfloat16
@@ -951,7 +1060,7 @@
             jax.ShapeDtypeStruct((8, 2, half, columns), bf),
             jax.ShapeDtypeStruct((hidden, width), bf),
         ),
-        in_specs=[ANY] * 6,
+        in_specs=[ANY] * 7,
         out_specs=(ANY, ANY, VMEM),
         scratch_shapes=[
             pltpu.VMEM((8, 2, half, width), bf),
@@ -966,12 +1075,12 @@
             pltpu.SemaphoreType.DMA((8, 2)),
             pltpu.SemaphoreType.DMA((5,)),
         ]
-        + [pltpu.SemaphoreType.DMA((16,))] * 4,
+        + [pltpu.SemaphoreType.DMA((16,))] * 5,
         compiler_params=pltpu.CompilerParams(
             collective_id=3, has_side_effects=True, vmem_limit_bytes=VMEM_BYTES
         ),
         name="expert_back",
-    )(own, rows_all, gua, gate_w, up_w, down_w)
+    )(own, rows_all, gate_val, ua, gate_w, up_w, down_w)
 
 
 def expert_grads_kernel(part_hbm, rows_hbm, dgu_hbm, out, gate_out, up_out, rows, dgu, acc, mine, load, block_load, *scratch):
@@ -1105,115 +1214,83 @@
     )(part.reshape(8, 2, 1, half, columns), rows_all, dgu)
 
 
-def line_peers():
-    line = lax.axis_index("dp")
-    return (
-        line,
-        line + 1 - 2 * lax.rem(line, 2),
-        line + 2 - 4 * lax.div(line, 2),
-        3 - line,
-    )
-
-
-def line_remote(src, dst, send_sem, recv_sem, peer):
-    return pltpu.make_async_remote_copy(
-        src_ref=src,
-        dst_ref=dst,
-        send_sem=send_sem,
-        recv_sem=recv_sem,
-        device_id={"dp": peer},
-        device_id_type=MESH,
-    )
-
-
-def full_barrier(plane, line):
-    barrier = pltpu.get_barrier_semaphore()
-    for peer in plane:
-        pl.semaphore_signal(barrier, inc=1, device_id={"exp": peer}, device_id_type=MESH)
-    for peer in line:
-        pl.semaphore_signal(barrier, inc=1, device_id={"dp": peer}, device_id_type=MESH)
-    pl.semaphore_wait(barrier, len(plane) + len(line))
-
-
-def dense_gather_kernel(own, everything, stage, send, recv, local):
-    me, sib, xn, yn = plane_peers()
-    diag = xn + yn - me
-    line = line_peers()
-    into = pltpu.make_async_copy(own, stage, local.at[0])
-    into.start()
-    full_barrier((sib, xn, yn), line[1:])
-    started = []
-
-    def put(src, slot, turn, peer):
-        copy = remote(
-            src, everything.at[line[turn], slot], send.at[len(started)], recv.at[line[turn], slot], peer
-        )
-        copy.start()
-        started.append(copy)
-
-    def pass_on(slot, turn, peer):
-        put(everything.at[line[turn], slot], slot, turn, peer)
-
-    def wait(slot, turn):
-        ref = everything.at[line[turn], slot]
-        remote(ref, ref, send.at[0], recv.at[line[turn], slot], sib).wait_recv()
-
-    put(own, me, 0, xn)
-    put(own, me, 0, yn)
-    for turn in (1, 2, 3):
-        copy = line_remote(
-            own, everything.at[line[0], me], send.at[len(started)], recv.at[line[0], me], line[turn]
-        )
-        copy.start()
-        started.append(copy)
-    put(own, me, 0, sib)
-    into.wait()
-    out = pltpu.make_async_copy(stage, everything.at[line[0], me], local.at[1])
-    out.start()
-    for turn in (0, 1, 2, 3):
+class DenseGather:
+    def __init__(self, own, everything, send, recv, local):
+        self.own, self.everything, self.send, self.recv = own, everything, send, recv
+        self.me, self.sib, self.xn, self.yn = plane_peers()
+        self.diag = self.xn + self.yn - self.me
+        self.line = line_peers()
+        self.home = pltpu.make_async_copy(own, everything.at[self.line[0], self.me], local)
+        self.started = []
+
+    def copy(self, index, own, slot, turn, peer, make):
+        target = self.everything.at[self.line[turn], slot]
+        return make(
+            self.own if own else target,
+            target,
+            self.send.at[index],
+            self.recv.at[self.line[turn], slot],
+            peer,
+        )
+
+    def put(self, own, slot, turn, peer, make=remote):
+        what = (len(self.started), own, slot, turn, peer, make)
+        self.started.append(what)
+        self.copy(*what).start()
+
+    def pass_on(self, slot, turn, peer):
+        self.put(False, slot, turn, peer)
+
+    def wait(self, slot, turn):
+        ref = self.everything.at[self.line[turn], slot]
+        remote(ref, ref, self.send.at[0], self.recv.at[self.line[turn], slot], self.sib).wait_recv()
+
+    def start_line(self):
+        for turn in (1, 2, 3):
+            self.put(True, self.me, 0, self.line[turn], line_remote)
+
+    def start_plane(self):
+        for peer in (self.xn, self.yn, self.sib):
+            self.put(True, self.me, 0, peer)
+
+    def turn(self, turn):
         if turn > 0:
-            wait(me, turn)
-            for peer in (xn, yn, sib):
-                pass_on(me, turn, peer)
-        wait(xn, turn)
+            self.wait(self.me, turn)
+            for peer in (self.xn, self.yn, self.sib):
+                self.pass_on(self.me, turn, peer)
+        self.wait(self.xn, turn)
         if turn % 2 == 0:
-            pass_on(xn, turn, yn)
-        pass_on(xn, turn, sib)
-        wait(yn, turn)
+            self.pass_on(self.xn, turn, self.yn)
+        self.pass_on(self.xn, turn, self.sib)
+        self.wait(self.yn, turn)
         if turn % 2 == 1:
-            pass_on(yn, turn, xn)
-        pass_on(yn, turn, sib)
+            self.pass_on(self.yn, turn, self.xn)
+        self.pass_on(self.yn, turn, self.sib)
         if turn > 0:
-            wait(diag, turn - 1)
-            pass_on(diag, turn - 1, sib)
-    wait(diag, 3)
-    pass_on(diag, 3, sib)
-    for turn in (0, 1, 2, 3):
-        for slot in (sib, xn + sib - me, yn + sib - me, diag + sib - me):
-            wait(slot, turn)
-    out.wait()
-    for copy in started:
-        copy.wait_send()
-
-
-def dense_gather(own):
-    rows, columns = own.shape
-    return pl.pallas_call(
-        dense_gather_kernel,
-        out_shape=jax.ShapeDtypeStruct((4, 8, rows, columns), own.dtype),
-        in_specs=[ANY],
-        out_specs=ANY,
-        scratch_shapes=[
-            pltpu.VMEM((rows, columns), own.dtype),
-            pltpu.SemaphoreType.DMA((32,)),
-            pltpu.SemaphoreType.DMA((4, 8)),
-            pltpu.SemaphoreType.DMA((2,)),
-        ],
-        compiler_params=pltpu.CompilerParams(
-            collective_id=5, has_side_effects=True, vmem_limit_bytes=48 * 2**20
-        ),
-        name="dense_gather",
-    )(own).reshape(32 * rows, columns)
+            self.far(turn - 1)
+
+    def far(self, turn):
+        self.wait(self.diag, turn)
+        self.pass_on(self.diag, turn, self.sib)
+
+    def arrived(self):
+        for turn in (0, 1, 2, 3):
+            for slot in (self.me, self.xn, self.yn, self.diag):
+                self.wait(slot + self.sib - self.me, turn)
+        self.home.wait()
+
+    def finish(self):
+        for what in self.started:
+            self.copy(*what).wait_send()
+
+
+def gather_scratch(rows, columns):
+    return [
+        pltpu.VMEM((4, 8, rows, columns), jnp.bfloat16),
+        pltpu.SemaphoreType.DMA((32,)),
+        pltpu.SemaphoreType.DMA((4, 8)),
+        pltpu.SemaphoreType.DMA((2,)),
+    ]
 
 
 class LineScatter:
@@ -1308,9 +1385,9 @@
 
 
 def gain_rows(misc, out):
-    for index in range(misc.shape[0] // 128):
+    for index in range(out.shape[1] // 128):
         rows = pl.ds(index * 128, 128)
-        out[:, rows] = jnp.transpose(misc[rows, :].astype(jnp.float32))
+        out[:, rows] = jnp.transpose(misc(rows).astype(jnp.float32))
 
 
 def inverse_rms(values):
@@ -1333,21 +1410,38 @@
 TILE = 256
 
 
-def attend_kernel(q_heads, kv_heads, experts, tokens, dense_hbm, cosine, sine, bias, picked, rows_out, resid, heads, mixed, lse, prob, qkv_w, rest_w, gains, hidden, load):
+def attend_kernel(q_heads, kv_heads, experts, tokens, qkv_own, out_own, cosine, sine, bias, picked, rows_out, resid, heads, mixed, lse, prob, qkv_hbm, out_hbm, gains, hidden, *scratch):
     num_rows, width = tokens.shape
     group = q_heads // kv_heads
-    q_cols = q_heads * HD
-    loads = (
-        pltpu.make_async_copy(dense_hbm.at[:, pl.ds(0, qkv_w.shape[1])], qkv_w, load.at[0]),
-        pltpu.make_async_copy(
-            dense_hbm.at[:, pl.ds(qkv_w.shape[1], rest_w.shape[1])], rest_w, load.at[1]
-        ),
-    )
-    for copy in loads:
-        copy.start()
-    loads[1].wait()
-    misc = rest_w.at[:, pl.ds(width, 128)]
-    gain_rows(misc, gains)
+    qkv_cols = (q_heads + 2 * kv_heads) * HD
+    qkv_w, out_w = scratch[0], scratch[4]
+    first = DenseGather(qkv_own, qkv_w, scratch[1], scratch[2], scratch[3].at[0])
+    second = DenseGather(out_own, out_w, scratch[5], scratch[6], scratch[7].at[0])
+    stores = (
+        pltpu.make_async_copy(qkv_w, qkv_hbm, scratch[3].at[1]),
+        pltpu.make_async_copy(out_w, out_hbm, scratch[7].at[1]),
+    )
+    for gather in (first, second):
+        gather.home.start()
+    full_barrier((first.sib, first.xn, first.yn), first.line[1:])
+    first.start_line()
+    first.start_plane()
+    second.start_line()
+    for turn in (0, 1, 2, 3):
+        first.turn(turn)
+    first.far(3)
+    second.start_plane()
+    first.arrived()
+    stores[0].start()
+    second.turn(0)
+
+    def flat(ref, cols):
+        return ref[:, :, :, cols].reshape(-1, cols.size)
+
+    misc = flat(qkv_w, pl.ds(qkv_cols, 128))
+    for index in range(width // 128):
+        rows = slice(index * 128, (index + 1) * 128)
+        gains[:, rows] = jnp.transpose(misc[rows, :].astype(jnp.float32))
 
     def norm_one(rows):
         value = tokens[rows, :].astype(jnp.float32)
@@ -1355,11 +1449,10 @@
         hidden[rows, :] = (normed * gains[experts : experts + 1, :]).astype(jnp.bfloat16)
 
     row_loop(num_rows, ROW_CHUNK, norm_one)
-    loads[0].wait()
 
     def project(index, carry):
         cols = pl.ds(pl.multiple_of(index * TILE, TILE), TILE)
-        raw = nn_dot(hidden[...], qkv_w[:, cols])
+        raw = nn_dot(hidden[...], flat(qkv_w, cols))
         turned = index < (q_heads + kv_heads) // 2
         cos_now = jnp.where(turned, cosine[...], 1.0)
         sin_now = jnp.where(turned, sine[...], 0.0)
@@ -1369,6 +1462,7 @@
         return carry
 
     lax.fori_loop(0, (q_heads + 2 * kv_heads) // 2, project, 0)
+    second.turn(1)
     lse[...] = jnp.zeros_like(lse)
 
     def head_step(head, carry):
@@ -1385,12 +1479,25 @@
             mixed[rows, cols] = (value / total).astype(jnp.bfloat16)
             lanes = lax.broadcasted_iota(jnp.int32, (keys - first, 128), 1)
             lse[rows, :] = jnp.where(lanes == head, top + jnp.log(total), lse[rows, :])
+
+        @pl.when(head == q_heads // 3)
+        def _():
+            second.turn(2)
+
+        @pl.when(head == 2 * q_heads // 3)
+        def _():
+            second.turn(3)
+
         return carry
 
     lax.fori_loop(0, q_heads, head_step, 0)
 
+    second.far(3)
+    second.arrived()
+    stores[1].start()
+
     def out_tile(cols):
-        resid[:, cols] = tokens[:, cols].astype(jnp.float32) + nn_dot(mixed[...], rest_w[:, cols])
+        resid[:, cols] = tokens[:, cols].astype(jnp.float32) + nn_dot(mixed[...], flat(out_w, cols))
 
     tile_loop(width, TILE, out_tile)
 
@@ -1400,7 +1507,7 @@
         rows_out[rows, :width] = (normed * gains[experts + 1 : experts + 2, :]).astype(jnp.bfloat16)
 
     row_loop(num_rows, ROW_CHUNK, norm_two)
-    logits = nn_dot(rows_out[:, :width], misc[...])
+    logits = nn_dot(rows_out[:, :width], flat(qkv_w, pl.ds(qkv_cols, 128)))
     lanes = lax.broadcasted_iota(jnp.int32, logits.shape, 1)
     logits = jnp.where(lanes < experts, logits, NEG_BIG)
     weight = jnp.exp(logits - jnp.max(logits, axis=1, keepdims=True))
@@ -1408,9 +1515,12 @@
     prob[...] = value
     chosen = value * picked[...]
     rows_out[:, width:] = (chosen / jnp.sum(chosen, axis=1, keepdims=True)).astype(jnp.bfloat16)
-
-
-def attend(tokens, dense_w, cosine, sine, bias, picked, q_heads, kv_heads, experts):
+    for gather, store in zip((first, second), stores):
+        store.wait()
+        gather.finish()
+
+
+def attend(tokens, qkv_own, out_own, cosine, sine, bias, picked, q_heads, kv_heads, experts):
     num_rows, width = tokens.shape
     bf = jnp.bfloat16
     all_heads = q_heads + 2 * kv_heads
@@ -1423,22 +1533,25 @@
             jax.ShapeDtypeStruct((num_rows, q_heads * HD), bf),
             jax.ShapeDtypeStruct((num_rows, 128), jnp.float32),
             jax.ShapeDtypeStruct((num_rows, 128), jnp.float32),
+            jax.ShapeDtypeStruct((4, 8, *qkv_own.shape), bf),
+            jax.ShapeDtypeStruct((4, 8, *out_own.shape), bf),
         ),
-        in_specs=[VMEM, ANY] + [VMEM] * 4,
-        out_specs=(VMEM,) * 6,
+        in_specs=[VMEM, ANY, ANY] + [VMEM] * 4,
+        out_specs=(VMEM,) * 6 + (ANY, ANY),
         scratch_shapes=[
-            pltpu.VMEM((width, all_heads * HD), bf),
-            pltpu.VMEM((q_heads * HD, width + 128), bf),
             pltpu.VMEM((128, width), jnp.float32),
             pltpu.VMEM((num_rows, width), bf),
-            pltpu.SemaphoreType.DMA((2,)),
-        ],
-        compiler_params=pltpu.CompilerParams(vmem_limit_bytes=VMEM_BYTES),
+        ]
+        + gather_scratch(*qkv_own.shape)
+        + gather_scratch(*out_own.shape),
+        compiler_params=pltpu.CompilerParams(
+            collective_id=5, has_side_effects=True, vmem_limit_bytes=VMEM_BYTES
+        ),
         name="attend",
-    )(tokens, dense_w, cosine, sine, bias, picked)
-
-
-def attend_back_kernel(q_heads, kv_heads, experts, back_hbm, grad_hbm, resid_hbm, rows_hbm, prob_hbm, picked_hbm, dense_hbm, mixed_hbm, heads_hbm, lse_hbm, bias_hbm, cos_hbm, sin_hbm, tokens_hbm, grad_in, out_sum, q_sum, k_sum, v_sum, misc_sum, back, grad, resid, hidden_two, prob, picked, dense, mixed, heads, lse, bias, cosine, sine, tokens, gains, gain_sums, grad_logit, grad_proj, grad_mixed, grad_qkv, grad_kv, hidden, load, *scratch):
+    )(tokens, qkv_own, out_own, cosine, sine, bias, picked)
+
+
+def attend_back_kernel(q_heads, kv_heads, experts, back_hbm, grad_hbm, resid_hbm, rows_hbm, prob_hbm, picked_hbm, qkv_hbm, out_hbm, mixed_hbm, heads_hbm, lse_hbm, bias_hbm, cos_hbm, sin_hbm, tokens_hbm, grad_in, out_sum, q_sum, k_sum, v_sum, misc_sum, back, grad, resid, hidden_two, prob, picked, qkv_w, out_w, mixed, heads, lse, bias, cosine, sine, tokens, gains, gain_sums, grad_logit, grad_proj, grad_mixed, grad_qkv, grad_kv, hidden, load, *scratch):
     num_rows, width = tokens.shape
     group = q_heads // kv_heads
     q_cols = q_heads * HD
@@ -1457,10 +1570,11 @@
         (prob_hbm, prob),
         (picked_hbm, picked),
         (back_hbm, back),
-        (dense_hbm, dense),
+        (qkv_hbm, qkv_w),
         (resid_hbm, resid),
         (grad_hbm, grad),
         (rows_hbm, hidden_two),
+        (out_hbm, out_w),
         (mixed_hbm, mixed),
         (heads_hbm, heads),
         (lse_hbm, lse),
@@ -1491,8 +1605,8 @@
 
     row_loop(num_rows, 64, router_rows)
     loads[3].wait()
-    misc = dense.at[:, pl.ds(qkv_cols + width, 128)]
-    gain_rows(misc, gains)
+    misc = qkv_w.at[:, pl.ds(qkv_cols, 128)]
+    gain_rows(lambda rows: misc[rows, :], gains)
     lanes = lax.broadcasted_iota(jnp.int32, (TILE, 128), 1)
 
     def hidden_tile(cols):
@@ -1537,7 +1651,7 @@
 
     def mixed_tile(cols):
         grad_mixed[:, cols] = nt_dot(
-            grad_proj[...], dense[cols, pl.ds(qkv_cols, width)]
+            grad_proj[...], out_w[cols, :]
         ).astype(bf)
 
     tile_loop(q_cols, TILE, mixed_tile)
@@ -1606,7 +1720,7 @@
     near_scatter.turn()
 
     def hidden_back_tile(cols):
-        back[:, cols] = nt_dot(grad_qkv[...], dense[cols, pl.ds(0, qkv_cols)])
+        back[:, cols] = nt_dot(grad_qkv[...], qkv_w[cols, pl.ds(0, qkv_cols)])
 
     tile_loop(width, TILE, hidden_back_tile)
     rest_scatter.forward()
@@ -1653,10 +1767,10 @@
     store.wait()
 
 
-def attend_back(back, grad, resid, rows_own, prob, picked, dense_w, mixed, heads, lse, bias, cosine, sine, tokens, q_heads, kv_heads, experts):
+def attend_back(back, grad, resid, rows_own, prob, picked, qkv_w, out_w, mixed, heads, lse, bias, cosine, sine, tokens, q_heads, kv_heads, experts):
     num_rows, width = tokens.shape
     bf = jnp.bfloat16
-    arrays = (back, grad, resid, rows_own, prob, picked, dense_w, mixed, heads, lse, bias, cosine, sine, tokens)
+    arrays = (back, grad, resid, rows_own, prob, picked, qkv_w, out_w, mixed, heads, lse, bias, cosine, sine, tokens)
     k_cols = kv_heads * HD
     q_cols = q_heads * HD
     qkv_cols = q_cols + 2 * k_cols
@@ -1720,12 +1834,11 @@
     num_heads = q_cols // HD
     kv_heads = k_cols // HD
     pad_cols = 128 - 2 - num_experts
-    dense_own = jnp.concatenate(
+    qkv_own = jnp.concatenate(
         [
             w_query,
             w_key,
             w_value,
-            w_out,
             w_router,
             gain_attn[:, None],
             gain_moe[:, None],
@@ -1733,10 +1846,8 @@
         ],
         axis=1,
     )
-    dense_w = dense_gather(dense_own)
     gate_w = lax.all_gather(w_gate, "dp", axis=1, tiled=True)[0]
     up_w = lax.all_gather(w_up, "dp", axis=1, tiled=True)[0]
-    down_w = lax.all_gather(w_down, "dp", axis=1, tiled=True)[0]
     tok_pos = positions(segments)
     bias = jnp.where(key_mask(segments), 0.0, NEG_BIG)
     freq = THETA ** (-2.0 * jnp.arange(HD // 2, dtype=jnp.float32) / HD)
@@ -1746,19 +1857,26 @@
     sine = jnp.concatenate([-sine_part, sine_part], axis=1)
     lane_ids = jnp.arange(128, dtype=jnp.int32)
     picked = jnp.sum((routes[:, :, None] == lane_ids[None, None, :]).astype(jnp.float32), axis=1)
-    rows_own, resid_mid, heads, mixed, lse, prob = attend(
-        tokens, dense_w, cosine, sine, bias, picked, num_heads, kv_heads, num_experts
-    )
-    rows_all, gua = expert_in(rows_own.reshape(2, half, width + 128), gate_w, up_w)
+    rows_own, resid_mid, heads, mixed, lse, prob, qkv_w, out_w = attend(
+        tokens, qkv_own, w_out, cosine, sine, bias, picked, num_heads, kv_heads, num_experts
+    )
+    rows_all, gate_val, down_w = expert_in(
+        rows_own.reshape(2, half, width + 128), gate_w, w_down[0]
+    )
+    down_w = down_w.reshape(-1, width)
     total_rows = num_rows * lax.axis_size(("dp", "exp"))
     global_row = lax.axis_index(("dp", "exp")) * num_rows + jnp.arange(num_rows, dtype=jnp.int32)
     loss_scale = total_rows / valid_count[0].astype(jnp.float32)
     scales = jnp.broadcast_to(
         jnp.where(global_row < valid_count[0], loss_scale, 0.0)[:, None], (num_rows, 128)
     )
-    layer_out, grad_out, grad_out_b = expert_out(gua, down_w, resid_mid, targets, scales)
+    layer_out, grad_out, grad_out_b, ua = expert_out(
+        rows_all, gate_val, up_w, down_w, resid_mid, targets, scales
+    )
     layer_out = layer_out.reshape(num_rows, width)
-    dgu, part, down_part = expert_back(grad_out_b, rows_all, gua, gate_w, up_w, down_w)
+    dgu, part, down_part = expert_back(
+        grad_out_b, rows_all, gate_val, ua, gate_w, up_w, down_w
+    )
     back, gate_part, up_part = expert_grads(part, rows_all, dgu)
     expert_sums = tuple(
         lax.psum_scatter(grad[None], "dp", scatter_dimension=1, tiled=True).astype(jnp.float32)
@@ -1771,7 +1889,8 @@
         rows_own,
         prob,
         picked,
-        dense_w,
+        qkv_w.reshape(width, -1),
+        out_w.reshape(q_cols, width),
         mixed,
         heads,
         lse,

time: 554 us -> 557 us (level)
    pallas_call x1 -> x0, Pallas kernels: 85.6 us -> none  [dense_gather(): pl.pallas_call(dense_gather_kernel, out_shape=jax.ShapeDtypeStruct((4, 8,...]
    pallas_call x1, Pallas kernels: 34.6 us -> 109 us  [attend(): pl.pallas_call(functools.partial(attend_kernel, q_heads, kv_heads, expert...]
  transfers between devices with their start and end apart: 6 -> 5, of which waited for: 1 -> 0; matrix products, arithmetic and copies ran while one was open for 3% -> 3% of each run, Pallas kernels for 67% -> 66%
where the time goes in v5:
time: 557 us; the launch traced here: 556 us
  Pallas kernels  511 us (92%)
  local copies, waits for them, and re-layouts  14.8 us (3%)
  between operations  14.6 us (3%)
  other arithmetic  13.2 us (2%)
    pallas_call x1, Pallas kernels, attend_back(): pl.pallas_call(functools.partial(attend_back_kernel, q_heads, kv_heads, e...  120 us
    pallas_call x1, Pallas kernels, attend(): pl.pallas_call(functools.partial(attend_kernel, q_heads, kv_heads, expert...  109 us
    pallas_call x1, Pallas kernels, expert_back(): pl.pallas_call(expert_back_kernel, out_shape=(jax.ShapeDtypeStruct((8, 2,...  73.4 us
    pallas_call x1, Pallas kernels, expert_out(): pl.pallas_call(expert_out_kernel, out_shape=(jax.ShapeDtypeStruct((2, hal...  71.5 us
    pallas_call x1, Pallas kernels, expert_in(): pl.pallas_call(expert_in_kernel, out_shape=(jax.ShapeDtypeStruct((8, 2, h...  69.8 us
    pallas_call x1, Pallas kernels, expert_grads(): pl.pallas_call(expert_grads_kernel, out_shape=(jax.ShapeDtypeStruct((2, h...  67.8 us
  transfers between devices with their start and end apart: 5, of which 0 were waited for; matrix products, arithmetic and copies ran while one was open for 3% of the time, Pallas kernels for 66%

profile of v5, /device:TPU:0, one launch (start us, length us, event | category | flops | bytes accessed | tf_op | source)
XLA Modules:
  0.0 556.4 jit_solution(513185185575422140)
XLA Ops:
  7.2 0.7 all-gather.3.cloned.1.call-update
  8.0 0.7 all-gather.5.cloned.1.call-update
  9.4 0.8 copy.38
  10.1 0.8 copy.39
  10.9 0.8 copy.37
  11.7 1.7 concatenate.9.qkv_own
  13.4 0.8 select_reduce_fusion.1
  14.2 0.8 select_reduce_fusion
  15.0 0.7 select_convert_fusion
  15.7 1.0 fusion.2
  16.7 1.0 pad_maximum_fusion
  17.7 1.0 convert_reduce_fusion.picked.picked_hbm
  18.7 1.2 fusion.1.bias.bias_hbm
  19.9 109.3 %attend.1 = (bf16[512,1664]{1,0:T(8,128)(2,1)}, f32[512,1536]{1,0:T(8,128)}, bf16[16,512,128]{2,1,0:T(8,128)(2,1)}, bf16[512,1536]{1,0:T(8,128)(2,1)}, f32[512,1...) custom-call(bf16[512,1536]{1,0:T(8,128)(2,1)} %tokens_hbm.1, ...), custom_call_target="tpu_custom_call" | custom-call | tf_op jit(solution)/shard_map/attend/pallas_call | solution.py:1527
  129.3 69.8 %expert_in.1 = (bf16[8,2,256,1664]{3,2,1,0:T(8,128)(2,1)}, bf16[8,2,256,768]{3,2,1,0:T(8,128)(2,1)}, bf16[4,192,1536]{2,1,0:T(8,128)(2,1)}) custom-call(bf16[2,256,1664]{2,1,0:T(8,128)(2,1)} %bitcast.30, bf16[1536,768]{1,0:T(8,128)(2,1)} %bitcast.28, bf16[192,1536]{1,0:T(8,128)(2,1)} %bitcast.40), custom_call_target="tpu_custom_call" | custom-call | tf_op jit(solution)/shard_map/expert_in/pallas_call | solution.py:580
  199.2 0.8 broadcast_in_dim.88.scales
  200.0 71.5 %expert_out.1 = (bf16[2,256,1536]{2,1,0:T(8,128)(2,1)}, f32[2,256,1536]{2,1,0:T(8,128)}, bf16[2,256,1536]{2,1,0:T(8,128)(2,1)}, bf16[8,2,256,1536]{3,2,1,0:T(8,128)(2,1)}) custom-call(bf16[8,2,256,1664]{3,2,1,0:T(8,128)(2,1)} %get-tuple-element.40.rows_hbm, bf16[8,2,256,768]{3,2,1,0:T(8,128)(2,1)} %get-tuple-element.41.gate_hbm.g_hbm, ...), custom_call_target="tpu_custom_call" | custom-call | tf_op jit(solution)/shard_map/expert_out/pallas_call | solution.py:878
  271.5 73.4 %expert_back.1 = (bf16[8,2,256,1536]{3,2,1,0:T(8,128)(2,1)}, bf16[8,2,256,1664]{3,2,1,0:T(8,128)(2,1)}, bf16[768,1536]{1,0:T(8,128)(2,1)}) custom-call(bf16[2,256,1536]{2,1,0:T(8,128)(2,1)} %get-tuple-element.45.own, bf16[8,2,256,1664]{3,2,1,0:T(8,128)(2,1)} %get-tuple-element.40.rows_hbm, bf16[8,2,256,768]{3,2,1,0:T(8,128)(2,1)} %get-tuple-element.41.gate_hbm.g_hbm, ...), custom_call_target="tpu_custom_call" | custom-call | tf_op jit(solution)/shard_map/expert_back/pallas_call | solution.py:1056
  345.1 67.8 %expert_grads.1 = (f32[2,256,1664]{2,1,0:T(8,128)}, bf16[1536,768]{1,0:T(8,128)(2,1)}, bf16[1536,768]{1,0:T(8,128)(2,1)}) custom-call(bf16[8,2,1,256,1664]{4,3,2,1,0:T(8,128)(2,1)} %bitcast.22, bf16[8,2,256,1664]{3,2,1,0:T(8,128)(2,1)} %get-tuple-element.40.rows_hbm, bf16[8,2,256,1536]{3,2,1,0:T(8,128)(2,1)} %get-tuple-element.48.dgu_hbm), custom_call_target="tpu_custom_call" | custom-call | tf_op jit(solution)/shard_map/expert_grads/pallas_call | solution.py:1192
  413.1 0.5 reduce-scatter.4.cloned.1.call-update
  413.6 119.6 %attend_back.1 = (f32[512,1536]{1,0:T(8,128)}, f32[48,1536]{1,0:T(8,128)}, f32[48,1536]{1,0:T(8,128)}, f32[48,256]{1,0:T(8,128)}, f32[48,256]{1,0:T(8,128)}, /*index=5*/f32[48,128]{1,0:T(8,128)}) custom-call(f32[512,1664]{1,0:T(8,128)} %bitcast.33, f32[512,1536]{1,0:T(8,128)} %bitcast.34, f32[512,1536]{1,0:T(8,128)} %get-tuple-element.43.resid_hbm, ...), custom_call_target="tpu_custom_call" | custom-call | tf_op jit(solution)/shard_map/attend_back/pallas_call | solution.py:1783
  533.2 1.4 copy.40
  534.6 1.5 slice_reduce_fusion
  536.1 2.2 convert_element_type.23
  538.3 2.2 convert_element_type.22
  540.5 2.3 convert_element_type.21
  542.8 2.7 copy.48
  545.5 1.7 copy.49
  547.2 0.7 copy.50
  547.9 0.6 copy.51
  548.5 0.6 copy.52
  549.1 0.7 copy.53
  (29 shorter events, 0.5 us)
Async XLA Ops:
  7.2 11.6 %copy-start.3 = (s32[512]{0:T(512)S(1)}, s32[512]{0:T(512)}, u32[]{:S(2)}) copy-start(s32[512]{0:T(512)} %param.18) | copy-start | bytes 6148
  7.2 10.5 %copy-start.6 = (s32[512,4]{0,1:T(4,128)S(1)}, s32[512,4]{0,1:T(4,128)}, u32[]{:S(2)}) copy-start(s32[512,4]{0,1:T(4,128)} %param.19) | copy-start | bytes 24580
  7.2 122.1 %all-gather.3.cloned.1.call-start = ((), (), s32[]{:S(2)}) async-start(), calls=%async_computation.3 | async-start | bytes 2949120 | tf_op jit(solution)/shard_map/all_gather | solution.py:1849
  7.9 191.2 %all-gather.5.cloned.1.call-start = ((), (), s32[]{:S(2)}) async-start(), calls=%async_computation.4 | async-start | bytes 2949120 | tf_op jit(solution)/shard_map/all_gather | solution.py:1850
  8.7 527.5 %reduce-scatter.8.cloned.1.call-start = ((), (), s32[]{:S(2)}) async-start(), calls=%async_computation.7 | async-start | bytes 2949120 | tf_op jit(solution)/shard_map/reduce_scatter | solution.py:1882
  344.9 193.4 %reduce-scatter.6.cloned.1.call-start = ((), (), s32[]{:S(2)}) async-start(), calls=%async_computation.6 | async-start | bytes 2949120 | tf_op jit(solution)/shard_map/reduce_scatter | solution.py:1882
  413.0 127.5 %reduce-scatter.4.cloned.1.call-start = ((), (), s32[]{:S(2)}) async-start(), calls=%async_computation.5 | async-start | bytes 2949120 | tf_op jit(solution)/shard_map/reduce_scatter | solution.py:1882
  540.5 5.0 copy-start
  545.5 1.7 copy-start.2
  545.5 2.4 copy-start.5
  545.5 3.0 copy-start.4
  545.5 3.6 copy-start.1
Sparse Core Ops, SparseCore 0:
  9.6 83.2 all-gather.2
  94.4 51.1 all-gather.4
  345.0 46.7 reduce-scatter.7
  413.1 46.7 reduce-scatter.5
  462.1 71.6 reduce-scatter.3

commit v6 on v5

--- a/solution.py
+++ b/solution.py
@@ -845,10 +845,14 @@
             mine[place, half_of(scatter, step), 0] = partial
 
         scatter.depart(step)
+
+        @pl.when(step == 12)
+        def _():
+            scatter.forward()
+
         return carry
 
     lax.fori_loop(0, 16, one, 0)
-    scatter.forward()
 
     def write(half, part, rows, total):
         value = resid[half, rows, :] + total
@@ -914,33 +918,41 @@
     )
 
 
-def expert_back_kernel(own, rows_hbm, g_hbm, ua_hbm, gate_hbm, up_hbm, down_hbm, dgu_out, part_out, down_out, buf, gua, tails, part, gate_w, up_w, down_w, down_acc, send, recv, load, load_g, load_ua, load_tail, store_b, store_c):
-    width, hidden = gate_w.shape
+BACK_SLOTS = 4
+
+
+def expert_back_kernel(own, rows_hbm, g_hbm, ua_hbm, down_hbm, dgu_out, tail_out, gate_out, up_out, down_out, buf, gua, rows, tails, down_w, acc, down_acc, send, recv, load, load_g, load_ua, load_rows, store_dgu, store_tail):
+    hidden, width = down_w.shape
     gather = Gather(own, buf, send, recv)
     loads = (
-        pltpu.make_async_copy(down_hbm, down_w, load.at[0]),
-        pltpu.make_async_copy(own.at[0], buf.at[gather.me, 0], load.at[1]),
-        pltpu.make_async_copy(own.at[1], buf.at[gather.me, 1], load.at[2]),
-        pltpu.make_async_copy(gate_hbm, gate_w, load.at[3]),
-        pltpu.make_async_copy(up_hbm, up_w, load.at[4]),
+        pltpu.make_async_copy(own.at[0], buf.at[gather.me, 0], load.at[0]),
+        pltpu.make_async_copy(own.at[1], buf.at[gather.me, 1], load.at[1]),
+        pltpu.make_async_copy(down_hbm, down_w, load.at[2]),
     )
     for copy in loads:
         copy.start()
 
     def block_loads(step):
         slot, half, _ = gather.place(step)
+        spot = lax.rem(step, BACK_SLOTS)
         return (
             pltpu.make_async_copy(
-                g_hbm.at[slot, half], gua.at[slot, half, :, pl.ds(0, hidden)], load_g.at[step]
+                g_hbm.at[slot, half], gua.at[spot, :, pl.ds(0, hidden)], load_g.at[step]
             ),
             pltpu.make_async_copy(
-                ua_hbm.at[slot, half],
-                gua.at[slot, half, :, pl.ds(hidden, 2 * hidden)],
-                load_ua.at[step],
+                ua_hbm.at[slot, half], gua.at[spot, :, pl.ds(hidden, 2 * hidden)], load_ua.at[step]
             ),
+            pltpu.make_async_copy(rows_hbm.at[slot, half], rows.at[spot], load_rows.at[step]),
+        )
+
+    def block_stores(step):
+        slot, half, _ = gather.place(step)
+        spot = lax.rem(step, BACK_SLOTS)
+        return (
             pltpu.make_async_copy(
-                rows_hbm.at[slot, half, :, pl.ds(width, 128)], tails.at[slot, half], load_tail.at[step]
+                gua.at[spot, :, pl.ds(0, 2 * hidden)], dgu_out.at[slot, half], store_dgu.at[step]
             ),
+            pltpu.make_async_copy(tails.at[spot], tail_out.at[slot, half], store_tail.at[step]),
         )
 
     def fetch(step, carry):
@@ -948,234 +960,199 @@
             copy.start()
         return carry
 
-    lax.fori_loop(0, 16, fetch, 0)
+    lax.fori_loop(0, BACK_SLOTS, fetch, 0)
     gather.begin()
     for copy in loads:
         copy.wait()
 
-    def dgu_store(step):
-        slot, half, _ = gather.place(step)
-        return pltpu.make_async_copy(
-            gua.at[slot, half, :, pl.ds(0, 2 * hidden)], dgu_out.at[slot, half], store_b.at[step]
-        )
-
-    def part_store(step):
-        slot, half, _ = gather.place(step)
-        return pltpu.make_async_copy(
-            part.at[lax.rem(step, PART_SLOTS)], part_out.at[slot, half], store_c.at[step]
-        )
-
-    def grad_down(step):
+    def weight_grads(step):
+        spot_a, spot_b = lax.rem(step - 1, BACK_SLOTS), lax.rem(step, BACK_SLOTS)
         slot_a, half_a, _ = gather.place(step - 1)
         slot_b, half_b, _ = gather.place(step)
 
-        def tile(index, carry):
-            rows = pl.ds(pl.multiple_of(index * 256, 256), 256)
-            cols = pl.ds(pl.multiple_of(2 * hidden + index * 256, 256), 256)
-            total = tn_dot(gua[slot_a, half_a, :, cols], buf[slot_a, half_a]) + tn_dot(
-                gua[slot_b, half_b, :, cols], buf[slot_b, half_b]
-            )
+        def add(ref, index, total):
+            at = pl.ds(pl.multiple_of(index * 256, 256), 256)
 
             @pl.when(step == 1)
             def _():
-                down_acc[rows, :] = total
+                ref[at, :] = total
 
             @pl.when(step > 1)
             def _():
-                down_acc[rows, :] = down_acc[rows, :] + total
-
+                ref[at, :] = ref[at, :] + total
+
+        def gate_up_tile(index, carry):
+            cols = pl.ds(pl.multiple_of(index * 256, 256), 256)
+            total = tn_dot(rows[spot_a, :, cols], gua[spot_a, :, : 2 * hidden])
+            total = total + tn_dot(rows[spot_b, :, cols], gua[spot_b, :, : 2 * hidden])
+            add(acc, index, total)
             return carry
 
-        lax.fori_loop(0, hidden // 256, tile, 0)
+        def down_tile(index, carry):
+            cols = pl.ds(pl.multiple_of(2 * hidden + index * 256, 256), 256)
+            total = tn_dot(gua[spot_a, :, cols], buf[slot_a, half_a])
+            total = total + tn_dot(gua[spot_b, :, cols], buf[slot_b, half_b])
+            add(down_acc, index, total)
+            return carry
+
+        lax.fori_loop(0, width // 256, gate_up_tile, 0)
+        lax.fori_loop(0, hidden // 256, down_tile, 0)
 
     def one(step, carry):
         slot, half = gather.arrive(step)
-
-        @pl.when(step >= PART_SLOTS)
-        def _():
-            part_store(step - PART_SLOTS).wait()
-
-        part_now = part.at[lax.rem(step, PART_SLOTS)]
+        spot = lax.rem(step, BACK_SLOTS)
         for copy in block_loads(step):
             copy.wait()
+
+        @pl.when((step >= 2) & (step < 14))
+        def _():
+            for copy in block_stores(step - 2):
+                copy.wait()
+            for copy in block_loads(step + 2):
+                copy.start()
+
         lanes = lax.broadcasted_iota(jnp.int32, (buf.shape[2], 128), 1)
-        tail = tails[slot, half].astype(jnp.float32)
+        tail = rows[spot, :, width:].astype(jnp.float32)
         weight = jnp.sum(jnp.where(lanes == gather.me, tail, 0.0), axis=1, keepdims=True)
         grad_act = nt_dot(buf[slot, half], down_w[...])
-        gate_val = gua[slot, half, :, :hidden].astype(jnp.float32)
-        up_val = gua[slot, half, :, hidden : 2 * hidden].astype(jnp.float32)
+        gate_val = gua[spot, :, :hidden].astype(jnp.float32)
+        up_val = gua[spot, :, hidden : 2 * hidden].astype(jnp.float32)
         gate_relu = jnp.maximum(gate_val, 0.0)
         grad_comb = jnp.sum(gate_relu * up_val * grad_act, axis=1, keepdims=True)
         grad_act = grad_act * weight
         grad_gate = jnp.where(gate_val > 0, grad_act * up_val, 0.0).astype(jnp.bfloat16)
         grad_up = (grad_act * gate_relu).astype(jnp.bfloat16)
-        gua[slot, half, :, :hidden] = grad_gate
-        gua[slot, half, :, hidden : 2 * hidden] = grad_up
-        dgu_store(step).start()
-        part_now[:, :width] = (
-            nt_dot(grad_gate, gate_w[...]) + nt_dot(grad_up, up_w[...])
-        ).astype(jnp.bfloat16)
-        part_now[:, width:] = jnp.where(lanes == gather.me, grad_comb, 0.0).astype(
-            jnp.bfloat16
-        )
-        part_store(step).start()
+        gua[spot, :, :hidden] = grad_gate
+        gua[spot, :, hidden : 2 * hidden] = grad_up
+        tails[spot] = jnp.where(lanes == gather.me, grad_comb, 0.0).astype(jnp.bfloat16)
+        for copy in block_stores(step):
+            copy.start()
 
         @pl.when(lax.rem(step, 2) == 1)
         def _():
-            grad_down(step)
+            weight_grads(step)
 
         return carry
 
     lax.fori_loop(0, 16, one, 0)
     gather.finish()
 
-    def round_down(rows):
-        down_out[rows, :] = down_acc[rows, :].astype(jnp.bfloat16)
+    def round_gate_up(at):
+        gate_out[at, :] = acc[at, :hidden].astype(jnp.bfloat16)
+        up_out[at, :] = acc[at, hidden:].astype(jnp.bfloat16)
+
+    row_loop(width, 64, round_gate_up)
+
+    def round_down(at):
+        down_out[at, :] = down_acc[at, :].astype(jnp.bfloat16)
 
     row_loop(hidden, 64, round_down)
 
     def drain(step, carry):
-        dgu_store(step).wait()
-
-        @pl.when(step >= 16 - PART_SLOTS)
-        def _():
-            part_store(step).wait()
-
+        for copy in block_stores(step):
+            copy.wait()
         return carry
 
-    lax.fori_loop(0, 16, drain, 0)
-
-
-PART_SLOTS = 4
-
-
-def expert_back(own, rows_all, gate_val, ua, gate_w, up_w, down_w):
-    _, half, columns = rows_all.shape[1:]
-    width, hidden = gate_w.shape
+    lax.fori_loop(12, 16, drain, 0)
+
+
+def expert_back(own, rows_all, gate_val, ua, down_w):
+    half, columns = rows_all.shape[2:]
+    hidden, width = down_w.shape
     bf = jnp.bfloat16
     return pl.pallas_call(
         expert_back_kernel,
         out_shape=(
             jax.ShapeDtypeStruct((8, 2, half, 2 * hidden), bf),
-            jax.ShapeDtypeStruct((8, 2, half, columns), bf),
+            jax.ShapeDtypeStruct((8, 2, half, 128), bf),
+            jax.ShapeDtypeStruct((width, hidden), bf),
+            jax.ShapeDtypeStruct((width, hidden), bf),
             jax.ShapeDtypeStruct((hidden, width), bf),
         ),
-        in_specs=[ANY] * 7,
-        out_specs=(ANY, ANY, VMEM),
+        in_specs=[ANY] * 5,
+        out_specs=(ANY, ANY, VMEM, VMEM, VMEM),
         scratch_shapes=[
             pltpu.VMEM((8, 2, half, width), bf),
-            pltpu.VMEM((8, 2, half, 3 * hidden), bf),
-            pltpu.VMEM((8, 2, half, 128), bf),
-            pltpu.VMEM((PART_SLOTS, half, columns), bf),
-            pltpu.VMEM((width, hidden), bf),
-            pltpu.VMEM((width, hidden), bf),
+            pltpu.VMEM((BACK_SLOTS, half, 3 * hidden), bf),
+            pltpu.VMEM((BACK_SLOTS, half, columns), bf),
+            pltpu.VMEM((BACK_SLOTS, half, 128), bf),
             pltpu.VMEM((hidden, width), bf),
+            pltpu.VMEM((width, 2 * hidden), jnp.float32),
             pltpu.VMEM((hidden, width), jnp.float32),
             pltpu.SemaphoreType.DMA((14,)),
             pltpu.SemaphoreType.DMA((8, 2)),
-            pltpu.SemaphoreType.DMA((5,)),
+            pltpu.SemaphoreType.DMA((3,)),
         ]
         + [pltpu.SemaphoreType.DMA((16,))] * 5,
         compiler_params=pltpu.CompilerParams(
             collective_id=3, has_side_effects=True, vmem_limit_bytes=VMEM_BYTES
         ),
         name="expert_back",
-    )(own, rows_all, gate_val, ua, gate_w, up_w, down_w)
-
-
-def expert_grads_kernel(part_hbm, rows_hbm, dgu_hbm, out, gate_out, up_out, rows, dgu, acc, mine, load, block_load, *scratch):
-    width = acc.shape[0]
-    hidden = acc.shape[1] // 2
+    )(own, rows_all, gate_val, ua, down_w)
+
+
+def expert_rows_kernel(dgu_hbm, tail_hbm, gate_hbm, up_hbm, out, dgu, tails, gate_w, up_w, mine, away, load_w, load_dgu, load_tail, *scratch):
+    width, hidden = gate_w.shape
     scatter = Scatter(
         lambda place, slot, half: mine.at[place, half],
-        lambda place, slot, half: part_hbm.at[slot, half],
+        lambda place, slot, half: away.at[place, half],
         scratch,
     )
-
-    def part_load(step):
-        slot, half, _, place = scatter.place(step)
-        return pltpu.make_async_copy(
-            part_hbm.at[slot, half], mine.at[place, half], load.at[step]
-        )
-
-    def fetch(step, carry):
-        @pl.when(scatter.place(step)[2] == 0)
-        def _():
-            part_load(step).start()
+    weights = (
+        pltpu.make_async_copy(gate_hbm, gate_w, load_w.at[0]),
+        pltpu.make_async_copy(up_hbm, up_w, load_w.at[1]),
+    )
+
+    def loads(step):
+        slot, half, _, _ = scatter.place(step)
+        spot = lax.rem(step, OUT_SLOTS)
+        return (
+            pltpu.make_async_copy(dgu_hbm.at[slot, half], dgu.at[spot], load_dgu.at[step]),
+            pltpu.make_async_copy(tail_hbm.at[slot, half], tails.at[spot], load_tail.at[step]),
+        )
+
+    for copy in weights:
+        copy.start()
+    for step in (0, 1):
+        for copy in loads(step):
+            copy.start()
+    plane_barrier(scatter.peers())
+    for copy in weights:
+        copy.wait()
+
+    def one(step, carry):
+        _, half, other, place = scatter.place(step)
+        spot = lax.rem(step, OUT_SLOTS)
+        for copy in loads(step):
+            copy.wait()
+
+        @pl.when(step < 14)
+        def _():
+            for copy in loads(step + 2):
+                copy.start()
+
+        total = nt_dot(dgu[spot, :, :hidden], gate_w[...]) + nt_dot(dgu[spot, :, hidden:], up_w[...])
+        partial = total.astype(jnp.bfloat16)
+
+        @pl.when(other == 1)
+        def _():
+            away[place, half, 0, :, :width] = partial
+            away[place, half, 0, :, width:] = tails[spot]
+
+        @pl.when(other == 0)
+        def _():
+            mine[place, half, 0, :, :width] = partial
+            mine[place, half, 0, :, width:] = tails[spot]
+
+        scatter.depart(step)
+
+        @pl.when(step == 12)
+        def _():
+            scatter.forward()
 
         return carry
 
-    def block_copies(block):
-        slot = lax.rem(block, 2)
-        return (
-            pltpu.make_async_copy(
-                rows_hbm.at[block, :, :, pl.ds(0, width)], rows.at[slot], block_load.at[slot, 0]
-            ),
-            pltpu.make_async_copy(dgu_hbm.at[block], dgu.at[slot], block_load.at[slot, 1]),
-        )
-
-    lax.fori_loop(0, 16, fetch, 0)
-    plane_barrier(scatter.peers())
-
-    def one(step, carry):
-        @pl.when(scatter.place(step)[2] == 0)
-        def _():
-            part_load(step).wait()
-
-        scatter.depart(step)
-        return carry
-
     lax.fori_loop(0, 16, one, 0)
-    for copy in block_copies(0):
-        copy.start()
-    tile = 256
-
-    def accumulate(block, carry):
-        for copy in block_copies(block):
-            copy.wait()
-
-        @pl.when(block < 7)
-        def _():
-            for copy in block_copies(block + 1):
-                copy.start()
-
-        slot = lax.rem(block, 2)
-
-        def add_tile(index, carry):
-            cols = pl.ds(pl.multiple_of(index * tile, tile), tile)
-            total = tn_dot(
-                rows[slot, :, :, cols].reshape(-1, tile), dgu[slot].reshape(-1, 2 * hidden)
-            )
-
-            @pl.when(block == 0)
-            def _():
-                acc[cols, :] = total
-
-            @pl.when(block > 0)
-            def _():
-                acc[cols, :] = acc[cols, :] + total
-
-            return carry
-
-        lax.fori_loop(0, width // tile, add_tile, 0)
-        return carry
-
-    def blocks(index, carry):
-        @pl.when(index == 3)
-        def _():
-            scatter.forward()
-
-        return accumulate(index, carry)
-
-    lax.fori_loop(0, 8, blocks, 0)
-
-    def round_tile(index, carry):
-        cols = pl.ds(pl.multiple_of(index * 64, 64), 64)
-        gate_out[cols, :] = acc[cols, :hidden].astype(jnp.bfloat16)
-        up_out[cols, :] = acc[cols, hidden:].astype(jnp.bfloat16)
-        return carry
-
-    lax.fori_loop(0, width // 64, round_tile, 0)
 
     def write(half, part, rows, total):
         out[half, rows, :] = total
@@ -1184,49 +1161,92 @@
     scatter.drain()
 
 
-def expert_grads(part, rows_all, dgu):
-    _, _, half, columns = part.shape
-    width = columns - 128
-    hidden = dgu.shape[3] // 2
+def expert_rows(dgu, tails, gate_w, up_w):
+    half = dgu.shape[2]
+    width, hidden = gate_w.shape
+    columns = width + 128
     bf = jnp.bfloat16
     return pl.pallas_call(
-        expert_grads_kernel,
-        out_shape=(
-            jax.ShapeDtypeStruct((2, half, columns), jnp.float32),
-            jax.ShapeDtypeStruct((width, hidden), bf),
-            jax.ShapeDtypeStruct((width, hidden), bf),
-        ),
-        in_specs=[ANY] * 3,
-        out_specs=(VMEM,) * 3,
+        expert_rows_kernel,
+        out_shape=jax.ShapeDtypeStruct((2, half, columns), jnp.float32),
+        in_specs=[ANY] * 4,
+        out_specs=VMEM,
         scratch_shapes=[
-            pltpu.VMEM((2, 2, half, width), bf),
-            pltpu.VMEM((2, 2, half, 2 * hidden), bf),
-            pltpu.VMEM((width, 2 * hidden), jnp.float32),
+            pltpu.VMEM((OUT_SLOTS, half, 2 * hidden), bf),
+            pltpu.VMEM((OUT_SLOTS, half, 128), bf),
+            pltpu.VMEM((width, hidden), bf),
+            pltpu.VMEM((width, hidden), bf),
             pltpu.VMEM((4, 2, 1, half, columns), bf),
+            pltpu.VMEM((4, 2, 1, half, columns), bf),
+            pltpu.SemaphoreType.DMA((2,)),
             pltpu.SemaphoreType.DMA((16,)),
-            pltpu.SemaphoreType.DMA((2, 2)),
+            pltpu.SemaphoreType.DMA((16,)),
         ]
         + scatter_scratch(1, half, columns),
         compiler_params=pltpu.CompilerParams(
             collective_id=4, has_side_effects=True, vmem_limit_bytes=VMEM_BYTES
         ),
-        name="expert_grads",
-    )(part.reshape(8, 2, 1, half, columns), rows_all, dgu)
+        name="expert_rows",
+    )(dgu, tails, gate_w, up_w)
+
+
+def line_gather_kernel(own, everything, stage, send, recv, local):
+    line = line_peers()
+    into = pltpu.make_async_copy(own, stage, local.at[0])
+    into.start()
+    full_barrier((), line[1:])
+
+    def copy(turn, block):
+        return line_remote(
+            own, everything.at[block], send.at[turn - 1], recv.at[turn - 1], line[turn]
+        )
+
+    for turn in (1, 2, 3):
+        copy(turn, line[0]).start()
+    into.wait()
+    out = pltpu.make_async_copy(stage, everything.at[line[0]], local.at[1])
+    out.start()
+    out.wait()
+    for turn in (1, 2, 3):
+        copy(turn, line[turn]).wait()
+
+
+def line_gather(own):
+    return pl.pallas_call(
+        line_gather_kernel,
+        out_shape=jax.ShapeDtypeStruct((4, *own.shape), own.dtype),
+        in_specs=[ANY],
+        out_specs=ANY,
+        scratch_shapes=[
+            pltpu.VMEM(own.shape, own.dtype),
+            pltpu.SemaphoreType.DMA((3,)),
+            pltpu.SemaphoreType.DMA((3,)),
+            pltpu.SemaphoreType.DMA((2,)),
+        ],
+        compiler_params=pltpu.CompilerParams(
+            collective_id=7, has_side_effects=True, vmem_limit_bytes=VMEM_BYTES
+        ),
+        name="line_gather",
+    )(own)
 
 
 class DenseGather:
-    def __init__(self, own, everything, send, recv, local):
+    def __init__(self, own, everything, send, recv, local, lined):
         self.own, self.everything, self.send, self.recv = own, everything, send, recv
+        self.lined = lined
         self.me, self.sib, self.xn, self.yn = plane_peers()
         self.diag = self.xn + self.yn - self.me
         self.line = line_peers()
-        self.home = pltpu.make_async_copy(own, everything.at[self.line[0], self.me], local)
+        if lined:
+            self.home = pltpu.make_async_copy(own, everything.at[:, self.me], local)
+        else:
+            self.home = pltpu.make_async_copy(own, everything.at[self.line[0], self.me], local)
         self.started = []
 
     def copy(self, index, own, slot, turn, peer, make):
         target = self.everything.at[self.line[turn], slot]
         return make(
-            self.own if own else target,
+            (self.own.at[self.line[turn]] if self.lined else self.own) if own else target,
             target,
             self.send.at[index],
             self.recv.at[self.line[turn], slot],
@@ -1250,11 +1270,12 @@
             self.put(True, self.me, 0, self.line[turn], line_remote)
 
     def start_plane(self):
-        for peer in (self.xn, self.yn, self.sib):
-            self.put(True, self.me, 0, peer)
+        for turn in (0, 1, 2, 3) if self.lined else (0,):
+            for peer in (self.xn, self.yn, self.sib):
+                self.put(True, self.me, turn, peer)
 
     def turn(self, turn):
-        if turn > 0:
+        if turn > 0 and not self.lined:
             self.wait(self.me, turn)
             for peer in (self.xn, self.yn, self.sib):
                 self.pass_on(self.me, turn, peer)
@@ -1410,13 +1431,13 @@
 TILE = 256
 
 
-def attend_kernel(q_heads, kv_heads, experts, tokens, qkv_own, out_own, cosine, sine, bias, picked, rows_out, resid, heads, mixed, lse, prob, qkv_hbm, out_hbm, gains, hidden, *scratch):
+def attend_kernel(q_heads, kv_heads, experts, tokens, qkv_own, out_own, cosine, sine, segments, routes, rows_out, resid, heads, mixed, lse, prob, bias, picked, qkv_hbm, out_hbm, gains, hidden, *scratch):
     num_rows, width = tokens.shape
     group = q_heads // kv_heads
     qkv_cols = (q_heads + 2 * kv_heads) * HD
     qkv_w, out_w = scratch[0], scratch[4]
-    first = DenseGather(qkv_own, qkv_w, scratch[1], scratch[2], scratch[3].at[0])
-    second = DenseGather(out_own, out_w, scratch[5], scratch[6], scratch[7].at[0])
+    first = DenseGather(qkv_own, qkv_w, scratch[1], scratch[2], scratch[3].at[0], True)
+    second = DenseGather(out_own, out_w, scratch[5], scratch[6], scratch[7].at[0], False)
     stores = (
         pltpu.make_async_copy(qkv_w, qkv_hbm, scratch[3].at[1]),
         pltpu.make_async_copy(out_w, out_hbm, scratch[7].at[1]),
@@ -1424,9 +1445,21 @@
     for gather in (first, second):
         gather.home.start()
     full_barrier((first.sib, first.xn, first.yn), first.line[1:])
-    first.start_line()
     first.start_plane()
     second.start_line()
+    picked[...] = jnp.zeros_like(picked)
+    lane_ids = lax.broadcasted_iota(jnp.int32, picked.shape, 1)
+    for index in range(routes.shape[1]):
+        picked[...] = picked[...] + jnp.where(lane_ids == routes[:, index : index + 1], 1.0, 0.0)
+    seg_row = segments[0:1, :]
+    for index in range(num_rows // 128):
+        rows = slice(index * 128, (index + 1) * 128)
+        wide = jnp.broadcast_to(seg_row[:, rows].astype(jnp.float32), (128, 128))
+        seg_col = jnp.transpose(wide)[:, 0:1].astype(jnp.int32)
+        keys = lax.broadcasted_iota(jnp.int32, (128, num_rows), 1)
+        queries = lax.broadcasted_iota(jnp.int32, (128, num_rows), 0) + index * 128
+        visible = (keys <= queries) & ((seg_row == 0) | (seg_row == seg_col))
+        bias[rows, :] = jnp.where(visible, 0.0, NEG_BIG)
     for turn in (0, 1, 2, 3):
         first.turn(turn)
     first.far(3)
@@ -1520,7 +1553,7 @@
         gather.finish()
 
 
-def attend(tokens, qkv_own, out_own, cosine, sine, bias, picked, q_heads, kv_heads, experts):
+def attend(tokens, qkv_own, out_own, cosine, sine, segments, routes, q_heads, kv_heads, experts):
     num_rows, width = tokens.shape
     bf = jnp.bfloat16
     all_heads = q_heads + 2 * kv_heads
@@ -1533,22 +1566,24 @@
             jax.ShapeDtypeStruct((num_rows, q_heads * HD), bf),
             jax.ShapeDtypeStruct((num_rows, 128), jnp.float32),
             jax.ShapeDtypeStruct((num_rows, 128), jnp.float32),
-            jax.ShapeDtypeStruct((4, 8, *qkv_own.shape), bf),
+            jax.ShapeDtypeStruct((num_rows, num_rows), jnp.float32),
+            jax.ShapeDtypeStruct((num_rows, 128), jnp.float32),
+            jax.ShapeDtypeStruct((4, 8, *qkv_own.shape[1:]), bf),
             jax.ShapeDtypeStruct((4, 8, *out_own.shape), bf),
         ),
         in_specs=[VMEM, ANY, ANY] + [VMEM] * 4,
-        out_specs=(VMEM,) * 6 + (ANY, ANY),
+        out_specs=(VMEM,) * 8 + (ANY, ANY),
         scratch_shapes=[
             pltpu.VMEM((128, width), jnp.float32),
             pltpu.VMEM((num_rows, width), bf),
         ]
-        + gather_scratch(*qkv_own.shape)
+        + gather_scratch(*qkv_own.shape[1:])
         + gather_scratch(*out_own.shape),
         compiler_params=pltpu.CompilerParams(
             collective_id=5, has_side_effects=True, vmem_limit_bytes=VMEM_BYTES
         ),
         name="attend",
-    )(tokens, qkv_own, out_own, cosine, sine, bias, picked)
+    )(tokens, qkv_own, out_own, cosine, sine, segments.reshape(1, num_rows), routes)
 
 
 def attend_back_kernel(q_heads, kv_heads, experts, back_hbm, grad_hbm, resid_hbm, rows_hbm, prob_hbm, picked_hbm, qkv_hbm, out_hbm, mixed_hbm, heads_hbm, lse_hbm, bias_hbm, cos_hbm, sin_hbm, tokens_hbm, grad_in, out_sum, q_sum, k_sum, v_sum, misc_sum, back, grad, resid, hidden_two, prob, picked, qkv_w, out_w, mixed, heads, lse, bias, cosine, sine, tokens, gains, gain_sums, grad_logit, grad_proj, grad_mixed, grad_qkv, grad_kv, hidden, load, *scratch):
@@ -1846,19 +1881,17 @@
         ],
         axis=1,
     )
+    qkv_line, w_gate, w_up = lax.optimization_barrier((line_gather(qkv_own), w_gate, w_up))
     gate_w = lax.all_gather(w_gate, "dp", axis=1, tiled=True)[0]
     up_w = lax.all_gather(w_up, "dp", axis=1, tiled=True)[0]
     tok_pos = positions(segments)
-    bias = jnp.where(key_mask(segments), 0.0, NEG_BIG)
     freq = THETA ** (-2.0 * jnp.arange(HD // 2, dtype=jnp.float32) / HD)
     angle = tok_pos.astype(jnp.float32)[:, None] * freq[None, :]
     cosine, sine_part = jnp.cos(angle), jnp.sin(angle)
     cosine = jnp.concatenate([cosine, cosine], axis=1)
     sine = jnp.concatenate([-sine_part, sine_part], axis=1)
-    lane_ids = jnp.arange(128, dtype=jnp.int32)
-    picked = jnp.sum((routes[:, :, None] == lane_ids[None, None, :]).astype(jnp.float32), axis=1)
-    rows_own, resid_mid, heads, mixed, lse, prob, qkv_w, out_w = attend(
-        tokens, qkv_own, w_out, cosine, sine, bias, picked, num_heads, kv_heads, num_experts
+    rows_own, resid_mid, heads, mixed, lse, prob, bias, picked, qkv_w, out_w = attend(
+        tokens, qkv_line, w_out, cosine, sine, segments, routes, num_heads, kv_heads, num_experts
     )
     rows_all, gate_val, down_w = expert_in(
         rows_own.reshape(2, half, width + 128), gate_w, w_down[0]
@@ -1874,10 +1907,10 @@
         rows_all, gate_val, up_w, down_w, resid_mid, targets, scales
     )
     layer_out = layer_out.reshape(num_rows, width)
-    dgu, part, down_part = expert_back(
-        grad_out_b, rows_all, gate_val, ua, gate_w, up_w, down_w
-    )
-    back, gate_part, up_part = expert_grads(part, rows_all, dgu)
+    dgu, tails, gate_part, up_part, down_part = expert_back(
+        grad_out_b, rows_all, gate_val, ua, down_w
+    )
+    back = expert_rows(dgu, tails, gate_w, up_w)
     expert_sums = tuple(
         lax.psum_scatter(grad[None], "dp", scatter_dimension=1, tiled=True).astype(jnp.float32)
         for grad in (gate_part, up_part, down_part)

time: 557 us -> 549 us (0.986)
    pallas_call x1 -> x2, Pallas kernels: 67.8 us -> 92.1 us  [the longest x1 71 us: expert_rows(): pl.pallas_call(expert_rows_kernel, out_shape=jax.ShapeDtypeStruct((2, hal...]
    pallas_call x1, Pallas kernels: 109 us -> 87.7 us  [attend(): pl.pallas_call(functools.partial(attend_kernel, q_heads, kv_heads, expert...]
    pallas_call x1, Pallas kernels: 120 us -> 110 us  [attend_back(): pl.pallas_call(functools.partial(attend_back_kernel, q_heads, kv_heads, e...]
    pallas_call x1, Pallas kernels: 73.4 us -> 79.5 us  [expert_back(): pl.pallas_call(expert_back_kernel, out_shape=(jax.ShapeDtypeStruct((8, 2,...]
  transfers between devices with their start and end apart: 5 -> 5, of which waited for: 0 -> 0; matrix products, arithmetic and copies ran while one was open for 3% -> 2% of each run, Pallas kernels for 66% -> 61%
where the time goes in v6:
time: 549 us
  Pallas kernels  508 us (93%)
  local copies, waits for them, and re-layouts  15.6 us (3%)
  between operations  14.6 us (3%)
  other arithmetic  8.9 us (2%)
    pallas_call x1, Pallas kernels, attend_back(): pl.pallas_call(functools.partial(attend_back_kernel, q_heads, kv_heads, e...  110 us
    pallas_call x1, Pallas kernels, attend(): pl.pallas_call(functools.partial(attend_kernel, q_heads, kv_heads, expert...  87.7 us
    pallas_call x1, Pallas kernels, expert_back(): pl.pallas_call(expert_back_kernel, out_shape=(jax.ShapeDtypeStruct((8, 2,...  79.5 us
    pallas_call x1, Pallas kernels, expert_rows(): pl.pallas_call(expert_rows_kernel, out_shape=jax.ShapeDtypeStruct((2, hal...  71 us
    pallas_call x1, Pallas kernels, expert_out(): pl.pallas_call(expert_out_kernel, out_shape=(jax.ShapeDtypeStruct((2, hal...  70.6 us
    pallas_call x1, Pallas kernels, expert_in(): pl.pallas_call(expert_in_kernel, out_shape=(jax.ShapeDtypeStruct((8, 2, h...  68.3 us
    pallas_call x1, Pallas kernels, line_gather(): pl.pallas_call(line_gather_kernel, out_shape=jax.ShapeDtypeStruct((4, *ow...  21 us
  transfers between devices with their start and end apart: 5, of which 0 were waited for; matrix products, arithmetic and copies ran while one was open for 2% of the time, Pallas kernels for 61%

profile of v6, /device:TPU:0, one launch (start us, length us, event | category | flops | bytes accessed | tf_op | source)
XLA Modules:
  0.0 548.9 jit_solution(9290789604771922782)
XLA Ops:
  7.2 0.8 copy.38
  8.0 0.8 copy.39
  8.8 0.8 copy.37
  9.5 1.7 concatenate.9.own
  11.2 21.0 %line_gather.1.qkv_own = bf16[4,48,2176]{2,1,0:T(8,128)(2,1)} custom-call(bf16[48,2176]{1,0:T(8,128)(2,1)} %concatenate.9.own), custom_call_target="tpu_custom_call" | custom-call | tf_op jit(solution)/shard_map/line_gather/pallas_call | solution.py:1215
  32.3 0.7 all-gather.5.cloned.1.call-update
  33.8 0.9 copy.40.routes
  34.7 0.1 select_reduce_fusion.1
  34.8 0.1 select_reduce_fusion
  34.9 1.0 fusion
  35.9 1.0 pad_maximum_fusion
  36.9 87.7 %attend.1 = (bf16[512,1664]{1,0:T(8,128)(2,1)}, f32[512,1536]{1,0:T(8,128)}, bf16[16,512,128]{2,1,0:T(8,128)(2,1)}, bf16[512,1536]{1,0:T(8,128)(2,1)}, f32[512,1...) custom-call(bf16[512,1536]{1,0:T(8,128)(2,1)} %tokens_hbm.1, ...), custom_call_target="tpu_custom_call" | custom-call | tf_op jit(solution)/shard_map/attend/pallas_call | solution.py:1560
  124.6 68.3 %expert_in.1 = (bf16[8,2,256,1664]{3,2,1,0:T(8,128)(2,1)}, bf16[8,2,256,768]{3,2,1,0:T(8,128)(2,1)}, bf16[4,192,1536]{2,1,0:T(8,128)(2,1)}) custom-call(bf16[2,256,1664]{2,1,0:T(8,128)(2,1)} %bitcast.30, bf16[1536,768]{1,0:T(8,128)(2,1)} %bitcast.28, bf16[192,1536]{1,0:T(8,128)(2,1)} %bitcast.39), custom_call_target="tpu_custom_call" | custom-call | tf_op jit(solution)/shard_map/expert_in/pallas_call | solution.py:580
  193.0 0.8 broadcast_in_dim.71.scales
  193.9 70.6 %expert_out.1 = (bf16[2,256,1536]{2,1,0:T(8,128)(2,1)}, f32[2,256,1536]{2,1,0:T(8,128)}, bf16[2,256,1536]{2,1,0:T(8,128)(2,1)}, bf16[8,2,256,1536]{3,2,1,0:T(8,128)(2,1)}) custom-call(bf16[8,2,256,1664]{3,2,1,0:T(8,128)(2,1)} %get-tuple-element.46.rows_hbm, bf16[8,2,256,768]{3,2,1,0:T(8,128)(2,1)} %get-tuple-element.47.gate_hbm.g_hbm, ...), custom_call_target="tpu_custom_call" | custom-call | tf_op jit(solution)/shard_map/expert_out/pallas_call | solution.py:882
  264.5 79.5 %expert_back.1 = (bf16[8,2,256,1536]{3,2,1,0:T(8,128)(2,1)}, bf16[8,2,256,128]{3,2,1,0:T(8,128)(2,1)}, bf16[1536,768]{1,0:T(8,128)(2,1)}, bf16[1536,768]{1,0:T(8,128)(2,1)}, bf16[768,1536]{1,0:T(8,128)(2,1)}) custom-call(bf16[2,256,1536]{2,1,0:T(8,128)(2,1)} %get-tuple-element.52.own, bf16[8,2,256,1664]{3,2,1,0:T(8,128)(2,1)} %get-tuple-element.46.rows_hbm, ...), custom_call_target="tpu_custom_call" | custom-call | tf_op jit(solution)/shard_map/expert_back/pallas_call | solution.py:1063
  344.1 0.5 reduce-scatter.6.cloned.1.call-update
  344.6 0.2 reduce-scatter.4.cloned.1.call-start
  344.8 0.4 reduce-scatter.4.cloned.1.call-update
  345.2 71.0 %expert_rows.1 = f32[2,256,1664]{2,1,0:T(8,128)} custom-call(bf16[8,2,256,1536]{3,2,1,0:T(8,128)(2,1)} %get-tuple-element.54.dgu_hbm, bf16[8,2,256,128]{3,2,1,0:T(8,128)(2,1)} %get-tuple-element.55.tail_hbm, bf16[1536,768]{1,0:T(8,128)(2,1)} %bitcast.29, bf16[1536,768]{1,0:T(8,128)(2,1)} %bitcast.27), custom_call_target="tpu_custom_call" | custom-call | tf_op jit(solution)/shard_map/expert_rows/pallas_call | solution.py:1169
  416.3 109.5 %attend_back.1 = (f32[512,1536]{1,0:T(8,128)}, f32[48,1536]{1,0:T(8,128)}, f32[48,1536]{1,0:T(8,128)}, f32[48,256]{1,0:T(8,128)}, f32[48,256]{1,0:T(8,128)}, /*index=5*/f32[48,128]{1,0:T(8,128)}) custom-call(f32[512,1664]{1,0:T(8,128)} %bitcast.22, f32[512,1536]{1,0:T(8,128)} %bitcast.33, f32[512,1536]{1,0:T(8,128)} %get-tuple-element.50.resid_hbm, ...), custom_call_target="tpu_custom_call" | custom-call | tf_op jit(solution)/shard_map/attend_back/pallas_call | solution.py:1818
  525.8 1.4 copy.41
  527.2 1.5 slice_reduce_fusion
  528.7 2.2 convert_element_type.19
  530.9 2.2 convert_element_type.18
  533.1 2.3 convert_element_type.17
  535.4 2.7 copy.49
  538.1 1.7 copy.50
  539.7 0.7 copy.51
  540.5 0.6 copy.52
  541.1 0.6 copy.53
  541.7 0.7 copy.54
  (29 shorter events, 0.3 us)
Async XLA Ops:
  7.2 26.6 %copy-start.6 = (s32[512,4]{0,1:T(4,128)S(1)}, s32[512,4]{0,1:T(4,128)}, u32[]{:S(2)}) copy-start(s32[512,4]{0,1:T(4,128)} %param.19) | copy-start | bytes 24580
  7.2 27.5 %copy-start.5 = (s32[512]{0:T(512)S(1)}, s32[512]{0:T(512)}, u32[]{:S(2)}) copy-start(s32[512]{0:T(512)} %param.18) | copy-start | bytes 6148
  7.2 117.4 %all-gather.3.cloned.1.call-start = ((), (), s32[]{:S(2)}) async-start(), calls=%async_computation.3 | async-start | bytes 2949120 | tf_op jit(solution)/shard_map/all_gather | solution.py:1885
  32.3 160.7 %all-gather.5.cloned.1.call-start = ((), (), s32[]{:S(2)}) async-start(), calls=%async_computation.4 | async-start | bytes 2949120 | tf_op jit(solution)/shard_map/all_gather | solution.py:1886
  33.1 495.7 %reduce-scatter.8.cloned.1.call-start = ((), (), s32[]{:S(2)}) async-start(), calls=%async_computation.7 | async-start | bytes 2949120 | tf_op jit(solution)/shard_map/reduce_scatter | solution.py:1915
  344.0 186.9 %reduce-scatter.6.cloned.1.call-start = ((), (), s32[]{:S(2)}) async-start(), calls=%async_computation.6 | async-start | bytes 2949120 | tf_op jit(solution)/shard_map/reduce_scatter | solution.py:1915
  344.6 188.5 %reduce-scatter.4.cloned.1.call-start = ((), (), s32[]{:S(2)}) async-start(), calls=%async_computation.5 | async-start | bytes 2949120 | tf_op jit(solution)/shard_map/reduce_scatter | solution.py:1915
  533.1 5.0 copy-start
  538.1 1.7 copy-start.2
  538.1 2.4 copy-start.4
  538.1 3.0 copy-start.3
  538.1 3.6 copy-start.1
Sparse Core Ops, SparseCore 0:
  32.4 63.6 all-gather.2
  97.7 67.1 all-gather.4
  344.2 50.9 reduce-scatter.7
  397.4 47.0 reduce-scatter.5
  446.6 63.2 reduce-scatter.3

commit v7 on v6

--- a/solution.py
+++ b/solution.py
@@ -709,6 +709,23 @@
                 self.side_wait(1 + way, way)
                 add_rows(self.mine(1 + way, way), (self.side.at[1 + way, way],))
                 self.final_copy(5 + 2 * way, way, way).start()
+
+    def send_theirs(self):
+        def one(index, carry):
+            self.side_copy(2 * index).start()
+            return carry
+
+        lax.fori_loop(0, 8, one, 0)
+
+    def send_mine(self):
+        for way in (0, 1):
+            self.side_wait(3, way)
+            add_rows(self.mine(3, way), (self.side.at[3, way],))
+            self.relay_copy(1 + 2 * way, way).start()
+        for way in (0, 1):
+            self.side_wait(1 + way, way)
+            add_rows(self.mine(1 + way, way), (self.side.at[1 + way, way],))
+            self.final_copy(5 + 2 * way, way, way).start()
 
     def forward(self):
         for way in (0, 1):
@@ -918,7 +935,7 @@
     )
 
 
-BACK_SLOTS = 4
+BACK_SLOTS = 8
 
 
 def expert_back_kernel(own, rows_hbm, g_hbm, ua_hbm, down_hbm, dgu_out, tail_out, gate_out, up_out, down_out, buf, gua, rows, tails, down_w, acc, down_acc, send, recv, load, load_g, load_ua, load_rows, store_dgu, store_tail):
@@ -966,32 +983,33 @@
         copy.wait()
 
     def weight_grads(step):
-        spot_a, spot_b = lax.rem(step - 1, BACK_SLOTS), lax.rem(step, BACK_SLOTS)
-        slot_a, half_a, _ = gather.place(step - 1)
-        slot_b, half_b, _ = gather.place(step)
+        first = 4 * lax.rem(lax.div(step, 4), 2)
+        spots = pl.ds(first, 4)
+        places = [gather.place(step - 3 + index)[:2] for index in range(4)]
 
         def add(ref, index, total):
             at = pl.ds(pl.multiple_of(index * 256, 256), 256)
 
-            @pl.when(step == 1)
+            @pl.when(step == 3)
             def _():
                 ref[at, :] = total
 
-            @pl.when(step > 1)
+            @pl.when(step > 3)
             def _():
                 ref[at, :] = ref[at, :] + total
 
         def gate_up_tile(index, carry):
             cols = pl.ds(pl.multiple_of(index * 256, 256), 256)
-            total = tn_dot(rows[spot_a, :, cols], gua[spot_a, :, : 2 * hidden])
-            total = total + tn_dot(rows[spot_b, :, cols], gua[spot_b, :, : 2 * hidden])
-            add(acc, index, total)
+            left = rows[spots, :, cols].reshape(-1, 256)
+            right = gua[spots, :, : 2 * hidden].reshape(-1, 2 * hidden)
+            add(acc, index, tn_dot(left, right))
             return carry
 
         def down_tile(index, carry):
             cols = pl.ds(pl.multiple_of(2 * hidden + index * 256, 256), 256)
-            total = tn_dot(gua[spot_a, :, cols], buf[slot_a, half_a])
-            total = total + tn_dot(gua[spot_b, :, cols], buf[slot_b, half_b])
+            total = jnp.zeros((256, width), jnp.float32)
+            for place, (slot, half) in enumerate(places):
+                total = total + tn_dot(gua[first + place, :, cols], buf[slot, half])
             add(down_acc, index, total)
             return carry
 
@@ -1003,13 +1021,6 @@
         spot = lax.rem(step, BACK_SLOTS)
         for copy in block_loads(step):
             copy.wait()
-
-        @pl.when((step >= 2) & (step < 14))
-        def _():
-            for copy in block_stores(step - 2):
-                copy.wait()
-            for copy in block_loads(step + 2):
-                copy.start()
 
         lanes = lax.broadcasted_iota(jnp.int32, (buf.shape[2], 128), 1)
         tail = rows[spot, :, width:].astype(jnp.float32)
@@ -1028,9 +1039,17 @@
         for copy in block_stores(step):
             copy.start()
 
-        @pl.when(lax.rem(step, 2) == 1)
+        @pl.when(lax.rem(step, 4) == 3)
         def _():
             weight_grads(step)
+
+            @pl.when(step < 8)
+            def _():
+                for index in range(4):
+                    for copy in block_stores(step - 3 + index):
+                        copy.wait()
+                    for copy in block_loads(step + 5 + index):
+                        copy.start()
 
         return carry
 
@@ -1053,7 +1072,7 @@
             copy.wait()
         return carry
 
-    lax.fori_loop(12, 16, drain, 0)
+    lax.fori_loop(8, 16, drain, 0)
 
 
 def expert_back(own, rows_all, gate_val, ua, down_w):
@@ -1274,11 +1293,7 @@
             for peer in (self.xn, self.yn, self.sib):
                 self.put(True, self.me, turn, peer)
 
-    def turn(self, turn):
-        if turn > 0 and not self.lined:
-            self.wait(self.me, turn)
-            for peer in (self.xn, self.yn, self.sib):
-                self.pass_on(self.me, turn, peer)
+    def near(self, turn):
         self.wait(self.xn, turn)
         if turn % 2 == 0:
             self.pass_on(self.xn, turn, self.yn)
@@ -1287,8 +1302,11 @@
         if turn % 2 == 1:
             self.pass_on(self.yn, turn, self.xn)
         self.pass_on(self.yn, turn, self.sib)
-        if turn > 0:
-            self.far(turn - 1)
+
+    def from_line(self, turn):
+        self.wait(self.me, turn)
+        for peer in (self.xn, self.yn, self.sib):
+            self.pass_on(self.me, turn, peer)
 
     def far(self, turn):
         self.wait(self.diag, turn)
@@ -1368,11 +1386,10 @@
         )
 
     def begin(self):
-        def one(step, carry):
-            self.plane.depart(step)
-            return carry
-
-        lax.fori_loop(0, 16, one, 0)
+        self.plane.send_theirs()
+
+    def own(self):
+        self.plane.send_mine()
 
     def forward(self):
         self.plane.forward()
@@ -1461,12 +1478,13 @@
         visible = (keys <= queries) & ((seg_row == 0) | (seg_row == seg_col))
         bias[rows, :] = jnp.where(visible, 0.0, NEG_BIG)
     for turn in (0, 1, 2, 3):
-        first.turn(turn)
+        first.near(turn)
+        if turn > 0:
+            first.far(turn - 1)
     first.far(3)
     second.start_plane()
     first.arrived()
     stores[0].start()
-    second.turn(0)
 
     def flat(ref, cols):
         return ref[:, :, :, cols].reshape(-1, cols.size)
@@ -1482,6 +1500,9 @@
         hidden[rows, :] = (normed * gains[experts : experts + 1, :]).astype(jnp.bfloat16)
 
     row_loop(num_rows, ROW_CHUNK, norm_one)
+
+    for turn in (1, 2, 3):
+        second.from_line(turn)
 
     def project(index, carry):
         cols = pl.ds(pl.multiple_of(index * TILE, TILE), TILE)
@@ -1495,7 +1516,7 @@
         return carry
 
     lax.fori_loop(0, (q_heads + 2 * kv_heads) // 2, project, 0)
-    second.turn(1)
+    second.near(0)
     lse[...] = jnp.zeros_like(lse)
 
     def head_step(head, carry):
@@ -1513,13 +1534,17 @@
             lanes = lax.broadcasted_iota(jnp.int32, (keys - first, 128), 1)
             lse[rows, :] = jnp.where(lanes == head, top + jnp.log(total), lse[rows, :])
 
-        @pl.when(head == q_heads // 3)
-        def _():
-            second.turn(2)
-
-        @pl.when(head == 2 * q_heads // 3)
-        def _():
-            second.turn(3)
+        for turn in (1, 2, 3):
+
+            @pl.when(head == 2 * turn - 1)
+            def _():
+                second.near(turn)
+
+        for turn in (0, 1, 2):
+
+            @pl.when(head == 6 + turn)
+            def _():
+                second.far(turn)
 
         return carry
 
@@ -1690,6 +1715,7 @@
         ).astype(bf)
 
     tile_loop(q_cols, TILE, mixed_tile)
+    out_scatter.own()
 
     def norm_one(rows):
         value = tokens[rows, :].astype(jnp.float32)
@@ -1739,6 +1765,10 @@
             weight_loop(near_part, hidden, grad_qkv.at[:, pl.ds(0, near_cols)])
             near_scatter.begin()
 
+        @pl.when(head == group)
+        def _():
+            near_scatter.own()
+
         @pl.when(head == group + 1)
         def _():
             out_scatter.turn()
@@ -1757,8 +1787,14 @@
     def hidden_back_tile(cols):
         back[:, cols] = nt_dot(grad_qkv[...], qkv_w[cols, pl.ds(0, qkv_cols)])
 
-    tile_loop(width, TILE, hidden_back_tile)
-    rest_scatter.forward()
+    tile_loop(width // 2, TILE, hidden_back_tile)
+    rest_scatter.own()
+
+    def late_tile(index, carry):
+        hidden_back_tile(pl.ds(pl.multiple_of(width // 2 + index * TILE, TILE), TILE))
+        return carry
+
+    lax.fori_loop(0, width // 2 // TILE, late_tile, 0)
 
     def last_rows(rows):
         value = tokens[rows, :].astype(jnp.float32)
@@ -1771,6 +1807,7 @@
         grad[rows, :] = grad[rows, :] + inverse * (grad_norm - normed * mean)
 
     row_loop(num_rows, ROW_CHUNK, last_rows)
+    rest_scatter.forward()
     store = pltpu.make_async_copy(grad, grad_in, load.at[0])
     store.start()
     gains[0:16, :] = gain_sums[...]
@@ -1790,8 +1827,9 @@
 
     lax.fori_loop(0, 4, misc_line, 0)
     misc_scatter.begin()
+    misc_scatter.own()
+    rest_scatter.turn()
     misc_scatter.forward()
-    rest_scatter.turn()
     misc_scatter.turn()
     out_scatter.finish(((out_sum, 0, width),))
     near_scatter.finish(((q_sum, 0, near_cols),))

time: 549 us -> 544 us (level)
  Pallas kernels: 508 us -> 501 us
    pallas_call x1, Pallas kernels: 87.7 us -> 73.7 us  [attend(): pl.pallas_call(functools.partial(attend_kernel, q_heads, kv_heads, expert...]
    pallas_call x1, Pallas kernels: 68.3 us -> 75.1 us  [expert_in(): pl.pallas_call(expert_in_kernel, out_shape=(jax.ShapeDtypeStruct((8, 2, h...]
    pallas_call x1, Pallas kernels: 79.5 us -> 73.3 us  [expert_back(): pl.pallas_call(expert_back_kernel, out_shape=(jax.ShapeDtypeStruct((8, 2,...]
  transfers between devices with their start and end apart: 5 -> 5, of which waited for: 0 -> 1; matrix products, arithmetic and copies ran while one was open for 2% -> 2% of each run, Pallas kernels for 61% -> 61%
where the time goes in v7:
time: 544 us
  Pallas kernels  501 us (92%)
  local copies, waits for them, and re-layouts  15.6 us (3%)
  between operations  14.6 us (3%)
  other arithmetic  8.9 us (2%)
    pallas_call x1, Pallas kernels, attend_back(): pl.pallas_call(functools.partial(attend_back_kernel, q_heads, kv_heads, e...  114 us
    pallas_call x1, Pallas kernels, expert_in(): pl.pallas_call(expert_in_kernel, out_shape=(jax.ShapeDtypeStruct((8, 2, h...  75.1 us
    pallas_call x1, Pallas kernels, attend(): pl.pallas_call(functools.partial(attend_kernel, q_heads, kv_heads, expert...  73.7 us
    pallas_call x1, Pallas kernels, expert_back(): pl.pallas_call(expert_back_kernel, out_shape=(jax.ShapeDtypeStruct((8, 2,...  73.3 us
    pallas_call x1, Pallas kernels, expert_out(): pl.pallas_call(expert_out_kernel, out_shape=(jax.ShapeDtypeStruct((2, hal...  73.1 us
    pallas_call x1, Pallas kernels, expert_rows(): pl.pallas_call(expert_rows_kernel, out_shape=jax.ShapeDtypeStruct((2, hal...  70.4 us
    pallas_call x1, Pallas kernels, line_gather(): pl.pallas_call(line_gather_kernel, out_shape=jax.ShapeDtypeStruct((4, *ow...  21 us
  transfers between devices with their start and end apart: 5, of which 1 were waited for; matrix products, arithmetic and copies ran while one was open for 2% of the time, Pallas kernels for 61%

profile of v7, /device:TPU:0, one launch (start us, length us, event | category | flops | bytes accessed | tf_op | source)
XLA Modules:
  0.0 543.5 jit_solution(14812601586868183937)
XLA Ops:
  7.2 0.8 copy.38
  8.0 0.8 copy.39
  8.8 0.8 copy.37
  9.5 1.7 concatenate.9.own
  11.2 21.0 %line_gather.1.qkv_own = bf16[4,48,2176]{2,1,0:T(8,128)(2,1)} custom-call(bf16[48,2176]{1,0:T(8,128)(2,1)} %concatenate.9.own), custom_call_target="tpu_custom_call" | custom-call | tf_op jit(solution)/shard_map/line_gather/pallas_call | solution.py:1234
  32.3 0.7 all-gather.5.cloned.1.call-update
  33.8 0.9 copy.40.routes
  34.7 0.1 select_reduce_fusion.1
  34.9 1.0 fusion
  35.9 1.0 pad_maximum_fusion
  36.9 73.7 %attend.1 = (bf16[512,1664]{1,0:T(8,128)(2,1)}, f32[512,1536]{1,0:T(8,128)}, bf16[16,512,128]{2,1,0:T(8,128)(2,1)}, bf16[512,1536]{1,0:T(8,128)(2,1)}, f32[512,1...) custom-call(bf16[512,1536]{1,0:T(8,128)(2,1)} %tokens_hbm.1, ...), custom_call_target="tpu_custom_call" | custom-call | tf_op jit(solution)/shard_map/attend/pallas_call | solution.py:1585
  110.7 75.1 %expert_in.1 = (bf16[8,2,256,1664]{3,2,1,0:T(8,128)(2,1)}, bf16[8,2,256,768]{3,2,1,0:T(8,128)(2,1)}, bf16[4,192,1536]{2,1,0:T(8,128)(2,1)}) custom-call(bf16[2,256,1664]{2,1,0:T(8,128)(2,1)} %bitcast.30, bf16[1536,768]{1,0:T(8,128)(2,1)} %bitcast.28, bf16[192,1536]{1,0:T(8,128)(2,1)} %bitcast.39), custom_call_target="tpu_custom_call" | custom-call | tf_op jit(solution)/shard_map/expert_in/pallas_call | solution.py:580
  185.8 1.5 all-gather.5.cloned.1.call-done
  187.3 0.8 broadcast_in_dim.71.scales
  188.2 73.1 %expert_out.1 = (bf16[2,256,1536]{2,1,0:T(8,128)(2,1)}, f32[2,256,1536]{2,1,0:T(8,128)}, bf16[2,256,1536]{2,1,0:T(8,128)(2,1)}, bf16[8,2,256,1536]{3,2,1,0:T(8,128)(2,1)}) custom-call(bf16[8,2,256,1664]{3,2,1,0:T(8,128)(2,1)} %get-tuple-element.46.rows_hbm, bf16[8,2,256,768]{3,2,1,0:T(8,128)(2,1)} %get-tuple-element.47.gate_hbm.g_hbm, ...), custom_call_target="tpu_custom_call" | custom-call | tf_op jit(solution)/shard_map/expert_out/pallas_call | solution.py:899
  261.3 73.3 %expert_back.1 = (bf16[8,2,256,1536]{3,2,1,0:T(8,128)(2,1)}, bf16[8,2,256,128]{3,2,1,0:T(8,128)(2,1)}, bf16[1536,768]{1,0:T(8,128)(2,1)}, bf16[1536,768]{1,0:T(8,128)(2,1)}, bf16[768,1536]{1,0:T(8,128)(2,1)}) custom-call(bf16[2,256,1536]{2,1,0:T(8,128)(2,1)} %get-tuple-element.52.own, bf16[8,2,256,1664]{3,2,1,0:T(8,128)(2,1)} %get-tuple-element.46.rows_hbm, ...), custom_call_target="tpu_custom_call" | custom-call | tf_op jit(solution)/shard_map/expert_back/pallas_call | solution.py:1082
  334.6 0.5 reduce-scatter.6.cloned.1.call-update
  335.1 0.2 reduce-scatter.4.cloned.1.call-start
  335.4 0.4 reduce-scatter.4.cloned.1.call-update
  335.7 70.4 %expert_rows.1 = f32[2,256,1664]{2,1,0:T(8,128)} custom-call(bf16[8,2,256,1536]{3,2,1,0:T(8,128)(2,1)} %get-tuple-element.54.dgu_hbm, bf16[8,2,256,128]{3,2,1,0:T(8,128)(2,1)} %get-tuple-element.55.tail_hbm, bf16[1536,768]{1,0:T(8,128)(2,1)} %bitcast.29, bf16[1536,768]{1,0:T(8,128)(2,1)} %bitcast.27), custom_call_target="tpu_custom_call" | custom-call | tf_op jit(solution)/shard_map/expert_rows/pallas_call | solution.py:1188
  406.1 114.2 %attend_back.1 = (f32[512,1536]{1,0:T(8,128)}, f32[48,1536]{1,0:T(8,128)}, f32[48,1536]{1,0:T(8,128)}, f32[48,256]{1,0:T(8,128)}, f32[48,256]{1,0:T(8,128)}, /*index=5*/f32[48,128]{1,0:T(8,128)}) custom-call(f32[512,1664]{1,0:T(8,128)} %bitcast.22, f32[512,1536]{1,0:T(8,128)} %bitcast.33, f32[512,1536]{1,0:T(8,128)} %get-tuple-element.50.resid_hbm, ...), custom_call_target="tpu_custom_call" | custom-call | tf_op jit(solution)/shard_map/attend_back/pallas_call | solution.py:1856
  520.4 1.4 copy.41
  521.8 1.5 slice_reduce_fusion
  523.3 2.2 convert_element_type.19
  525.5 2.2 convert_element_type.18
  527.7 2.3 convert_element_type.17
  530.0 2.7 copy.49
  532.6 1.7 copy.50
  534.3 0.7 copy.51
  535.0 0.6 copy.52
  535.7 0.6 copy.53
  536.3 0.7 copy.54
  (29 shorter events, 0.4 us)
Async XLA Ops:
  7.2 26.6 %copy-start.6 = (s32[512,4]{0,1:T(4,128)S(1)}, s32[512,4]{0,1:T(4,128)}, u32[]{:S(2)}) copy-start(s32[512,4]{0,1:T(4,128)} %param.19) | copy-start | bytes 24580
  7.2 27.5 %copy-start.5 = (s32[512]{0:T(512)S(1)}, s32[512]{0:T(512)}, u32[]{:S(2)}) copy-start(s32[512]{0:T(512)} %param.18) | copy-start | bytes 6148
  7.2 103.5 %all-gather.3.cloned.1.call-start = ((), (), s32[]{:S(2)}) async-start(), calls=%async_computation.3 | async-start | bytes 2949120 | tf_op jit(solution)/shard_map/all_gather | solution.py:1923
  32.3 155.0 %all-gather.5.cloned.1.call-start = ((), (), s32[]{:S(2)}) async-start(), calls=%async_computation.4 | async-start | bytes 2949120 | tf_op jit(solution)/shard_map/all_gather | solution.py:1924
  33.1 490.2 %reduce-scatter.8.cloned.1.call-start = ((), (), s32[]{:S(2)}) async-start(), calls=%async_computation.7 | async-start | bytes 2949120 | tf_op jit(solution)/shard_map/reduce_scatter | solution.py:1953
  334.6 190.9 %reduce-scatter.6.cloned.1.call-start = ((), (), s32[]{:S(2)}) async-start(), calls=%async_computation.6 | async-start | bytes 2949120 | tf_op jit(solution)/shard_map/reduce_scatter | solution.py:1953
  335.1 192.5 %reduce-scatter.4.cloned.1.call-start = ((), (), s32[]{:S(2)}) async-start(), calls=%async_computation.5 | async-start | bytes 2949120 | tf_op jit(solution)/shard_map/reduce_scatter | solution.py:1953
  527.7 5.0 copy-start
  532.6 1.7 copy-start.2
  532.6 2.4 copy-start.4
  532.6 3.0 copy-start.3
  532.6 3.6 copy-start.1
Sparse Core Ops, SparseCore 0:
  32.4 63.6 all-gather.2
  97.7 89.6 all-gather.4
  334.7 55.0 reduce-scatter.7
  392.0 47.1 reduce-scatter.5
  441.3 69.9 reduce-scatter.3

commit v8 on v7

--- a/solution.py
+++ b/solution.py
@@ -938,7 +938,7 @@
 BACK_SLOTS = 8
 
 
-def expert_back_kernel(own, rows_hbm, g_hbm, ua_hbm, down_hbm, dgu_out, tail_out, gate_out, up_out, down_out, buf, gua, rows, tails, down_w, acc, down_acc, send, recv, load, load_g, load_ua, load_rows, store_dgu, store_tail):
+def expert_back_kernel(own, rows_hbm, g_hbm, ua_hbm, down_hbm, dgu_out, tail_out, parts_out, buf, gua, rows, tails, down_w, acc, down_acc, send, recv, load, load_g, load_ua, load_rows, store_dgu, store_tail):
     hidden, width = down_w.shape
     gather = Gather(own, buf, send, recv)
     loads = (
@@ -1056,16 +1056,19 @@
     lax.fori_loop(0, 16, one, 0)
     gather.finish()
 
-    def round_gate_up(at):
-        gate_out[at, :] = acc[at, :hidden].astype(jnp.bfloat16)
-        up_out[at, :] = acc[at, hidden:].astype(jnp.bfloat16)
-
-    row_loop(width, 64, round_gate_up)
-
-    def round_down(at):
-        down_out[at, :] = down_acc[at, :].astype(jnp.bfloat16)
-
-    row_loop(hidden, 64, round_down)
+    def round_rows(source, rows_each, first):
+        chunks = rows_each // 64
+
+        def one(index, carry):
+            rows = pl.ds(pl.multiple_of(index * 64, 64), 64)
+            place = pl.ds(pl.multiple_of(first + lax.rem(index, chunks) * 64, 64), 64)
+            parts_out[lax.div(index, chunks), place, :] = source[rows, :].astype(jnp.bfloat16)
+            return carry
+
+        lax.fori_loop(0, 4 * chunks, one, 0)
+
+    round_rows(acc, width // 4, 0)
+    round_rows(down_acc, hidden // 4, width // 4)
 
     def drain(step, carry):
         for copy in block_stores(step):
@@ -1084,12 +1087,10 @@
         out_shape=(
             jax.ShapeDtypeStruct((8, 2, half, 2 * hidden), bf),
             jax.ShapeDtypeStruct((8, 2, half, 128), bf),
-            jax.ShapeDtypeStruct((width, hidden), bf),
-            jax.ShapeDtypeStruct((width, hidden), bf),
-            jax.ShapeDtypeStruct((hidden, width), bf),
+            jax.ShapeDtypeStruct((4, (width + hidden) // 4, width), bf),
         ),
         in_specs=[ANY] * 5,
-        out_specs=(ANY, ANY, VMEM, VMEM, VMEM),
+        out_specs=(ANY, ANY, VMEM),
         scratch_shapes=[
             pltpu.VMEM((8, 2, half, width), bf),
             pltpu.VMEM((BACK_SLOTS, half, 3 * hidden), bf),
@@ -1945,13 +1946,16 @@
         rows_all, gate_val, up_w, down_w, resid_mid, targets, scales
     )
     layer_out = layer_out.reshape(num_rows, width)
-    dgu, tails, gate_part, up_part, down_part = expert_back(
+    dgu, tails, expert_parts = expert_back(
         grad_out_b, rows_all, gate_val, ua, down_w
     )
     back = expert_rows(dgu, tails, gate_w, up_w)
-    expert_sums = tuple(
-        lax.psum_scatter(grad[None], "dp", scatter_dimension=1, tiled=True).astype(jnp.float32)
-        for grad in (gate_part, up_part, down_part)
+    expert_sum = lax.psum_scatter(expert_parts, "dp", scatter_dimension=0, tiled=True)
+    hidden, shard = w_gate.shape[2], w_gate.shape[1]
+    expert_sums = (
+        expert_sum[:, :shard, :hidden].astype(jnp.float32),
+        expert_sum[:, :shard, hidden:].astype(jnp.float32),
+        expert_sum[:, shard:].astype(jnp.float32),
     )
     grad_in, out_sum, q_sum, k_sum, v_sum, misc_sum = attend_back(
         back.reshape(num_rows, width + 128),

time: 544 us -> 524 us (0.963)
  Pallas kernels: 501 us -> 485 us
    pallas_call x1, Pallas kernels: 114 us -> 98.1 us  [attend_back(): pl.pallas_call(functools.partial(attend_back_kernel, q_heads, kv_heads, e...]
  transfers between devices with their start and end apart: 5 -> 3, of which waited for: 1 -> 1; matrix products, arithmetic and copies ran while one was open for 2% -> 1% of each run, Pallas kernels for 61% -> 61%
where the time goes in v8:
time: 524 us; the launch traced here: 523 us
  Pallas kernels  485 us (93%)
  local copies, waits for them, and re-layouts  15.5 us (3%)
  between operations  14.6 us (3%)
  other arithmetic  6.13 us (1%)
    pallas_call x1, Pallas kernels, attend_back(): pl.pallas_call(functools.partial(attend_back_kernel, q_heads, kv_heads, e...  98.1 us
    pallas_call x1, Pallas kernels, expert_in(): pl.pallas_call(expert_in_kernel, out_shape=(jax.ShapeDtypeStruct((8, 2, h...  74.9 us
    pallas_call x1, Pallas kernels, attend(): pl.pallas_call(functools.partial(attend_kernel, q_heads, kv_heads, expert...  74 us
    pallas_call x1, Pallas kernels, expert_out(): pl.pallas_call(expert_out_kernel, out_shape=(jax.ShapeDtypeStruct((2, hal...  73.1 us
    pallas_call x1, Pallas kernels, expert_back(): pl.pallas_call(expert_back_kernel, out_shape=(jax.ShapeDtypeStruct((8, 2,...  73.1 us
    pallas_call x1, Pallas kernels, expert_rows(): pl.pallas_call(expert_rows_kernel, out_shape=jax.ShapeDtypeStruct((2, hal...  70.4 us
    pallas_call x1, Pallas kernels, line_gather(): pl.pallas_call(line_gather_kernel, out_shape=jax.ShapeDtypeStruct((4, *ow...  21 us
  transfers between devices with their start and end apart: 3, of which 1 were waited for; matrix products, arithmetic and copies ran while one was open for 1% of the time, Pallas kernels for 61%

profile of v8, /device:TPU:0, one launch (start us, length us, event | category | flops | bytes accessed | tf_op | source)
XLA Modules:
  0.0 523.1 jit_solution(8798189096392153878)
XLA Ops:
  7.2 0.8 copy.38
  8.0 0.8 copy.39
  8.8 0.8 copy.37
  9.5 1.7 concatenate.9.own
  11.2 21.0 %line_gather.1.qkv_own = bf16[4,48,2176]{2,1,0:T(8,128)(2,1)} custom-call(bf16[48,2176]{1,0:T(8,128)(2,1)} %concatenate.9.own), custom_call_target="tpu_custom_call" | custom-call | tf_op jit(solution)/shard_map/line_gather/pallas_call | solution.py:1235
  32.3 0.0 all-gather.5.cloned.1.call-start
  32.3 0.7 all-gather.5.cloned.1.call-update
  33.8 0.9 copy.40.routes
  34.7 0.1 select_reduce_fusion.1
  34.8 0.1 select_reduce_fusion
  34.9 1.0 fusion
  35.9 1.0 pad_maximum_fusion
  36.9 74.0 %attend.1 = (bf16[512,1664]{1,0:T(8,128)(2,1)}, f32[512,1536]{1,0:T(8,128)}, bf16[16,512,128]{2,1,0:T(8,128)(2,1)}, bf16[512,1536]{1,0:T(8,128)(2,1)}, f32[512,1...) custom-call(bf16[512,1536]{1,0:T(8,128)(2,1)} %tokens_hbm.1, ...), custom_call_target="tpu_custom_call" | custom-call | tf_op jit(solution)/shard_map/attend/pallas_call | solution.py:1586
  110.9 74.9 %expert_in.1 = (bf16[8,2,256,1664]{3,2,1,0:T(8,128)(2,1)}, bf16[8,2,256,768]{3,2,1,0:T(8,128)(2,1)}, bf16[4,192,1536]{2,1,0:T(8,128)(2,1)}) custom-call(bf16[2,256,1664]{2,1,0:T(8,128)(2,1)} %bitcast.27, bf16[1536,768]{1,0:T(8,128)(2,1)} %bitcast.25, bf16[192,1536]{1,0:T(8,128)(2,1)} %bitcast.33), custom_call_target="tpu_custom_call" | custom-call | tf_op jit(solution)/shard_map/expert_in/pallas_call | solution.py:580
  185.9 1.3 all-gather.5.cloned.1.call-done
  187.2 0.8 broadcast_in_dim.62.scales
  188.0 73.1 %expert_out.1 = (bf16[2,256,1536]{2,1,0:T(8,128)(2,1)}, f32[2,256,1536]{2,1,0:T(8,128)}, bf16[2,256,1536]{2,1,0:T(8,128)(2,1)}, bf16[8,2,256,1536]{3,2,1,0:T(8,128)(2,1)}) custom-call(bf16[8,2,256,1664]{3,2,1,0:T(8,128)(2,1)} %get-tuple-element.44.rows_hbm, bf16[8,2,256,768]{3,2,1,0:T(8,128)(2,1)} %get-tuple-element.45.gate_hbm.g_hbm, ...), custom_call_target="tpu_custom_call" | custom-call | tf_op jit(solution)/shard_map/expert_out/pallas_call | solution.py:899
  261.2 73.1 %expert_back.1 = (bf16[8,2,256,1536]{3,2,1,0:T(8,128)(2,1)}, bf16[8,2,256,128]{3,2,1,0:T(8,128)(2,1)}, bf16[4,576,1536]{2,1,0:T(8,128)(2,1)}) custom-call(bf16[2,256,1536]{2,1,0:T(8,128)(2,1)} %get-tuple-element.50.own, bf16[8,2,256,1664]{3,2,1,0:T(8,128)(2,1)} %get-tuple-element.44.rows_hbm, bf16[8,2,256,768]{3,2,1,0:T(8,128)(2,1)} %get-tuple-element.45.gate_hbm.g_hbm, ...), custom_call_target="tpu_custom_call" | custom-call | tf_op jit(solution)/shard_map/expert_back/pallas_call | solution.py:1085
  334.3 70.4 %expert_rows.1 = f32[2,256,1664]{2,1,0:T(8,128)} custom-call(bf16[8,2,256,1536]{3,2,1,0:T(8,128)(2,1)} %get-tuple-element.52.dgu_hbm, bf16[8,2,256,128]{3,2,1,0:T(8,128)(2,1)} %get-tuple-element.53.tail_hbm, bf16[1536,768]{1,0:T(8,128)(2,1)} %bitcast.26, bf16[1536,768]{1,0:T(8,128)(2,1)} %bitcast.24), custom_call_target="tpu_custom_call" | custom-call | tf_op jit(solution)/shard_map/expert_rows/pallas_call | solution.py:1189
  404.7 98.1 %attend_back.1 = (f32[512,1536]{1,0:T(8,128)}, f32[48,1536]{1,0:T(8,128)}, f32[48,1536]{1,0:T(8,128)}, f32[48,256]{1,0:T(8,128)}, f32[48,256]{1,0:T(8,128)}, /*index=5*/f32[48,128]{1,0:T(8,128)}) custom-call(f32[512,1664]{1,0:T(8,128)} %bitcast.19, f32[512,1536]{1,0:T(8,128)} %bitcast.30, f32[512,1536]{1,0:T(8,128)} %get-tuple-element.48.resid_hbm, ...), custom_call_target="tpu_custom_call" | custom-call | tf_op jit(solution)/shard_map/attend_back/pallas_call | solution.py:1857
  502.8 1.4 copy.41
  504.2 1.5 slice_reduce_fusion
  505.8 2.3 slice_convert_fusion
  508.1 1.6 slice_convert_fusion.1
  509.7 0.6 copy-done.2
  510.3 1.1 copy.49
  511.4 0.8 copy-done
  512.2 1.7 copy.50
  513.9 0.7 copy.51
  514.6 0.6 copy.52
  515.3 0.6 copy.53
  515.9 0.7 copy.54
  (26 shorter events, 0.2 us)
Async XLA Ops:
  7.2 26.6 %copy-start.8 = (s32[512,4]{0,1:T(4,128)S(1)}, s32[512,4]{0,1:T(4,128)}, u32[]{:S(2)}) copy-start(s32[512,4]{0,1:T(4,128)} %param.19) | copy-start | bytes 24580
  7.2 27.5 %copy-start.7 = (s32[512]{0:T(512)S(1)}, s32[512]{0:T(512)}, u32[]{:S(2)}) copy-start(s32[512]{0:T(512)} %param.18) | copy-start | bytes 6148
  7.2 103.7 %all-gather.3.cloned.1.call-start = ((), (), s32[]{:S(2)}) async-start(), calls=%async_computation.1 | async-start | bytes 2949120 | tf_op jit(solution)/shard_map/all_gather | solution.py:1924
  32.3 154.9 %all-gather.5.cloned.1.call-start = ((), (), s32[]{:S(2)}) async-start(), calls=%async_computation.2 | async-start | bytes 2949120 | tf_op jit(solution)/shard_map/all_gather | solution.py:1925
  33.1 472.7 %reduce-scatter.2.cloned.1.call-start = ((), (), s32[]{:S(2)}) async-start(), calls=%async_computation.3 | async-start | bytes 8847360 | tf_op jit(solution)/shard_map/reduce_scatter | solution.py:1953
  505.8 2.3 copy-start.1
  508.1 2.2 copy-start.2
  509.7 2.6 copy-start
  512.2 1.7 copy-start.4
  512.2 2.4 copy-start.6
  512.2 3.0 copy-start.5
  512.2 3.6 copy-start.3
Sparse Core Ops, SparseCore 0:
  32.4 63.6 all-gather.2
  97.7 89.4 all-gather.4
  334.4 136.7 reduce-scatter.1

commit v9 on v8

--- a/solution.py
+++ b/solution.py
@@ -825,8 +825,7 @@
             copy.start()
     weights[1].start()
     plane_barrier(scatter.peers())
-    for copy in weights:
-        copy.wait()
+    weights[0].wait()
 
     def one(step, carry):
         _, _, other, place = scatter.place(step)
@@ -851,6 +850,11 @@
         ua[spot, :, :hidden] = up_val.astype(jnp.bfloat16)
         ua[spot, :, hidden:] = act_val.astype(jnp.bfloat16)
         ua_store(step).start()
+
+        @pl.when(step == 0)
+        def _():
+            weights[1].wait()
+
         partial = nn_dot(ua[spot, :, hidden:], down_w[...]).astype(jnp.bfloat16)
 
         @pl.when(other == 1)
@@ -1508,12 +1512,13 @@
     def project(index, carry):
         cols = pl.ds(pl.multiple_of(index * TILE, TILE), TILE)
         raw = nn_dot(hidden[...], flat(qkv_w, cols))
-        turned = index < (q_heads + kv_heads) // 2
-        cos_now = jnp.where(turned, cosine[...], 1.0)
-        sin_now = jnp.where(turned, sine[...], 0.0)
         for part in (0, 1):
+            slot = 2 * index + part
+            turned = lax.rem(slot, group + 2) != group + 1
+            cos_now = jnp.where(turned, cosine[...], 1.0)
+            sin_now = jnp.where(turned, sine[...], 0.0)
             value = rope(raw[:, part * HD : (part + 1) * HD], cos_now, sin_now)
-            heads[2 * index + part] = value.astype(jnp.bfloat16)
+            heads[slot] = value.astype(jnp.bfloat16)
         return carry
 
     lax.fori_loop(0, (q_heads + 2 * kv_heads) // 2, project, 0)
@@ -1521,16 +1526,17 @@
     lse[...] = jnp.zeros_like(lse)
 
     def head_step(head, carry):
-        kv_head = q_heads + lax.div(head, group)
+        key_slot = lax.div(head, group) * (group + 2) + group
+        query_slot = head + 2 * lax.div(head, group)
         cols = pl.ds(pl.multiple_of(head * HD, HD), HD)
         for first, keys in ((0, PROMPT), (PROMPT, num_rows)):
             rows = pl.ds(first, keys - first)
-            query = heads[head, rows, :]
-            score = nt_dot(query, heads[kv_head, :keys, :]) * HD ** (-0.5) + bias[rows, :keys]
+            query = heads[query_slot, rows, :]
+            score = nt_dot(query, heads[key_slot, :keys, :]) * HD ** (-0.5) + bias[rows, :keys]
             top = jnp.max(score, axis=1, keepdims=True)
             weight = jnp.exp(score - top)
             total = jnp.sum(weight, axis=1, keepdims=True)
-            value = nn_dot(weight.astype(jnp.bfloat16), heads[kv_head + kv_heads, :keys, :])
+            value = nn_dot(weight.astype(jnp.bfloat16), heads[key_slot + 1, :keys, :])
             mixed[rows, cols] = (value / total).astype(jnp.bfloat16)
             lanes = lax.broadcasted_iota(jnp.int32, (keys - first, 128), 1)
             lse[rows, :] = jnp.where(lanes == head, top + jnp.log(total), lse[rows, :])
@@ -1612,13 +1618,13 @@
     )(tokens, qkv_own, out_own, cosine, sine, segments.reshape(1, num_rows), routes)
 
 
-def attend_back_kernel(q_heads, kv_heads, experts, back_hbm, grad_hbm, resid_hbm, rows_hbm, prob_hbm, picked_hbm, qkv_hbm, out_hbm, mixed_hbm, heads_hbm, lse_hbm, bias_hbm, cos_hbm, sin_hbm, tokens_hbm, grad_in, out_sum, q_sum, k_sum, v_sum, misc_sum, back, grad, resid, hidden_two, prob, picked, qkv_w, out_w, mixed, heads, lse, bias, cosine, sine, tokens, gains, gain_sums, grad_logit, grad_proj, grad_mixed, grad_qkv, grad_kv, hidden, load, *scratch):
+def attend_back_kernel(q_heads, kv_heads, experts, back_hbm, grad_hbm, resid_hbm, rows_hbm, prob_hbm, picked_hbm, qkv_hbm, out_hbm, mixed_hbm, heads_hbm, lse_hbm, bias_hbm, cos_hbm, sin_hbm, tokens_hbm, grad_in, out_sum, q_sum, k_sum, v_sum, misc_sum, back, grad, resid, hidden_two, prob, picked, qkv_w, out_w, mixed, heads, lse, bias, cosine, sine, tokens, misc, gains, gain_sums, grad_logit, grad_proj, grad_mixed, grad_qkv, grad_kv, hidden, load, *scratch):
     num_rows, width = tokens.shape
     group = q_heads // kv_heads
     q_cols = q_heads * HD
     k_cols = kv_heads * HD
     qkv_cols = q_cols + 2 * k_cols
-    near_cols = group * HD
+    near_cols = (group + 2) * HD
     bf = jnp.bfloat16
     parts, scatters = [], []
     for index in range(4):
@@ -1631,25 +1637,34 @@
         (prob_hbm, prob),
         (picked_hbm, picked),
         (back_hbm, back),
-        (qkv_hbm, qkv_w),
+        (qkv_hbm.at[:, pl.ds(qkv_cols, 128)], misc),
         (resid_hbm, resid),
         (grad_hbm, grad),
-        (rows_hbm, hidden_two),
+        (mixed_hbm, mixed),
         (out_hbm, out_w),
-        (mixed_hbm, mixed),
+        (tokens_hbm, tokens),
         (heads_hbm, heads),
         (lse_hbm, lse),
         (bias_hbm, bias),
         (cos_hbm, cosine),
         (sin_hbm, sine),
-        (tokens_hbm, tokens),
+        (qkv_hbm, qkv_w),
+        (rows_hbm, hidden_two),
     )
     loads = [pltpu.make_async_copy(src, dst, load.at[i]) for i, (src, dst) in enumerate(pairs)]
-    for copy in loads:
-        copy.start()
+
+    def start(first, last):
+        for copy in loads[first:last]:
+            copy.start()
+
+    def wait(first, last):
+        for copy in loads[first:last]:
+            copy.wait()
+
+    start(0, 6)
     full_barrier(out_scatter.plane.peers(), out_scatter.line.line[1:])
-    for copy in loads[:3]:
-        copy.wait()
+    wait(0, 3)
+    start(6, 9)
     gain_sums[...] = jnp.zeros_like(gain_sums)
 
     def router_rows(rows):
@@ -1665,8 +1680,7 @@
         grad_logit[rows, :] = logit.astype(bf)
 
     row_loop(num_rows, 64, router_rows)
-    loads[3].wait()
-    misc = qkv_w.at[:, pl.ds(qkv_cols, 128)]
+    wait(3, 4)
     gain_rows(lambda rows: misc[rows, :], gains)
     lanes = lax.broadcasted_iota(jnp.int32, (TILE, 128), 1)
 
@@ -1675,8 +1689,8 @@
         back[:, cols] = back[:, cols] + nt_dot(grad_logit[...], router)
 
     tile_loop(width, TILE, hidden_tile)
-    for copy in loads[4:]:
-        copy.wait()
+    wait(4, 6)
+    start(9, 16)
 
     def fold(values):
         return jnp.sum(values.reshape(-1, 8, width), axis=0)
@@ -1707,6 +1721,7 @@
 
         lax.fori_loop(0, 4, one, 0)
 
+    wait(6, 7)
     weight_loop(out_part, mixed, grad_proj)
     out_scatter.begin()
 
@@ -1715,6 +1730,7 @@
             grad_proj[...], out_w[cols, :]
         ).astype(bf)
 
+    wait(7, 9)
     tile_loop(q_cols, TILE, mixed_tile)
     out_scatter.own()
 
@@ -1725,10 +1741,13 @@
 
     row_loop(num_rows, ROW_CHUNK, norm_one)
     scale = HD ** (-0.5)
+    wait(9, 14)
 
     def head_step(head, carry):
-        kv_head = lax.div(head, group)
+        key_slot = lax.div(head, group) * (group + 2) + group
+        query_slot = head + 2 * lax.div(head, group)
         cols = pl.ds(pl.multiple_of(head * HD, HD), HD)
+        query_cols = pl.ds(pl.multiple_of(query_slot * HD, HD), HD)
 
         @pl.when(lax.rem(head, group) == 0)
         def _():
@@ -1736,24 +1755,24 @@
 
         for first, keys in ((0, PROMPT), (PROMPT, num_rows)):
             rows = pl.ds(first, keys - first)
-            key = heads[q_heads + kv_head, :keys, :]
-            query = heads[head, rows, :]
+            key = heads[key_slot, :keys, :]
+            query = heads[query_slot, rows, :]
             up = grad_mixed[rows, cols]
             lane = lax.broadcasted_iota(jnp.int32, (keys - first, 128), 1)
             total = jnp.sum(jnp.where(lane == head, lse[rows, :], 0.0), axis=1, keepdims=True)
             weight = jnp.exp(nt_dot(query, key) * scale + bias[rows, :keys] - total)
-            grad_weight = nt_dot(up, heads[q_heads + kv_heads + kv_head, :keys, :])
+            grad_weight = nt_dot(up, heads[key_slot + 1, :keys, :])
             delta = jnp.sum(weight * grad_weight, axis=1, keepdims=True)
             score = (weight * (grad_weight - delta)).astype(bf)
             grad_kv[1, :keys, :] = grad_kv[1, :keys, :] + tn_dot(weight.astype(bf), up)
             grad_kv[0, :keys, :] = grad_kv[0, :keys, :] + tn_dot(score, query) * scale
             value = rope(nn_dot(score, key) * scale, cosine[rows, :], -sine[rows, :])
-            grad_qkv[rows, cols] = value.astype(bf)
+            grad_qkv[rows, query_cols] = value.astype(bf)
 
         @pl.when(lax.rem(head, group) == group - 1)
         def _():
-            key_cols = pl.ds(pl.multiple_of(q_cols + kv_head * HD, HD), HD)
-            value_cols = pl.ds(pl.multiple_of(q_cols + (kv_heads + kv_head) * HD, HD), HD)
+            key_cols = pl.ds(pl.multiple_of(key_slot * HD, HD), HD)
+            value_cols = pl.ds(pl.multiple_of((key_slot + 1) * HD, HD), HD)
             grad_qkv[:, key_cols] = rope(grad_kv[0], cosine[...], -sine[...]).astype(bf)
             grad_qkv[:, value_cols] = grad_kv[1].astype(bf)
 
@@ -1788,6 +1807,7 @@
     def hidden_back_tile(cols):
         back[:, cols] = nt_dot(grad_qkv[...], qkv_w[cols, pl.ds(0, qkv_cols)])
 
+    wait(14, 16)
     tile_loop(width // 2, TILE, hidden_back_tile)
     rest_scatter.own()
 
@@ -1833,10 +1853,9 @@
     misc_scatter.forward()
     misc_scatter.turn()
     out_scatter.finish(((out_sum, 0, width),))
-    near_scatter.finish(((q_sum, 0, near_cols),))
-    rest_scatter.finish(
-        ((q_sum, near_cols, q_cols - near_cols), (k_sum, 0, k_cols), (v_sum, 0, k_cols))
-    )
+    half_cols = group * HD
+    near_scatter.finish(((q_sum, 0, half_cols), (k_sum, 0, HD), (v_sum, 0, HD)))
+    rest_scatter.finish(((q_sum, half_cols, half_cols), (k_sum, HD, HD), (v_sum, HD, HD)))
     misc_scatter.finish(((misc_sum, 0, 128),))
     store.wait()
 
@@ -1848,7 +1867,7 @@
     k_cols = kv_heads * HD
     q_cols = q_heads * HD
     qkv_cols = q_cols + 2 * k_cols
-    near_cols = q_cols // kv_heads
+    near_cols = qkv_cols // kv_heads
     block_rows = width // 32
     scratch = []
     for columns in (width, near_cols, qkv_cols - near_cols, 128):
@@ -1865,6 +1884,7 @@
         out_specs=(ANY,) + (VMEM,) * 5,
         scratch_shapes=[pltpu.VMEM(array.shape, array.dtype) for array in arrays]
         + [
+            pltpu.VMEM((width, 128), bf),
             pltpu.VMEM((128, width), jnp.float32),
             pltpu.VMEM((16, width), jnp.float32),
             pltpu.VMEM((num_rows, 128), bf),
@@ -1873,7 +1893,7 @@
             pltpu.VMEM((num_rows, qkv_cols), bf),
             pltpu.VMEM((2, num_rows, HD), jnp.float32),
             pltpu.VMEM((num_rows, width), bf),
-            pltpu.SemaphoreType.DMA((len(arrays),)),
+            pltpu.SemaphoreType.DMA((len(arrays) + 1,)),
         ]
         + scratch,
         compiler_params=pltpu.CompilerParams(
@@ -1910,9 +1930,11 @@
     pad_cols = 128 - 2 - num_experts
     qkv_own = jnp.concatenate(
         [
-            w_query,
-            w_key,
-            w_value,
+            *(
+                weight[:, index * columns : (index + 1) * columns]
+                for index in range(kv_heads)
+                for weight, columns in ((w_query, q_cols // kv_heads), (w_key, HD), (w_value, HD))
+            ),
             w_router,
             gain_attn[:, None],
             gain_moe[:, None],

time: 524 us -> 519 us (level)
  Pallas kernels: 485 us -> 479 us
    pallas_call x1, Pallas kernels: 98.1 us -> 92.9 us  [attend_back(): pl.pallas_call(functools.partial(attend_back_kernel, q_heads, kv_heads, e...]
  transfers between devices with their start and end apart: 3 -> 3, of which waited for: 1 -> 1; matrix products, arithmetic and copies ran while one was open for 1% -> 1% of each run, Pallas kernels for 61% -> 60%
where the time goes in v9:
time: 519 us; the launch traced here: 518 us
  Pallas kernels  479 us (92%)
  local copies, waits for them, and re-layouts  16.3 us (3%)
  between operations  14.6 us (3%)
  other arithmetic  6.13 us (1%)
    pallas_call x1, Pallas kernels, attend_back(): pl.pallas_call(functools.partial(attend_back_kernel, q_heads, kv_heads, e...  92.9 us
    pallas_call x1, Pallas kernels, expert_in(): pl.pallas_call(expert_in_kernel, out_shape=(jax.ShapeDtypeStruct((8, 2, h...  74.9 us
    pallas_call x1, Pallas kernels, attend(): pl.pallas_call(functools.partial(attend_kernel, q_heads, kv_heads, expert...  74 us
    pallas_call x1, Pallas kernels, expert_back(): pl.pallas_call(expert_back_kernel, out_shape=(jax.ShapeDtypeStruct((8, 2,...  73.2 us
    pallas_call x1, Pallas kernels, expert_out(): pl.pallas_call(expert_out_kernel, out_shape=(jax.ShapeDtypeStruct((2, hal...  72.8 us
    pallas_call x1, Pallas kernels, expert_rows(): pl.pallas_call(expert_rows_kernel, out_shape=jax.ShapeDtypeStruct((2, hal...  70.4 us
    pallas_call x1, Pallas kernels, line_gather(): pl.pallas_call(line_gather_kernel, out_shape=jax.ShapeDtypeStruct((4, *ow...  21 us
  transfers between devices with their start and end apart: 3, of which 1 were waited for; matrix products, arithmetic and copies ran while one was open for 1% of the time, Pallas kernels for 60%

profile of v9, /device:TPU:0, one launch (start us, length us, event | category | flops | bytes accessed | tf_op | source)
XLA Modules:
  0.0 518.3 jit_solution(382893520906180295)
XLA Ops:
  7.2 0.8 copy.38
  8.0 0.8 copy.39
  8.8 0.8 copy.37
  9.5 0.9 fusion.1
  10.5 0.8 fusion.2
  11.2 0.8 concatenate.9.own
  12.0 21.0 %line_gather.1.qkv_own = bf16[4,48,2176]{2,1,0:T(8,128)(2,1)} custom-call(bf16[48,2176]{1,0:T(8,128)(2,1)} %concatenate.9.own), custom_call_target="tpu_custom_call" | custom-call | tf_op jit(solution)/shard_map/line_gather/pallas_call | solution.py:1239
  33.1 0.7 all-gather.5.cloned.1.call-update
  34.5 0.9 copy.40.routes
  35.5 0.1 select_reduce_fusion.1
  35.7 1.0 fusion
  36.7 1.0 pad_maximum_fusion
  37.7 74.0 %attend.1 = (bf16[512,1664]{1,0:T(8,128)(2,1)}, f32[512,1536]{1,0:T(8,128)}, bf16[16,512,128]{2,1,0:T(8,128)(2,1)}, bf16[512,1536]{1,0:T(8,128)(2,1)}, f32[512,1...) custom-call(bf16[512,1536]{1,0:T(8,128)(2,1)} %tokens_hbm.1, ...), custom_call_target="tpu_custom_call" | custom-call | tf_op jit(solution)/shard_map/attend/pallas_call | solution.py:1592
  111.7 74.9 %expert_in.1 = (bf16[8,2,256,1664]{3,2,1,0:T(8,128)(2,1)}, bf16[8,2,256,768]{3,2,1,0:T(8,128)(2,1)}, bf16[4,192,1536]{2,1,0:T(8,128)(2,1)}) custom-call(bf16[2,256,1664]{2,1,0:T(8,128)(2,1)} %bitcast.27, bf16[1536,768]{1,0:T(8,128)(2,1)} %bitcast.25, bf16[192,1536]{1,0:T(8,128)(2,1)} %bitcast.33), custom_call_target="tpu_custom_call" | custom-call | tf_op jit(solution)/shard_map/expert_in/pallas_call | solution.py:580
  186.6 1.3 all-gather.5.cloned.1.call-done
  188.0 0.8 broadcast_in_dim.62.scales
  188.8 72.8 %expert_out.1 = (bf16[2,256,1536]{2,1,0:T(8,128)(2,1)}, f32[2,256,1536]{2,1,0:T(8,128)}, bf16[2,256,1536]{2,1,0:T(8,128)(2,1)}, bf16[8,2,256,1536]{3,2,1,0:T(8,128)(2,1)}) custom-call(bf16[8,2,256,1664]{3,2,1,0:T(8,128)(2,1)} %get-tuple-element.44.rows_hbm, bf16[8,2,256,768]{3,2,1,0:T(8,128)(2,1)} %get-tuple-element.45.gate_hbm.g_hbm, ...), custom_call_target="tpu_custom_call" | custom-call | tf_op jit(solution)/shard_map/expert_out/pallas_call | solution.py:903
  261.6 73.2 %expert_back.1 = (bf16[8,2,256,1536]{3,2,1,0:T(8,128)(2,1)}, bf16[8,2,256,128]{3,2,1,0:T(8,128)(2,1)}, bf16[4,576,1536]{2,1,0:T(8,128)(2,1)}) custom-call(bf16[2,256,1536]{2,1,0:T(8,128)(2,1)} %get-tuple-element.50.own, bf16[8,2,256,1664]{3,2,1,0:T(8,128)(2,1)} %get-tuple-element.44.rows_hbm, bf16[8,2,256,768]{3,2,1,0:T(8,128)(2,1)} %get-tuple-element.45.gate_hbm.g_hbm, ...), custom_call_target="tpu_custom_call" | custom-call | tf_op jit(solution)/shard_map/expert_back/pallas_call | solution.py:1089
  334.8 70.4 %expert_rows.1 = f32[2,256,1664]{2,1,0:T(8,128)} custom-call(bf16[8,2,256,1536]{3,2,1,0:T(8,128)(2,1)} %get-tuple-element.52.dgu_hbm, bf16[8,2,256,128]{3,2,1,0:T(8,128)(2,1)} %get-tuple-element.53.tail_hbm, bf16[1536,768]{1,0:T(8,128)(2,1)} %bitcast.26, bf16[1536,768]{1,0:T(8,128)(2,1)} %bitcast.24), custom_call_target="tpu_custom_call" | custom-call | tf_op jit(solution)/shard_map/expert_rows/pallas_call | solution.py:1193
  405.2 92.9 %attend_back.1 = (f32[512,1536]{1,0:T(8,128)}, f32[48,1536]{1,0:T(8,128)}, f32[48,1536]{1,0:T(8,128)}, f32[48,256]{1,0:T(8,128)}, f32[48,256]{1,0:T(8,128)}, /*index=5*/f32[48,128]{1,0:T(8,128)}) custom-call(f32[512,1664]{1,0:T(8,128)} %bitcast.19, f32[512,1536]{1,0:T(8,128)} %bitcast.30, f32[512,1536]{1,0:T(8,128)} %get-tuple-element.48.resid_hbm, ...), custom_call_target="tpu_custom_call" | custom-call | tf_op jit(solution)/shard_map/attend_back/pallas_call | solution.py:1876
  498.1 1.4 copy.41
  499.5 1.5 slice_reduce_fusion
  501.0 2.3 slice_convert_fusion
  503.3 1.6 slice_convert_fusion.1
  504.9 0.6 copy-done.2
  505.5 1.1 copy.49
  506.6 0.8 copy-done
  507.5 1.7 copy.50
  509.1 0.7 copy.51
  509.9 0.6 copy.52
  510.5 0.6 copy.53
  511.1 0.7 copy.54
  (28 shorter events, 0.3 us)
Async XLA Ops:
  7.2 27.4 %copy-start.8 = (s32[512,4]{0,1:T(4,128)S(1)}, s32[512,4]{0,1:T(4,128)}, u32[]{:S(2)}) copy-start(s32[512,4]{0,1:T(4,128)} %param.19) | copy-start | bytes 24580
  7.2 28.3 %copy-start.7 = (s32[512]{0:T(512)S(1)}, s32[512]{0:T(512)}, u32[]{:S(2)}) copy-start(s32[512]{0:T(512)} %param.18) | copy-start | bytes 6148
  7.2 104.5 %all-gather.3.cloned.1.call-start = ((), (), s32[]{:S(2)}) async-start(), calls=%async_computation.1 | async-start | bytes 2949120 | tf_op jit(solution)/shard_map/all_gather | solution.py:1946
  33.1 154.9 %all-gather.5.cloned.1.call-start = ((), (), s32[]{:S(2)}) async-start(), calls=%async_computation.2 | async-start | bytes 2949120 | tf_op jit(solution)/shard_map/all_gather | solution.py:1947
  33.8 467.1 %reduce-scatter.2.cloned.1.call-start = ((), (), s32[]{:S(2)}) async-start(), calls=%async_computation.3 | async-start | bytes 8847360 | tf_op jit(solution)/shard_map/reduce_scatter | solution.py:1975
  501.0 2.3 copy-start.1
  503.3 2.2 copy-start.2
  504.9 2.6 copy-start
  507.5 1.7 copy-start.4
  507.5 2.4 copy-start.6
  507.5 3.0 copy-start.5
  507.5 3.6 copy-start.3
Sparse Core Ops, SparseCore 0:
  33.2 63.6 all-gather.2
  98.4 89.4 all-gather.4
  334.9 136.6 reduce-scatter.1
